TPU v7x, 32 devices: a whole 2x2x4 slice. The times are simulated.
32 devices in a mesh: row: 8 (over z, x), col: 4 (over y, core).
Axes of the slice: x: 2, y: 2, z: 4, core: 2. Of those that a mesh axis runs over, the one named last changes fastest.
Arguments:
- dense_a: bfloat16 [64, 512, 512], P(('row', 'col')), may hold values from -6 to 6
- dense_b: bfloat16 [64, 512, 512], P(('row', 'col')), may hold values from -0.25 to 0.25
- inner_basis_stack: bfloat16 [64, 2, 512, 128], P(('row', 'col')), may hold values from -0.25 to 0.25
- outer_basis_stack: bfloat16 [64, 2, 512, 128], P(('row', 'col')), may hold values from -1 to 1
- ascent: bfloat16 [32, 4, 2, 128, 128], P(('row', 'col')), may hold values from -0.4375 to 0.4375
- descent: bfloat16 [32, 4, 2, 128, 128], P(('row', 'col')), may hold values from -0.5 to 0.5
- couplings: bfloat16 [32, 2, 4, 128, 128], P(('row', 'col')), may hold values from -0.5 to 0.5
Outputs:
- product_diag: bfloat16 [64, 512, 512], P(('row', 'col'))
All inputs are finite; a program needn't handle non-finite values.
Results may differ from a plain program's by a relative error of at most 0.015.
Values may be sent and summed in bfloat16 or wider, within the bound.
No kernel may reach another device: no remote copies, remote signals or barrier semaphores. Data moves between devices by JAX's collectives and lax.ppermute only.
A program may use at most 64 MiB of HBM per device.

v0:
```python
import functools

import jax
import jax.numpy as jnp
from jax import lax
from jax.experimental import pallas as pl
from jax.experimental.pallas import tpu as pltpu
from jax.sharding import PartitionSpec as P

AXES = ("row", "col")
BF16 = jnp.bfloat16
F32 = jnp.float32
VMEM = pltpu.VMEM


def contract(a, b, left, right):
    return lax.dot_general(a, b, (((left,), (right,)), ((), ())), preferred_element_type=F32)


def dot(a, b):
    return contract(a, b, 1, 0)


def lift(p, f, q):
    return dot(contract(p, f, 0, 0).astype(BF16), q)


def couple(k, f, k2):
    return dot(dot(k, f).astype(BF16), k2)


def lower(s, g, w):
    return contract(dot(s, g).astype(BF16), w, 1, 1)


def pick(first, first_ref, second_ref, i):
    return jnp.where(first, first_ref[i], second_ref[i])


def head_kernel(inner_hbm, up_hbm, down_hbm, block_hbm, swk_ref, leaf_ref, pair_ref, inner, up, sems):
    copies = [
        pltpu.make_async_copy(inner_hbm, inner, sems.at[0]),
        pltpu.make_async_copy(up_hbm.at[0, 0:3], up, sems.at[1]),
        pltpu.make_async_copy(up_hbm.at[0, 3], pair_ref.at[2:4], sems.at[2]),
        pltpu.make_async_copy(down_hbm.at[0, 3], swk_ref.at[0:2], sems.at[3]),
        pltpu.make_async_copy(block_hbm.at[0, 1], swk_ref.at[2:6], sems.at[4]),
    ]
    for copy in copies:
        copy.start()
    copies[0].wait()
    leaves = [contract(inner[i, 0], inner[i, 1], 0, 0).astype(BF16) for i in range(2)]
    copies[1].wait()
    total = None
    for i in range(2):
        leaf_ref[i] = leaves[i]
        t = lift(up[i, 0], leaves[i], up[i, 1])
        total = t if total is None else total + t
    f0 = total.astype(BF16)
    pair_ref[0] = f0
    pair_ref[1] = lift(up[2, 0], f0, up[2, 1]).astype(BF16)
    for copy in copies[2:]:
        copy.wait()


def round_kernel(b, position_ref, pair_ref, received_ref, out_ref):
    low = ((position_ref[0] >> b) & 1) == 0
    f = (pair_ref[1].astype(F32) + received_ref[1].astype(F32)).astype(BF16)
    out_ref[0] = f
    if out_ref.shape[0] > 1:
        p = pick(low, pair_ref, received_ref, 2)
        q = pick(low, pair_ref, received_ref, 3)
        out_ref[1] = lift(p, f, q).astype(BF16)
    if out_ref.shape[0] > 2:
        out_ref[2] = pick(low, received_ref, pair_ref, 2)
        out_ref[3] = pick(low, received_ref, pair_ref, 3)


def carry_kernel(b, position_ref, carry_ref, got_ref, out_ref):
    low = ((position_ref[0] >> b) & 1) == 0
    n = out_ref.shape[0]
    skip = carry_ref.shape[0] - n

    @pl.when(low)
    def _():
        out_ref[...] = got_ref[skip:]

    @pl.when(jnp.logical_not(low))
    def _():
        out_ref[...] = carry_ref[skip:]


def dense_kernel(a_ref, b_ref, o_ref):
    for i in range(2):
        o_ref[i] = dot(a_ref[i], b_ref[i])


def near_term(position, height, carry_ref, got_ref, sibling):
    bit = (position >> (height - 1)) & 1
    base = carry_ref.shape[0] - 4
    left = pick(bit == 0, carry_ref, got_ref, base + bit)
    right = pick(bit == 0, carry_ref, got_ref, base + 3 - bit)
    return couple(left, sibling, right)


def upper_kernel(levels, position_ref, *refs):
    position = position_ref[0]
    received = refs[: levels - 1]
    carries = refs[levels - 1 : 3 * levels - 1 : 2]
    gots = refs[levels : 3 * levels - 1 : 2]
    out_ref = refs[3 * levels - 1]
    coupling = None
    for height in range(levels, 1, -1):
        near = near_term(
            position, height, carries[height - 1], gots[height - 1], received[height - 2][0]
        )
        if coupling is not None:
            low = ((position >> (height - 1)) & 1) == 0
            below = height - 2
            low = ((position >> below) & 1) == 0
            s = pick(low, carries[below], gots[below], 0)
            w = pick(low, carries[below], gots[below], 1)
            near = near + lower(s, coupling, w)
        coupling = near.astype(BF16)
    out_ref[0] = coupling


def final_kernel(
    position_ref, top_ref, got_top_ref, received_ref, carry_ref, got_ref, leaf_ref, down_ref,
    block_ref, dense_ref, outer_ref, out_hbm, out, sems,
):
    position = position_ref[0]
    odd = (position & 1) == 1
    near = near_term(position, 1, carry_ref, got_ref, received_ref[0])
    nears = [couple(block_ref[0, 0, i], leaf_ref[1 - i], block_ref[0, 0, 3 - i]) for i in range(2)]
    top = pick(odd, top_ref, got_top_ref, 0)
    g = (near + lower(down_ref[0, 2, 0], top, down_ref[0, 2, 1])).astype(BF16)
    copies = []
    for i in range(2):
        gb = (nears[i] + lower(down_ref[0, i, 0], g, down_ref[0, i, 1])).astype(BF16)
        e = dot(outer_ref[i, 0], gb).astype(BF16)
        out[i] = (dense_ref[i] + contract(e, outer_ref[i, 1], 1, 1)).astype(BF16)
        copies.append(pltpu.make_async_copy(out.at[i], out_hbm.at[i], sems.at[i]))
        copies[-1].start()
    for copy in copies:
        copy.wait()


def in_vmem(n, scalar=True):
    specs = [pl.BlockSpec(memory_space=VMEM)] * n
    return [pl.BlockSpec(memory_space=pltpu.SMEM)] + specs if scalar else specs


def small(mib=2):
    return pltpu.CompilerParams(vmem_limit_bytes=mib << 20)


def exchange(block, b, count, keep=lambda p: True):
    route = [(p, p ^ (1 << b)) for p in range(count) if keep(p)]
    return lax.ppermute(block, AXES, route)


def stages(dense_a, dense_b, inner_basis_stack, outer_basis_stack, ascent, descent, couplings):
    count = lax.axis_size("row") * lax.axis_size("col")
    levels = count.bit_length() - 1
    rank = ascent.shape[-1]
    place = lax.axis_index(AXES).reshape(1).astype(jnp.int32)

    def mats(n):
        return jax.ShapeDtypeStruct((n, rank, rank), BF16)

    def odd(p):
        return p & 1 == 1

    swk, leaf_inner, pair = pl.pallas_call(
        head_kernel,
        out_shape=(mats(6), mats(2), mats(4)),
        in_specs=[pl.BlockSpec(memory_space=pltpu.HBM)] * 4,
        out_specs=tuple(in_vmem(3, False)),
        scratch_shapes=[
            VMEM(inner_basis_stack.shape, BF16),
            VMEM((3, 2, rank, rank), BF16),
            pltpu.SemaphoreType.DMA((5,)),
        ],
        compiler_params=small(4),
        cost_estimate=pl.CostEstimate(flops=1 << 28, bytes_accessed=0, transcendentals=0),
        name="head",
    )(inner_basis_stack, ascent, descent, couplings)

    carries, gots = [swk], []
    for b in range(levels):
        carry = carries[b]
        if b == 0:
            keep = lambda p: not odd(p)
        elif b == levels - 1:
            keep = lambda p: odd(p) and not (p >> b) & 1
        else:
            keep = odd
        got = exchange(carry, b, count, keep)
        gots.append(got)
        if b + 1 == levels:
            break
        if b == 0:
            carries.append(swk)
            continue
        carries.append(
            pl.pallas_call(
                functools.partial(carry_kernel, b),
                out_shape=mats(6 if b + 1 <= levels - 3 else 4),
                in_specs=in_vmem(2),
                out_specs=in_vmem(1, False)[0],
                compiler_params=small(),
                name="carry",
            )(place, carry, got)
        )

    dense = pl.pallas_call(
        dense_kernel,
        out_shape=jax.ShapeDtypeStruct(dense_a.shape, F32),
        in_specs=in_vmem(2, False),
        out_specs=in_vmem(1, False)[0],
        compiler_params=small(8),
        name="dense",
    )(dense_a, dense_b)

    received = []
    for b in range(levels):
        received.append(exchange(pair, b, count, odd if b else lambda p: True))
        if b + 1 < levels:
            out = 1 if b + 1 == levels - 1 else 2 if b + 1 == levels - 2 else 4
            pair = pl.pallas_call(
                functools.partial(round_kernel, b),
                out_shape=mats(out),
                in_specs=in_vmem(2),
                out_specs=in_vmem(1, False)[0],
                compiler_params=small(),
                name="round",
            )(place, pair, received[b])

    blocks = [block for both in zip(carries, gots) for block in both]
    top = pl.pallas_call(
        functools.partial(upper_kernel, levels),
        out_shape=mats(1),
        in_specs=in_vmem(levels - 1 + 2 * levels),
        out_specs=in_vmem(1, False)[0],
        compiler_params=small(4),
        name="upper",
    )(place, *received[1:], *blocks)
    got_top = exchange(top, 0, count, odd)

    return pl.pallas_call(
        final_kernel,
        out_shape=jax.ShapeDtypeStruct(dense.shape, BF16),
        in_specs=in_vmem(10),
        out_specs=pl.BlockSpec(memory_space=pltpu.HBM),
        scratch_shapes=[VMEM(dense.shape, BF16), pltpu.SemaphoreType.DMA((2,))],
        compiler_params=small(12),
        name="final",
    )(
        place,
        top,
        got_top,
        received[0],
        carries[0],
        gots[0],
        leaf_inner,
        descent,
        couplings,
        dense,
        outer_basis_stack,
    )


def solution(mesh):
    placed = (
        P(AXES, None, None),
        P(AXES, None, None),
        P(AXES, None, None, None),
        P(AXES, None, None, None),
        P(AXES, None, None, None, None),
        P(AXES, None, None, None, None),
        P(AXES, None, None, None, None),
    )
    return jax.shard_map(
        stages, mesh=mesh, in_specs=placed, out_specs=P(AXES, None, None), check_vma=False
    )
```

profile of v0, /device:TPU:0, one launch (start us, length us, event | category | flops | bytes accessed | tf_op | source)
XLA Modules:
  0.0 48.7 jit_solution(5710047203434332477)
XLA Ops:
  0.0 0.0 copy-start
  0.0 0.9 %copy-done = bf16[1,4,2,128,128]{4,3,2,1,0:T(8,128)(2,1)S(1)} copy-done((bf16[1,4,2,128,128]{4,3,2,1,0:T(8,128)(2,1)S(1)}, bf16[1,4,2,128,128]{4,3,2,1,0:T(8,128)(2,1)}, u32[]{:S(2)}) %copy-start) | copy-done | bytes 262168
  1.0 0.0 copy-start.2
  1.0 0.9 %copy-done.2 = bf16[1,2,4,128,128]{4,3,2,1,0:T(8,128)(2,1)S(1)} copy-done((bf16[1,2,4,128,128]{4,3,2,1,0:T(8,128)(2,1)S(1)}, bf16[1,2,4,128,128]{4,3,2,1,0:T(8,128)(2,1)}, u32[]{:S(2)}) %copy-start.2) | copy-done | bytes 262168
  1.9 0.0 copy-start.7
  1.9 1.0 %copy-done.7 = bf16[2,2,512,128]{3,2,1,0:T(8,128)(2,1)S(1)} copy-done((bf16[2,2,512,128]{3,2,1,0:T(8,128)(2,1)S(1)}, bf16[2,2,512,128]{3,2,1,0:T(8,128)(2,1)}, u32[]{:S(2)}) %copy-start.7) | copy-done | bytes 524312
  2.9 0.0 copy-start.8
  2.9 0.9 %copy-done.8 = bf16[1,4,2,128,128]{4,3,2,1,0:T(8,128)(2,1)S(1)} copy-done((bf16[1,4,2,128,128]{4,3,2,1,0:T(8,128)(2,1)S(1)}, bf16[1,4,2,128,128]{4,3,2,1,0:T(8,128)(2,1)}, u32[]{:S(2)}) %copy-start.8) | copy-done | bytes 262168
  3.9 1.5 %head.1 = (bf16[6,128,128]{2,1,0:T(8,128)(2,1)S(1)}, bf16[2,128,128]{2,1,0:T(8,128)(2,1)S(1)}, bf16[4,128,128]{2,1,0:T(8,128)(2,1)S(1)}) custom-call(bf16[2,2,512,128]{3,2,1,0:T(8,128)(2,1)S(1)} %copy-done.7, bf16[1,4,2,128,128]{4,3,2,1,0:T(8,128)(2,1)S(1)} %copy-done.8, bf16[1,4,2,128,128]{4,3,2,1,0:T(8,128)(2,1)S(1)} %copy-done, ...), custom_call_target="tpu_custom_call" | custom-call | flops 268435456 | tf_op jit(solution)/shard_map/head/pallas_call | solution.py:174
  5.4 0.7 %collective-permute-start.6 = (bf16[6,128,128]{2,1,0:T(8,128)(2,1)S(1)}, bf16[6,128,128]{2,1,0:T(8,128)(2,1)S(1)}, u32[]{:S(2)}, u32[]{:S(2)}) collective-permute-start(bf16[6,128,128]{2,1,0:T(8,128)(2,1)S(1)} %get-tuple-element.9.carry_ref.refs_4_.refs_6_), channel_id=1, source_target_pairs={{1,3},{3,1},{5,7},{7,5},{9,11},{11,9},{13,15},{15,13},{17,19},{19,... | collective-permute-start | bytes 589832 | tf_op jit(solution)/shard_map/ppermute | solution.py:159
  6.1 3.9 %collective-permute-start = (bf16[4,128,128]{2,1,0:T(8,128)(2,1)S(1)}, bf16[4,128,128]{2,1,0:T(8,128)(2,1)S(1)}, u32[]{:S(2)}, u32[]{:S(2)}) collective-permute-start(bf16[4,128,128]{2,1,0:T(8,128)(2,1)S(1)} %get-tuple-element.8.pair_ref), channel_id=1, source_target_pairs={{0,1},{1,0},{2,3},{3,2},{4,5},{5,4},{6,7},{7,6},{8,9},{9,8},{10,11... | collective-permute-start | bytes 393224 | tf_op jit(solution)/shard_map/ppermute | solution.py:159
  10.0 0.0 collective-permute-done.6.got_ref.refs_7_
  10.0 0.0 copy-start.4
  10.0 0.0 copy-start.5
  10.0 0.8 %collective-permute-start.7 = (bf16[6,128,128]{2,1,0:T(8,128)(2,1)S(1)}, bf16[6,128,128]{2,1,0:T(8,128)(2,1)S(1)}, u32[]{:S(2)}, u32[]{:S(2)}) collective-permute-start(bf16[6,128,128]{2,1,0:T(8,128)(2,1)S(1)} %carry.3.carry_ref.refs_8_), channel_id=1, source_target_pairs={{1,5},{3,7},{5,1},{7,3},{9,13},{11,15},{13,9},{15,11},{17,21},{19,... | collective-permute-start | bytes 589832 | tf_op jit(solution)/shard_map/ppermute | solution.py:159
  10.8 0.1 collective-permute-done.received_ref
  10.9 0.3 round.4.pair_ref
  11.3 0.7 %collective-permute-start.1 = (bf16[4,128,128]{2,1,0:T(8,128)(2,1)S(1)}, bf16[4,128,128]{2,1,0:T(8,128)(2,1)S(1)}, u32[]{:S(2)}, u32[]{:S(2)}) collective-permute-start(bf16[4,128,128]{2,1,0:T(8,128)(2,1)S(1)} %round.4.pair_ref), channel_id=1, source_target_pairs={{1,3},{3,1},{5,7},{7,5},{9,11},{11,9},{13,15},{15,13},{17,19},{19,... | collective-permute-start | bytes 393224 | tf_op jit(solution)/shard_map/ppermute | solution.py:159
  11.9 0.0 collective-permute-done.7.got_ref.refs_9_
  12.0 0.7 %collective-permute-start.8 = (bf16[4,128,128]{2,1,0:T(8,128)(2,1)S(1)}, bf16[4,128,128]{2,1,0:T(8,128)(2,1)S(1)}, u32[]{:S(2)}, u32[]{:S(2)}) collective-permute-start(bf16[4,128,128]{2,1,0:T(8,128)(2,1)S(1)} %carry.4.carry_ref.refs_10_), channel_id=1, source_target_pairs={{1,9},{3,11},{5,13},{7,15},{9,1},{11,3},{13,5},{15,7},{17,25},{19,... | collective-permute-start | bytes 393224 | tf_op jit(solution)/shard_map/ppermute | solution.py:159
  12.6 0.0 collective-permute-done.1.received_ref.refs_0_
  12.7 0.3 round.5.pair_ref
  13.0 0.7 %collective-permute-start.2 = (bf16[4,128,128]{2,1,0:T(8,128)(2,1)S(1)}, bf16[4,128,128]{2,1,0:T(8,128)(2,1)S(1)}, u32[]{:S(2)}, u32[]{:S(2)}) collective-permute-start(bf16[4,128,128]{2,1,0:T(8,128)(2,1)S(1)} %round.5.pair_ref), channel_id=1, source_target_pairs={{1,5},{3,7},{5,1},{7,3},{9,13},{11,15},{13,9},{15,11},{17,21},{19,... | collective-permute-start | bytes 393224 | tf_op jit(solution)/shard_map/ppermute | solution.py:159
  13.7 14.7 %collective-permute-start.5 = (bf16[6,128,128]{2,1,0:T(8,128)(2,1)S(1)}, bf16[6,128,128]{2,1,0:T(8,128)(2,1)S(1)}, u32[]{:S(2)}, u32[]{:S(2)}) collective-permute-start(bf16[6,128,128]{2,1,0:T(8,128)(2,1)S(1)} %get-tuple-element.9.carry_ref.refs_4_.refs_6_), channel_id=1, source_target_pairs={{0,1},{2,3},{4,5},{6,7},{8,9},{10,11},{12,13},{14,15},{16,17},{18,... | collective-permute-start | bytes 589832 | tf_op jit(solution)/shard_map/ppermute | solution.py:159
  28.3 0.0 collective-permute-done.8.got_ref.refs_11_
  28.4 0.7 %collective-permute-start.9 = (bf16[4,128,128]{2,1,0:T(8,128)(2,1)S(1)}, bf16[4,128,128]{2,1,0:T(8,128)(2,1)S(1)}, u32[]{:S(2)}, u32[]{:S(2)}) collective-permute-start(bf16[4,128,128]{2,1,0:T(8,128)(2,1)S(1)} %carry.5.refs_12_), channel_id=1, source_target_pairs={{1,17},{3,19},{5,21},{7,23},{9,25},{11,27},{13,29},{15,31}} | collective-permute-start | bytes 393224 | tf_op jit(solution)/shard_map/ppermute | solution.py:159
  29.1 0.0 collective-permute-done.2.received_ref.refs_1_
  29.1 0.3 round.6.pair_ref
  29.4 0.7 %collective-permute-start.3 = (bf16[2,128,128]{2,1,0:T(8,128)(2,1)S(1)}, bf16[2,128,128]{2,1,0:T(8,128)(2,1)S(1)}, u32[]{:S(2)}, u32[]{:S(2)}) collective-permute-start(bf16[2,128,128]{2,1,0:T(8,128)(2,1)S(1)} %round.6.pair_ref), channel_id=1, source_target_pairs={{1,9},{3,11},{5,13},{7,15},{9,1},{11,3},{13,5},{15,7},{17,25},{19,... | collective-permute-start | bytes 196616 | tf_op jit(solution)/shard_map/ppermute | solution.py:159
  30.1 0.0 collective-permute-done.3.received_ref.refs_2_
  30.1 0.7 %collective-permute-start.4 = (bf16[1,128,128]{2,1,0:T(8,128)(2,1)S(1)}, bf16[1,128,128]{2,1,0:T(8,128)(2,1)S(1)}, u32[]{:S(2)}, u32[]{:S(2)}) collective-permute-start(bf16[1,128,128]{2,1,0:T(8,128)(2,1)S(1)} %round.7), channel_id=1, source_target_pairs={{1,17},{3,19},{5,21},{7,23},{9,25},{11,27},{13,29},{15,31},{17,1},... | collective-permute-start | bytes 98312 | tf_op jit(solution)/shard_map/ppermute | solution.py:159
  30.8 0.0 collective-permute-done.5.refs_5_.got_ref
  30.8 0.0 collective-permute-done.4.refs_3_
  30.8 0.0 collective-permute-done.9.refs_13_
  30.8 1.1 %upper.1.top_ref = bf16[1,128,128]{2,1,0:T(8,128)(2,1)S(1)} custom-call(s32[1]{0:T(128)} %bitcast.position_ref, bf16[4,128,128]{2,1,0:T(8,128)(2,1)S(1)} %collective-permute-done.1.received_ref.refs_0_, bf16[4,128,128]{2,1,0:T(8,128)(2,1)S(1)} %collective-permute-done.2.received_ref.refs_1_, ...), custom_call_target="tpu_custom_call" | custom-call | tf_op jit(solution)/shard_map/upper/pallas_call | solution.py:240
  31.9 0.0 copy-start.1
  31.9 0.0 copy-start.3
  31.9 0.0 copy-start.6
  31.9 1.4 %collective-permute-start.10 = (bf16[1,128,128]{2,1,0:T(8,128)(2,1)S(1)}, bf16[1,128,128]{2,1,0:T(8,128)(2,1)S(1)}, u32[]{:S(2)}, u32[]{:S(2)}) collective-permute-start(bf16[1,128,128]{2,1,0:T(8,128)(2,1)S(1)} %upper.1.top_ref), channel_id=1, source_target_pairs={{1,0},{3,2},{5,4},{7,6},{9,8},{11,10},{13,12},{15,14},{17,16},{19,... | collective-permute-start | bytes 98312 | tf_op jit(solution)/shard_map/ppermute | solution.py:159
  33.3 0.0 copy-done.4
  33.3 0.0 copy-done.5
  33.4 0.7 %dense.1.dense_ref = f32[2,512,512]{2,1,0:T(8,128)S(1)} custom-call(bf16[2,512,512]{2,1,0:T(8,128)(2,1)S(1)} %copy-done.4, bf16[2,512,512]{2,1,0:T(8,128)(2,1)S(1)} %copy-done.5), custom_call_target="tpu_custom_call" | custom-call | tf_op jit(solution)/shard_map/dense/pallas_call | solution.py:216
  34.1 12.3 %collective-permute-done.10.got_top_ref = bf16[1,128,128]{2,1,0:T(8,128)(2,1)S(1)} collective-permute-done((bf16[1,128,128]{2,1,0:T(8,128)(2,1)S(1)}, bf16[1,128,128]{2,1,0:T(8,128)(2,1)S(1)}, u32[]{:S(2)}, u32[]{:S(2)}) %collective-permute-start.10) | collective-permute-done | bytes 32800 | tf_op jit(solution)/shard_map/ppermute | solution.py:159
  46.4 0.0 copy-done.1
  46.4 0.0 copy-done.3
  46.4 0.0 copy-done.6
  46.4 2.3 %final.1 = bf16[2,512,512]{2,1,0:T(8,128)(2,1)} custom-call(s32[1]{0:T(128)} %bitcast.position_ref, bf16[1,128,128]{2,1,0:T(8,128)(2,1)S(1)} %upper.1.top_ref, bf16[1,128,128]{2,1,0:T(8,128)(2,1)S(1)} %collective-permute-done.10.got_top_ref, bf16[4,128,128]{2,1,0:T(8,128)(2,1)S(1)} %collective-permute-done.received_ref, ...), custom_call_target="tpu_custom_call" | custom-call | tf_op jit(solution)/shard_map/final/pallas_call | solution.py:250
  (4 shorter events, 0.1 us)
Async XLA Ops:
  0.0 0.9 %copy-start = (bf16[1,4,2,128,128]{4,3,2,1,0:T(8,128)(2,1)S(1)}, bf16[1,4,2,128,128]{4,3,2,1,0:T(8,128)(2,1)}, u32[]{:S(2)}) copy-start(bf16[1,4,2,128,128]{4,3,2,1,0:T(8,128)(2,1)} %down_ref.1) | copy-start | bytes 786436
  1.0 0.9 %copy-start.2 = (bf16[1,2,4,128,128]{4,3,2,1,0:T(8,128)(2,1)S(1)}, bf16[1,2,4,128,128]{4,3,2,1,0:T(8,128)(2,1)}, u32[]{:S(2)}) copy-start(bf16[1,2,4,128,128]{4,3,2,1,0:T(8,128)(2,1)} %block_ref.1) | copy-start | bytes 786436
  1.9 1.0 %copy-start.7 = (bf16[2,2,512,128]{3,2,1,0:T(8,128)(2,1)S(1)}, bf16[2,2,512,128]{3,2,1,0:T(8,128)(2,1)}, u32[]{:S(2)}) copy-start(bf16[2,2,512,128]{3,2,1,0:T(8,128)(2,1)} %inner_hbm.1) | copy-start | bytes 1572868
  2.9 0.9 %copy-start.8 = (bf16[1,4,2,128,128]{4,3,2,1,0:T(8,128)(2,1)S(1)}, bf16[1,4,2,128,128]{4,3,2,1,0:T(8,128)(2,1)}, u32[]{:S(2)}) copy-start(bf16[1,4,2,128,128]{4,3,2,1,0:T(8,128)(2,1)} %up_hbm.1) | copy-start | bytes 786436
  5.4 4.5 %collective-permute-start.6 = (bf16[6,128,128]{2,1,0:T(8,128)(2,1)S(1)}, bf16[6,128,128]{2,1,0:T(8,128)(2,1)S(1)}, u32[]{:S(2)}, u32[]{:S(2)}) collective-permute-start(bf16[6,128,128]{2,1,0:T(8,128)(2,1)S(1)} %get-tuple-element.9.carry_ref.refs_4_.refs_6_), channel_id=1, source_target_pairs={{1,3},{3,1},{5,7},{7,5},{9,11},{11,9},{13,15},{15,13},{17,19},{19,... | collective-permute-start | bytes 589832 | tf_op jit(solution)/shard_map/ppermute | solution.py:159
  6.1 4.8 %collective-permute-start = (bf16[4,128,128]{2,1,0:T(8,128)(2,1)S(1)}, bf16[4,128,128]{2,1,0:T(8,128)(2,1)S(1)}, u32[]{:S(2)}, u32[]{:S(2)}) collective-permute-start(bf16[4,128,128]{2,1,0:T(8,128)(2,1)S(1)} %get-tuple-element.8.pair_ref), channel_id=1, source_target_pairs={{0,1},{1,0},{2,3},{3,2},{4,5},{5,4},{6,7},{7,6},{8,9},{9,8},{10,11... | collective-permute-start | bytes 393224 | tf_op jit(solution)/shard_map/ppermute | solution.py:159
  10.0 23.3 %copy-start.4 = (bf16[2,512,512]{2,1,0:T(8,128)(2,1)S(1)}, bf16[2,512,512]{2,1,0:T(8,128)(2,1)}, u32[]{:S(2)}) copy-start(bf16[2,512,512]{2,1,0:T(8,128)(2,1)} %a_ref.1) | copy-start | bytes 3145732
  10.0 23.3 %copy-start.5 = (bf16[2,512,512]{2,1,0:T(8,128)(2,1)S(1)}, bf16[2,512,512]{2,1,0:T(8,128)(2,1)}, u32[]{:S(2)}) copy-start(bf16[2,512,512]{2,1,0:T(8,128)(2,1)} %b_ref.1) | copy-start | bytes 3145732
  10.0 1.9 %collective-permute-start.7 = (bf16[6,128,128]{2,1,0:T(8,128)(2,1)S(1)}, bf16[6,128,128]{2,1,0:T(8,128)(2,1)S(1)}, u32[]{:S(2)}, u32[]{:S(2)}) collective-permute-start(bf16[6,128,128]{2,1,0:T(8,128)(2,1)S(1)} %carry.3.carry_ref.refs_8_), channel_id=1, source_target_pairs={{1,5},{3,7},{5,1},{7,3},{9,13},{11,15},{13,9},{15,11},{17,21},{19,... | collective-permute-start | bytes 589832 | tf_op jit(solution)/shard_map/ppermute | solution.py:159
  11.3 1.4 %collective-permute-start.1 = (bf16[4,128,128]{2,1,0:T(8,128)(2,1)S(1)}, bf16[4,128,128]{2,1,0:T(8,128)(2,1)S(1)}, u32[]{:S(2)}, u32[]{:S(2)}) collective-permute-start(bf16[4,128,128]{2,1,0:T(8,128)(2,1)S(1)} %round.4.pair_ref), channel_id=1, source_target_pairs={{1,3},{3,1},{5,7},{7,5},{9,11},{11,9},{13,15},{15,13},{17,19},{19,... | collective-permute-start | bytes 393224 | tf_op jit(solution)/shard_map/ppermute | solution.py:159
  12.0 16.4 %collective-permute-start.8 = (bf16[4,128,128]{2,1,0:T(8,128)(2,1)S(1)}, bf16[4,128,128]{2,1,0:T(8,128)(2,1)S(1)}, u32[]{:S(2)}, u32[]{:S(2)}) collective-permute-start(bf16[4,128,128]{2,1,0:T(8,128)(2,1)S(1)} %carry.4.carry_ref.refs_10_), channel_id=1, source_target_pairs={{1,9},{3,11},{5,13},{7,15},{9,1},{11,3},{13,5},{15,7},{17,25},{19,... | collective-permute-start | bytes 393224 | tf_op jit(solution)/shard_map/ppermute | solution.py:159
  13.0 16.1 %collective-permute-start.2 = (bf16[4,128,128]{2,1,0:T(8,128)(2,1)S(1)}, bf16[4,128,128]{2,1,0:T(8,128)(2,1)S(1)}, u32[]{:S(2)}, u32[]{:S(2)}) collective-permute-start(bf16[4,128,128]{2,1,0:T(8,128)(2,1)S(1)} %round.5.pair_ref), channel_id=1, source_target_pairs={{1,5},{3,7},{5,1},{7,3},{9,13},{11,15},{13,9},{15,11},{17,21},{19,... | collective-permute-start | bytes 393224 | tf_op jit(solution)/shard_map/ppermute | solution.py:159
  13.7 17.1 %collective-permute-start.5 = (bf16[6,128,128]{2,1,0:T(8,128)(2,1)S(1)}, bf16[6,128,128]{2,1,0:T(8,128)(2,1)S(1)}, u32[]{:S(2)}, u32[]{:S(2)}) collective-permute-start(bf16[6,128,128]{2,1,0:T(8,128)(2,1)S(1)} %get-tuple-element.9.carry_ref.refs_4_.refs_6_), channel_id=1, source_target_pairs={{0,1},{2,3},{4,5},{6,7},{8,9},{10,11},{12,13},{14,15},{16,17},{18,... | collective-permute-start | bytes 589832 | tf_op jit(solution)/shard_map/ppermute | solution.py:159
  28.4 2.4 %collective-permute-start.9 = (bf16[4,128,128]{2,1,0:T(8,128)(2,1)S(1)}, bf16[4,128,128]{2,1,0:T(8,128)(2,1)S(1)}, u32[]{:S(2)}, u32[]{:S(2)}) collective-permute-start(bf16[4,128,128]{2,1,0:T(8,128)(2,1)S(1)} %carry.5.refs_12_), channel_id=1, source_target_pairs={{1,17},{3,19},{5,21},{7,23},{9,25},{11,27},{13,29},{15,31}} | collective-permute-start | bytes 393224 | tf_op jit(solution)/shard_map/ppermute | solution.py:159
  29.4 0.7 %collective-permute-start.3 = (bf16[2,128,128]{2,1,0:T(8,128)(2,1)S(1)}, bf16[2,128,128]{2,1,0:T(8,128)(2,1)S(1)}, u32[]{:S(2)}, u32[]{:S(2)}) collective-permute-start(bf16[2,128,128]{2,1,0:T(8,128)(2,1)S(1)} %round.6.pair_ref), channel_id=1, source_target_pairs={{1,9},{3,11},{5,13},{7,15},{9,1},{11,3},{13,5},{15,7},{17,25},{19,... | collective-permute-start | bytes 196616 | tf_op jit(solution)/shard_map/ppermute | solution.py:159
  30.1 0.7 %collective-permute-start.4 = (bf16[1,128,128]{2,1,0:T(8,128)(2,1)S(1)}, bf16[1,128,128]{2,1,0:T(8,128)(2,1)S(1)}, u32[]{:S(2)}, u32[]{:S(2)}) collective-permute-start(bf16[1,128,128]{2,1,0:T(8,128)(2,1)S(1)} %round.7), channel_id=1, source_target_pairs={{1,17},{3,19},{5,21},{7,23},{9,25},{11,27},{13,29},{15,31},{17,1},... | collective-permute-start | bytes 98312 | tf_op jit(solution)/shard_map/ppermute | solution.py:159
  31.9 14.5 %copy-start.1 = (bf16[1,4,2,128,128]{4,3,2,1,0:T(8,128)(2,1)S(1)}, bf16[1,4,2,128,128]{4,3,2,1,0:T(8,128)(2,1)}, u32[]{:S(2)}) copy-start(bf16[1,4,2,128,128]{4,3,2,1,0:T(8,128)(2,1)} %down_ref.1) | copy-start | bytes 786436
  31.9 14.5 %copy-start.3 = (bf16[1,2,4,128,128]{4,3,2,1,0:T(8,128)(2,1)S(1)}, bf16[1,2,4,128,128]{4,3,2,1,0:T(8,128)(2,1)}, u32[]{:S(2)}) copy-start(bf16[1,2,4,128,128]{4,3,2,1,0:T(8,128)(2,1)} %block_ref.1) | copy-start | bytes 786436
  31.9 14.5 %copy-start.6 = (bf16[2,2,512,128]{3,2,1,0:T(8,128)(2,1)S(1)}, bf16[2,2,512,128]{3,2,1,0:T(8,128)(2,1)}, u32[]{:S(2)}) copy-start(bf16[2,2,512,128]{3,2,1,0:T(8,128)(2,1)} %outer_ref.1) | copy-start | bytes 1572868
  31.9 14.4 %collective-permute-start.10 = (bf16[1,128,128]{2,1,0:T(8,128)(2,1)S(1)}, bf16[1,128,128]{2,1,0:T(8,128)(2,1)S(1)}, u32[]{:S(2)}, u32[]{:S(2)}) collective-permute-start(bf16[1,128,128]{2,1,0:T(8,128)(2,1)S(1)} %upper.1.top_ref), channel_id=1, source_target_pairs={{1,0},{3,2},{5,4},{7,6},{9,8},{11,10},{13,12},{15,14},{17,16},{19,... | collective-permute-start | bytes 98312 | tf_op jit(solution)/shard_map/ppermute | solution.py:159
where the time goes:
time: 49.2 us; the launch traced here: 48.7 us
  starting transfers between devices  25.4 us (52%)
  waiting for transfers between devices  12.4 us (25%)
  Pallas kernels  6.61 us (13%)
  local copies, waits for them, and re-layouts  3.92 us (8%)
    ppermute x11, starting transfers between devices, exchange(): return lax.ppermute(block, AXES, route)  25.4 us
    ppermute x11, waiting for transfers between devices, exchange(): return lax.ppermute(block, AXES, route)  12.4 us
    unnamed x18, local copies, waits for them, and re-layouts  3.92 us
    pallas_call x1, Pallas kernels, stages(): pl.pallas_call(final_kernel, out_shape=jax.ShapeDtypeStruct(dense.shape,...  2.33 us
    pallas_call x1, Pallas kernels, stages(): pl.pallas_call(head_kernel, out_shape=(mats(6), mats(2), mats(4)), in_spe...  1.53 us
    pallas_call x1, Pallas kernels, stages(): pl.pallas_call(functools.partial(upper_kernel, levels), out_shape=mats(1)...  1.06 us
  transfers between devices with their start and end apart: 11, of which 2 were waited for; matrix products, arithmetic and copies ran while one was open for 0% of the time, Pallas kernels for 3%

commit v1 on v0

v1 whole, which is shorter than its diff:
```python
import functools

import jax
import jax.numpy as jnp
from jax import lax
from jax.experimental import pallas as pl
from jax.experimental.pallas import tpu as pltpu
from jax.sharding import PartitionSpec as P

AXES = ("row", "col")
BF16 = jnp.bfloat16
F32 = jnp.float32
VMEM = pltpu.VMEM


def contract(a, b, left, right):
    return lax.dot_general(a, b, (((left,), (right,)), ((), ())), preferred_element_type=F32)


def dot(a, b):
    return contract(a, b, 1, 0)


def lift(p, f, q):
    return dot(contract(p, f, 0, 0).astype(BF16), q)


def couple(k, f, k2):
    return dot(dot(k, f).astype(BF16), k2)


def lower(s, g, w):
    return contract(dot(s, g).astype(BF16), w, 1, 1)


def pick(first, first_ref, second_ref, i):
    return jnp.where(first, first_ref[i], second_ref[i])


def head_kernel(inner_hbm, up_hbm, down_hbm, block_hbm, send_ref, leaf_ref, inner, up, sems):
    copies = [
        pltpu.make_async_copy(inner_hbm, inner, sems.at[0]),
        pltpu.make_async_copy(up_hbm.at[0, 0:3], up, sems.at[1]),
        pltpu.make_async_copy(up_hbm.at[0, 3], send_ref.at[2:4], sems.at[2]),
        pltpu.make_async_copy(down_hbm.at[0, 3], send_ref.at[4:6], sems.at[3]),
        pltpu.make_async_copy(block_hbm.at[0, 1], send_ref.at[6:10], sems.at[4]),
    ]
    for copy in copies:
        copy.start()
    copies[0].wait()
    leaves = [contract(inner[i, 0], inner[i, 1], 0, 0).astype(BF16) for i in range(2)]
    copies[1].wait()
    total = None
    for i in range(2):
        leaf_ref[i] = leaves[i]
        t = lift(up[i, 0], leaves[i], up[i, 1])
        total = t if total is None else total + t
    f0 = total.astype(BF16)
    send_ref[0] = f0
    send_ref[1] = lift(up[2, 0], f0, up[2, 1]).astype(BF16)
    for copy in copies[2:]:
        copy.wait()


def climb(low, r, levels, send_ref, got_ref, out_ref):
    f = (send_ref[1].astype(F32) + got_ref[1].astype(F32)).astype(BF16)
    out_ref[0] = f
    if r + 1 < levels - 1:
        p = pick(low, send_ref, got_ref, 2)
        q = pick(low, send_ref, got_ref, 3)
        out_ref[1] = lift(p, f, q).astype(BF16)
    if r + 1 < levels - 2:
        out_ref[2] = pick(low, got_ref, send_ref, 2)
        out_ref[3] = pick(low, got_ref, send_ref, 3)


def start_kernel(levels, position_ref, send_ref, got_ref, out_ref, carry_ref):
    odd = (position_ref[0] & 1) == 1

    @pl.when(odd)
    def _():
        climb(False, 0, levels, send_ref, got_ref, out_ref)

    @pl.when(jnp.logical_not(odd))
    def _():
        carry_ref[...] = got_ref[4:10]
        out_ref[0:2] = got_ref[7:9]


def sent(j, levels):
    return 6 if j <= levels - 4 else 4 if j == levels - 3 else 2


def fill(j, levels, position, carry_ref, out_ref):
    low = ((position >> j) & 1) == 0
    n = sent(j, levels)
    if n == 6:
        out_ref[0:6] = carry_ref[...]
        return

    @pl.when(low)
    def _():
        if n == 4:
            out_ref[0:2] = carry_ref[0:2]
        out_ref[n - 2 : n] = carry_ref[n - 1 : n + 1]

    @pl.when(jnp.logical_not(low))
    def _():
        out_ref[0:n] = carry_ref[2:6] if n == 4 else carry_ref[0:2]


def round_kernel(r, levels, position_ref, send_ref, got_ref, carry_ref, *out_refs):
    position = position_ref[0]
    odd = (position & 1) == 1
    out_ref = out_refs[0]

    @pl.when(odd)
    def _():
        low = ((position >> r) & 1) == 0
        if r == levels - 1:
            out_ref[0] = got_ref[0]
        else:
            climb(low, r, levels, send_ref, got_ref, out_ref)

    @pl.when(jnp.logical_not(odd))
    def _():
        if r == 1:
            new_ref = out_refs[1]
            mask = (1 << (levels - 2)) - 1
            top = ((position >> 1) & mask) == mask
            new_ref[...] = carry_ref[...]

            @pl.when(top)
            def _():
                left = ((position >> (levels - 1)) & 1) == 0
                new_ref[2] = pick(left, carry_ref.at[2:3], got_ref.at[0:1], 0)
                new_ref[3] = pick(left, carry_ref.at[5:6], got_ref.at[1:2], 0)

            fill(1, levels, position, new_ref, out_ref)
            return
        j = r - 1
        n = sent(j, levels)
        low = ((position >> j) & 1) == 0
        if n == 2:
            out_ref[0] = pick(low, carry_ref.at[0:1], got_ref.at[0:1], 0)
            out_ref[1] = pick(low, carry_ref.at[3:4], got_ref.at[1:2], 0)
            out_ref[2] = pick(low, got_ref.at[0:1], carry_ref.at[0:1], 0)
            out_ref[3] = pick(low, got_ref.at[1:2], carry_ref.at[1:2], 0)
            return
        new_ref, node_ref = out_refs[1:]

        @pl.when(low)
        def _():
            node_ref[0:3] = carry_ref[0:3]
            node_ref[3] = carry_ref[5]
            new_ref[...] = got_ref[0 : new_ref.shape[0]]

        @pl.when(jnp.logical_not(low))
        def _():
            node_ref[0:2] = got_ref[0:2]
            node_ref[2:4] = got_ref[3:5] if n == 6 else got_ref[2:4]
            new_ref[...] = carry_ref[...] if n == 6 else carry_ref[2:6]

        fill(j + 1, levels, position, new_ref, out_ref)


def pack_kernel(count, position_ref, *refs):
    odd = (position_ref[0] & 1) == 1
    received, nodes, out_ref = refs[:count], refs[count:-1], refs[-1]

    @pl.when(odd)
    def _():
        for i, ref in enumerate(received):
            out_ref[i] = ref[0]

    @pl.when(jnp.logical_not(odd))
    def _():
        for i, ref in enumerate(nodes):
            out_ref[4 * i : 4 * i + 4] = ref[...]


def dense_kernel(a_ref, b_ref, o_ref):
    for i in range(2):
        o_ref[i] = dot(a_ref[i], b_ref[i])


def final_kernel(
    levels, position_ref, send_ref, got_ref, mine_ref, other_ref, last_ref, other_last_ref,
    leaf_ref, down_ref, block_ref, dense_ref, outer_ref, out_hbm, out, sems,
):
    odd = (position_ref[0] & 1) == 1

    def inner(height):
        if height == levels - 1:
            return pick(odd, last_ref, other_last_ref, 0)
        return pick(odd, mine_ref, other_ref, height - 1)

    def generator(height, i):
        if height == 1:
            left, right = ((4, 4), (5, 5), (6, 7), (9, 8))[i]
            return jnp.where(odd, got_ref[right], send_ref[left])
        if height >= levels - 1:
            return pick(odd, other_last_ref, last_ref, 2 * (height - levels + 1) + i - 2)
        return pick(odd, other_ref, mine_ref, 4 * (height - 2) + i)

    coupling = None
    for height in range(levels, 1, -1):
        near = couple(generator(height, 2), inner(height - 1), generator(height, 3))
        if coupling is not None:
            near = near + lower(generator(height - 1, 0), coupling, generator(height - 1, 1))
        coupling = near.astype(BF16)
    near = couple(generator(1, 2), got_ref[0], generator(1, 3))
    g = (near + lower(down_ref[0, 2, 0], coupling, down_ref[0, 2, 1])).astype(BF16)
    copies = []
    for i in range(2):
        near = couple(block_ref[0, 0, i], leaf_ref[1 - i], block_ref[0, 0, 3 - i])
        gb = (near + lower(down_ref[0, i, 0], g, down_ref[0, i, 1])).astype(BF16)
        e = dot(outer_ref[i, 0], gb).astype(BF16)
        out[i] = (dense_ref[i] + contract(e, outer_ref[i, 1], 1, 1)).astype(BF16)
        copies.append(pltpu.make_async_copy(out.at[i], out_hbm.at[i], sems.at[i]))
        copies[-1].start()
    for copy in copies:
        copy.wait()


def in_vmem(n, scalar=True):
    specs = [pl.BlockSpec(memory_space=VMEM)] * n
    return [pl.BlockSpec(memory_space=pltpu.SMEM)] + specs if scalar else specs


def small(mib=2):
    return pltpu.CompilerParams(vmem_limit_bytes=mib << 20)


def exchange(block, count, odd_bit, even_bit):
    route = [(p, p ^ (1 << (odd_bit if p & 1 else even_bit))) for p in range(count)]
    return lax.ppermute(block, AXES, route)


def stages(dense_a, dense_b, inner_basis_stack, outer_basis_stack, ascent, descent, couplings):
    count = lax.axis_size("row") * lax.axis_size("col")
    levels = count.bit_length() - 1
    rank = ascent.shape[-1]
    place = lax.axis_index(AXES).reshape(1).astype(jnp.int32)

    def mats(n):
        return jax.ShapeDtypeStruct((n, rank, rank), BF16)

    def call(kernel, outs, *refs, **extra):
        return pl.pallas_call(
            kernel,
            out_shape=tuple(mats(n) for n in outs),
            in_specs=in_vmem(len(refs)),
            out_specs=tuple(in_vmem(len(outs), False)),
            compiler_params=small(),
        )(place, *refs)

    send, leaf_inner = pl.pallas_call(
        head_kernel,
        out_shape=(mats(10), mats(2)),
        in_specs=[pl.BlockSpec(memory_space=pltpu.HBM)] * 4,
        out_specs=tuple(in_vmem(2, False)),
        scratch_shapes=[
            VMEM(inner_basis_stack.shape, BF16),
            VMEM((3, 2, rank, rank), BF16),
            pltpu.SemaphoreType.DMA((5,)),
        ],
        compiler_params=small(4),
        name="head",
    )(*[
        pltpu.with_memory_space_constraint(x, pltpu.HBM)
        for x in (inner_basis_stack, ascent, descent, couplings)
    ])
    dense = pl.pallas_call(
        dense_kernel,
        out_shape=jax.ShapeDtypeStruct(dense_a.shape, F32),
        in_specs=in_vmem(2, False),
        out_specs=in_vmem(1, False)[0],
        compiler_params=small(8),
        name="dense",
    )(dense_a, dense_b)

    def width(r):
        climbing = 4 if r <= levels - 3 else 2 if r == levels - 2 else 1
        return max(climbing, 2 if r == 1 else sent(r - 1, levels))

    got = exchange(send, count, 0, 0)
    block, carry = call(functools.partial(start_kernel, levels), (width(1), 6), send, got)
    received, nodes = [], []
    for r in range(1, levels):
        new = exchange(block, count, r, levels - 1 if r == 1 else r - 1)
        kernel = functools.partial(round_kernel, r, levels)
        if r == levels - 1:
            (last,) = call(kernel, (4,), block, new, carry)
            break
        received.append(new)
        outs = (width(r + 1), 6 if r <= levels - 3 else 4) + ((4,) if r > 1 else ())
        block, carry, *node = call(kernel, outs, block, new, carry)
        nodes += node

    size = max(len(received), 4 * len(nodes))
    (mine,) = call(functools.partial(pack_kernel, len(received)), (size,), *received, *nodes)
    other = exchange(mine, count, 0, 0)
    other_last = exchange(last, count, 0, 0)

    return pl.pallas_call(
        functools.partial(final_kernel, levels),
        out_shape=jax.ShapeDtypeStruct(dense.shape, BF16),
        in_specs=in_vmem(11),
        out_specs=pl.BlockSpec(memory_space=pltpu.HBM),
        scratch_shapes=[VMEM(dense.shape, BF16), pltpu.SemaphoreType.DMA((2,))],
        compiler_params=small(12),
        name="final",
    )(
        place,
        send,
        got,
        mine,
        other,
        last,
        other_last,
        leaf_inner,
        descent,
        couplings,
        dense,
        outer_basis_stack,
    )


def solution(mesh):
    placed = (
        P(AXES, None, None),
        P(AXES, None, None),
        P(AXES, None, None, None),
        P(AXES, None, None, None),
        P(AXES, None, None, None, None),
        P(AXES, None, None, None, None),
        P(AXES, None, None, None, None),
    )
    return jax.shard_map(
        stages, mesh=mesh, in_specs=placed, out_specs=P(AXES, None, None), check_vma=False
    )
```

time: 49.2 us -> 33.1 us (0.67)
  starting transfers between devices: 25.4 us -> 11.3 us
  local copies, waits for them, and re-layouts: 3.92 us -> 0.03 us
  waiting for transfers between devices: 12.4 us -> 15.2 us
    ppermute x11 -> x7, starting transfers between devices: 25.4 us -> 11.3 us  [exchange(): return lax.ppermute(block, AXES, route)]
    unnamed x18 -> x10, local copies, waits for them, and re-layouts: 3.92 us -> 0.03 us
    ppermute x11 -> x7, waiting for transfers between devices: 12.4 us -> 15.2 us  [exchange(): return lax.ppermute(block, AXES, route)]
    pallas_call x10 -> x8, Pallas kernels: 5.9 us -> 5.49 us  [the longest x1 3.36 us: stages(): pl.pallas_call(functools.partial(final_kernel, levels), out_shape=jax.Sha...]
  transfers between devices with their start and end apart: 11 -> 7, of which waited for: 2 -> 6; matrix products, arithmetic and copies ran while one was open for 0% -> 0% of each run, Pallas kernels for 3% -> 2%
where the time goes in v1:
time: 33.1 us; the launch traced here: 32.9 us
  waiting for transfers between devices  15.2 us (46%)
  starting transfers between devices  11.3 us (34%)
  Pallas kernels  6.19 us (19%)
    ppermute x7, waiting for transfers between devices, exchange(): return lax.ppermute(block, AXES, route)  15.2 us
    ppermute x7, starting transfers between devices, exchange(): return lax.ppermute(block, AXES, route)  11.3 us
    pallas_call x1, Pallas kernels, stages(): pl.pallas_call(functools.partial(final_kernel, levels), out_shape=jax.Sha...  3.36 us
    pallas_call x1, Pallas kernels, stages(): pl.pallas_call(head_kernel, out_shape=(mats(10), mats(2)), in_specs=[pl.B...  1.94 us
    pallas_call x1, Pallas kernels, stages(): pl.pallas_call(dense_kernel, out_shape=jax.ShapeDtypeStruct(dense_a.shape...  0.71 us
  transfers between devices with their start and end apart: 7, of which 6 were waited for; matrix products, arithmetic and copies ran while one was open for 0% of the time, Pallas kernels for 2%

profile of v1, /device:TPU:0, one launch (start us, length us, event | category | flops | bytes accessed | tf_op | source)
XLA Modules:
  0.0 32.9 jit_solution(2493648197644984063)
XLA Ops:
  0.0 1.9 %head.1 = (bf16[10,128,128]{2,1,0:T(8,128)(2,1)S(1)}, bf16[2,128,128]{2,1,0:T(8,128)(2,1)S(1)}) custom-call(bf16[2,2,512,128]{3,2,1,0:T(8,128)(2,1)} %inner_hbm.1, bf16[1,4,2,128,128]{4,3,2,1,0:T(8,128)(2,1)} %up_hbm.1, bf16[1,4,2,128,128]{4,3,2,1,0:T(8,128)(2,1)} %down_ref.1, bf16[1,2,4,128,128]{4,3,2,1,0:T(8,128)(2,1)} %block_ref.1), custom_call_target="tpu_custom_call" | custom-call | tf_op jit(solution)/shard_map/head/pallas_call | solution.py:258
  2.0 0.0 copy-start.2
  2.0 0.0 copy-start.3
  2.0 0.6 %collective-permute-start = (bf16[10,128,128]{2,1,0:T(8,128)(2,1)S(1)}, bf16[10,128,128]{2,1,0:T(8,128)(2,1)S(1)}, u32[]{:S(2)}, u32[]{:S(2)}) collective-permute-start(bf16[10,128,128]{2,1,0:T(8,128)(2,1)S(1)} %get-tuple-element.17.send_ref), channel_id=1, source_target_pairs={{0,1},{1,0},{2,3},{3,2},{4,5},{5,4},{6,7},{7,6},{8,9},{9,8},{10,11... | collective-permute-start | bytes 983048 | tf_op jit(solution)/shard_map/ppermute | solution.py:237
  2.5 1.3 %collective-permute-done.got_ref = bf16[10,128,128]{2,1,0:T(8,128)(2,1)S(1)} collective-permute-done((bf16[10,128,128]{2,1,0:T(8,128)(2,1)S(1)}, bf16[10,128,128]{2,1,0:T(8,128)(2,1)S(1)}, u32[]{:S(2)}, u32[]{:S(2)}) %collective-permute-start) | collective-permute-done | bytes 327712 | tf_op jit(solution)/shard_map/ppermute | solution.py:237
  3.8 4.0 %collective-permute-start.1 = (bf16[4,128,128]{2,1,0:T(8,128)(2,1)S(1)}, bf16[4,128,128]{2,1,0:T(8,128)(2,1)S(1)}, u32[]{:S(2)}, u32[]{:S(2)}) collective-permute-start(bf16[4,128,128]{2,1,0:T(8,128)(2,1)S(1)} %get-tuple-element.18.send_ref), channel_id=1, source_target_pairs={{0,16},{1,3},{2,18},{3,1},{4,20},{5,7},{6,22},{7,5},{8,24},{9,11},... | collective-permute-start | bytes 393224 | tf_op jit(solution)/shard_map/ppermute | solution.py:237
  7.8 3.0 %collective-permute-done.1.got_ref.refs_0_ = bf16[4,128,128]{2,1,0:T(8,128)(2,1)S(1)} collective-permute-done((bf16[4,128,128]{2,1,0:T(8,128)(2,1)S(1)}, bf16[4,128,128]{2,1,0:T(8,128)(2,1)S(1)}, u32[]{:S(2)}, u32[]{:S(2)}) %collective-permute-start.1) | collective-permute-done | bytes 131104 | tf_op jit(solution)/shard_map/ppermute | solution.py:237
  10.8 3.3 %collective-permute-start.2 = (bf16[6,128,128]{2,1,0:T(8,128)(2,1)S(1)}, bf16[6,128,128]{2,1,0:T(8,128)(2,1)S(1)}, u32[]{:S(2)}, u32[]{:S(2)}) collective-permute-start(bf16[6,128,128]{2,1,0:T(8,128)(2,1)S(1)} %get-tuple-element.20.send_ref), channel_id=1, source_target_pairs={{0,2},{1,5},{2,0},{3,7},{4,6},{5,1},{6,4},{7,3},{8,10},{9,13},{10,... | collective-permute-start | bytes 589832 | tf_op jit(solution)/shard_map/ppermute | solution.py:237
  14.1 3.6 %collective-permute-done.2.got_ref.refs_1_ = bf16[6,128,128]{2,1,0:T(8,128)(2,1)S(1)} collective-permute-done((bf16[6,128,128]{2,1,0:T(8,128)(2,1)S(1)}, bf16[6,128,128]{2,1,0:T(8,128)(2,1)S(1)}, u32[]{:S(2)}, u32[]{:S(2)}) %collective-permute-start.2) | collective-permute-done | bytes 196640 | tf_op jit(solution)/shard_map/ppermute | solution.py:237
  17.8 2.1 %collective-permute-start.3 = (bf16[4,128,128]{2,1,0:T(8,128)(2,1)S(1)}, bf16[4,128,128]{2,1,0:T(8,128)(2,1)S(1)}, u32[]{:S(2)}, u32[]{:S(2)}) collective-permute-start(bf16[4,128,128]{2,1,0:T(8,128)(2,1)S(1)} %get-tuple-element.22.send_ref), channel_id=1, source_target_pairs={{0,4},{1,9},{2,6},{3,11},{4,0},{5,13},{6,2},{7,15},{8,12},{9,1},{1... | collective-permute-start | bytes 393224 | tf_op jit(solution)/shard_map/ppermute | solution.py:237
  19.9 3.0 %collective-permute-done.3.got_ref.refs_2_ = bf16[4,128,128]{2,1,0:T(8,128)(2,1)S(1)} collective-permute-done((bf16[4,128,128]{2,1,0:T(8,128)(2,1)S(1)}, bf16[4,128,128]{2,1,0:T(8,128)(2,1)S(1)}, u32[]{:S(2)}, u32[]{:S(2)}) %collective-permute-start.3) | collective-permute-done | bytes 131104 | tf_op jit(solution)/shard_map/ppermute | solution.py:237
  22.9 0.1 collective-permute-start.4
  23.0 1.2 %collective-permute-start.5 = (bf16[2,128,128]{2,1,0:T(8,128)(2,1)S(1)}, bf16[2,128,128]{2,1,0:T(8,128)(2,1)S(1)}, u32[]{:S(2)}, u32[]{:S(2)}) collective-permute-start(bf16[2,128,128]{2,1,0:T(8,128)(2,1)S(1)} %get-tuple-element.26.send_ref), channel_id=1, source_target_pairs={{0,8},{1,17},{2,10},{3,19},{4,12},{5,21},{6,14},{7,23},{8,0},{9,25... | collective-permute-start | bytes 196616 | tf_op jit(solution)/shard_map/ppermute | solution.py:237
  24.3 3.8 %collective-permute-done.5.got_ref = bf16[2,128,128]{2,1,0:T(8,128)(2,1)S(1)} collective-permute-done((bf16[2,128,128]{2,1,0:T(8,128)(2,1)S(1)}, bf16[2,128,128]{2,1,0:T(8,128)(2,1)S(1)}, u32[]{:S(2)}, u32[]{:S(2)}) %collective-permute-start.5) | collective-permute-done | bytes 65568 | tf_op jit(solution)/shard_map/ppermute | solution.py:237
  28.1 0.0 copy-start
  28.1 0.0 copy-start.1
  28.1 0.0 copy-start.4
  28.1 0.1 collective-permute-start.6
  28.2 0.0 copy-done.2
  28.2 0.0 copy-done.3
  28.2 0.7 %dense.1.dense_ref = f32[2,512,512]{2,1,0:T(8,128)S(1)} custom-call(bf16[2,512,512]{2,1,0:T(8,128)(2,1)S(1)} %copy-done.2, bf16[2,512,512]{2,1,0:T(8,128)(2,1)S(1)} %copy-done.3), custom_call_target="tpu_custom_call" | custom-call | tf_op jit(solution)/shard_map/dense/pallas_call | solution.py:274
  28.9 0.6 %collective-permute-done.6.other_last_ref = bf16[4,128,128]{2,1,0:T(8,128)(2,1)S(1)} collective-permute-done((bf16[4,128,128]{2,1,0:T(8,128)(2,1)S(1)}, bf16[4,128,128]{2,1,0:T(8,128)(2,1)S(1)}, u32[]{:S(2)}, u32[]{:S(2)}) %collective-permute-start.6) | collective-permute-done | bytes 131104 | tf_op jit(solution)/shard_map/ppermute | solution.py:237
  29.5 0.0 collective-permute-done.4.other_ref
  29.5 0.0 copy-done
  29.5 0.0 copy-done.1
  29.5 0.0 copy-done.4
  29.6 3.4 %final.1 = bf16[2,512,512]{2,1,0:T(8,128)(2,1)} custom-call(s32[1]{0:T(128)} %bitcast.position_ref, bf16[10,128,128]{2,1,0:T(8,128)(2,1)S(1)} %get-tuple-element.17.send_ref, bf16[10,128,128]{2,1,0:T(8,128)(2,1)S(1)} %collective-permute-done.got_ref, bf16[8,128,128]{2,1,0:T(8,128)(2,1)S(1)} %shard_map.77.mine_ref, ...), custom_call_target="tpu_custom_call" | custom-call | tf_op jit(solution)/shard_map/final/pallas_call | solution.py:306
  (6 shorter events, 0.2 us)
Async XLA Ops:
  2.0 26.2 %copy-start.2 = (bf16[2,512,512]{2,1,0:T(8,128)(2,1)S(1)}, bf16[2,512,512]{2,1,0:T(8,128)(2,1)}, u32[]{:S(2)}) copy-start(bf16[2,512,512]{2,1,0:T(8,128)(2,1)} %a_ref.1) | copy-start | bytes 3145732
  2.0 26.2 %copy-start.3 = (bf16[2,512,512]{2,1,0:T(8,128)(2,1)S(1)}, bf16[2,512,512]{2,1,0:T(8,128)(2,1)}, u32[]{:S(2)}) copy-start(bf16[2,512,512]{2,1,0:T(8,128)(2,1)} %b_ref.1) | copy-start | bytes 3145732
  2.0 1.8 %collective-permute-start = (bf16[10,128,128]{2,1,0:T(8,128)(2,1)S(1)}, bf16[10,128,128]{2,1,0:T(8,128)(2,1)S(1)}, u32[]{:S(2)}, u32[]{:S(2)}) collective-permute-start(bf16[10,128,128]{2,1,0:T(8,128)(2,1)S(1)} %get-tuple-element.17.send_ref), channel_id=1, source_target_pairs={{0,1},{1,0},{2,3},{3,2},{4,5},{5,4},{6,7},{7,6},{8,9},{9,8},{10,11... | collective-permute-start | bytes 983048 | tf_op jit(solution)/shard_map/ppermute | solution.py:237
  3.8 7.0 %collective-permute-start.1 = (bf16[4,128,128]{2,1,0:T(8,128)(2,1)S(1)}, bf16[4,128,128]{2,1,0:T(8,128)(2,1)S(1)}, u32[]{:S(2)}, u32[]{:S(2)}) collective-permute-start(bf16[4,128,128]{2,1,0:T(8,128)(2,1)S(1)} %get-tuple-element.18.send_ref), channel_id=1, source_target_pairs={{0,16},{1,3},{2,18},{3,1},{4,20},{5,7},{6,22},{7,5},{8,24},{9,11},... | collective-permute-start | bytes 393224 | tf_op jit(solution)/shard_map/ppermute | solution.py:237
  10.8 7.0 %collective-permute-start.2 = (bf16[6,128,128]{2,1,0:T(8,128)(2,1)S(1)}, bf16[6,128,128]{2,1,0:T(8,128)(2,1)S(1)}, u32[]{:S(2)}, u32[]{:S(2)}) collective-permute-start(bf16[6,128,128]{2,1,0:T(8,128)(2,1)S(1)} %get-tuple-element.20.send_ref), channel_id=1, source_target_pairs={{0,2},{1,5},{2,0},{3,7},{4,6},{5,1},{6,4},{7,3},{8,10},{9,13},{10,... | collective-permute-start | bytes 589832 | tf_op jit(solution)/shard_map/ppermute | solution.py:237
  17.8 5.0 %collective-permute-start.3 = (bf16[4,128,128]{2,1,0:T(8,128)(2,1)S(1)}, bf16[4,128,128]{2,1,0:T(8,128)(2,1)S(1)}, u32[]{:S(2)}, u32[]{:S(2)}) collective-permute-start(bf16[4,128,128]{2,1,0:T(8,128)(2,1)S(1)} %get-tuple-element.22.send_ref), channel_id=1, source_target_pairs={{0,4},{1,9},{2,6},{3,11},{4,0},{5,13},{6,2},{7,15},{8,12},{9,1},{1... | collective-permute-start | bytes 393224 | tf_op jit(solution)/shard_map/ppermute | solution.py:237
  22.9 6.6 %collective-permute-start.4 = (bf16[8,128,128]{2,1,0:T(8,128)(2,1)S(1)}, bf16[8,128,128]{2,1,0:T(8,128)(2,1)S(1)}, u32[]{:S(2)}, u32[]{:S(2)}) collective-permute-start(bf16[8,128,128]{2,1,0:T(8,128)(2,1)S(1)} %shard_map.77.mine_ref), channel_id=1, source_target_pairs={{0,1},{1,0},{2,3},{3,2},{4,5},{5,4},{6,7},{7,6},{8,9},{9,8},{10,11... | collective-permute-start | bytes 786440 | tf_op jit(solution)/shard_map/ppermute | solution.py:237
  23.0 5.0 %collective-permute-start.5 = (bf16[2,128,128]{2,1,0:T(8,128)(2,1)S(1)}, bf16[2,128,128]{2,1,0:T(8,128)(2,1)S(1)}, u32[]{:S(2)}, u32[]{:S(2)}) collective-permute-start(bf16[2,128,128]{2,1,0:T(8,128)(2,1)S(1)} %get-tuple-element.26.send_ref), channel_id=1, source_target_pairs={{0,8},{1,17},{2,10},{3,19},{4,12},{5,21},{6,14},{7,23},{8,0},{9,25... | collective-permute-start | bytes 196616 | tf_op jit(solution)/shard_map/ppermute | solution.py:237
  28.1 1.5 %copy-start = (bf16[1,4,2,128,128]{4,3,2,1,0:T(8,128)(2,1)S(1)}, bf16[1,4,2,128,128]{4,3,2,1,0:T(8,128)(2,1)}, u32[]{:S(2)}) copy-start(bf16[1,4,2,128,128]{4,3,2,1,0:T(8,128)(2,1)} %down_ref.1) | copy-start | bytes 786436
  28.1 1.4 %copy-start.1 = (bf16[1,2,4,128,128]{4,3,2,1,0:T(8,128)(2,1)S(1)}, bf16[1,2,4,128,128]{4,3,2,1,0:T(8,128)(2,1)}, u32[]{:S(2)}) copy-start(bf16[1,2,4,128,128]{4,3,2,1,0:T(8,128)(2,1)} %block_ref.1) | copy-start | bytes 786436
  28.1 1.4 %copy-start.4 = (bf16[2,2,512,128]{3,2,1,0:T(8,128)(2,1)S(1)}, bf16[2,2,512,128]{3,2,1,0:T(8,128)(2,1)}, u32[]{:S(2)}) copy-start(bf16[2,2,512,128]{3,2,1,0:T(8,128)(2,1)} %outer_ref.1) | copy-start | bytes 1572868
  28.1 1.4 %collective-permute-start.6 = (bf16[4,128,128]{2,1,0:T(8,128)(2,1)S(1)}, bf16[4,128,128]{2,1,0:T(8,128)(2,1)S(1)}, u32[]{:S(2)}, u32[]{:S(2)}) collective-permute-start(bf16[4,128,128]{2,1,0:T(8,128)(2,1)S(1)} %shard_map.78.last_ref), channel_id=1, source_target_pairs={{0,1},{1,0},{2,3},{3,2},{4,5},{5,4},{6,7},{7,6},{8,9},{9,8},{10,11... | collective-permute-start | bytes 393224 | tf_op jit(solution)/shard_map/ppermute | solution.py:237

commit v2 on v1

v2 whole, which is shorter than its diff:
```python
import functools

import jax
import jax.numpy as jnp
from jax import lax
from jax.experimental import pallas as pl
from jax.experimental.pallas import tpu as pltpu
from jax.sharding import PartitionSpec as P

AXES = ("row", "col")
BF16 = jnp.bfloat16
F32 = jnp.float32
VMEM = pltpu.VMEM


def contract(a, b, left, right):
    return lax.dot_general(a, b, (((left,), (right,)), ((), ())), preferred_element_type=F32)


def dot(a, b):
    return contract(a, b, 1, 0)


def lift(p, f, q):
    return dot(contract(p, f, 0, 0).astype(BF16), q)


def couple(k, f, k2):
    return dot(dot(k, f).astype(BF16), k2)


def lower(s, g, w):
    return contract(dot(s, g).astype(BF16), w, 1, 1)


def pick(first, first_ref, second_ref, i):
    return jnp.where(first, first_ref[i], second_ref[i])


def head_kernel(inner_hbm, up_hbm, down_hbm, block_hbm, send_ref, leaf_ref, inner, up, sems):
    copies = [
        pltpu.make_async_copy(inner_hbm, inner, sems.at[0]),
        pltpu.make_async_copy(up_hbm.at[0, 0:3], up, sems.at[1]),
        pltpu.make_async_copy(up_hbm.at[0, 3], send_ref.at[2:4], sems.at[2]),
        pltpu.make_async_copy(down_hbm.at[0, 3], send_ref.at[4:6], sems.at[3]),
        pltpu.make_async_copy(block_hbm.at[0, 1], send_ref.at[6:10], sems.at[4]),
    ]
    for copy in copies:
        copy.start()
    copies[0].wait()
    leaves = [contract(inner[i, 0], inner[i, 1], 0, 0).astype(BF16) for i in range(2)]
    copies[1].wait()
    total = None
    for i in range(2):
        leaf_ref[i] = leaves[i]
        t = lift(up[i, 0], leaves[i], up[i, 1])
        total = t if total is None else total + t
    f0 = total.astype(BF16)
    send_ref[0] = f0
    send_ref[1] = lift(up[2, 0], f0, up[2, 1]).astype(BF16)
    for copy in copies[2:]:
        copy.wait()


def climb(low, r, levels, send_ref, got_ref, out_ref):
    f = (send_ref[1].astype(F32) + got_ref[1].astype(F32)).astype(BF16)
    out_ref[0] = f
    if r + 1 < levels - 1:
        p = pick(low, send_ref, got_ref, 2)
        q = pick(low, send_ref, got_ref, 3)
        out_ref[1] = lift(p, f, q).astype(BF16)
        out_ref[2] = pick(low, got_ref, send_ref, 2)
        out_ref[3] = pick(low, got_ref, send_ref, 3)


def start_kernel(levels, position_ref, send_ref, got_ref, out_ref, carry_ref):
    position = position_ref[0]
    odd = (position & 1) == 1
    high = ((position >> (levels - 2)) & 1) == 1

    @pl.when(odd)
    def _():
        climb(False, 0, levels, send_ref, got_ref, out_ref)

    @pl.when(position == (1 << (levels - 1)) - 1)
    def _():
        out_ref[2:4] = send_ref[7:9]

    @pl.when(jnp.logical_not(odd))
    def _():
        carry_ref[...] = got_ref[4:10]
        out_ref[0] = jnp.where(high, got_ref[6], got_ref[7])
        out_ref[1] = jnp.where(high, got_ref[9], got_ref[8])


def sent(j, levels):
    return 6 if j <= levels - 4 else 4


def fill(j, levels, position, carry_ref, out_ref):
    if sent(j, levels) == 6:
        out_ref[0:6] = carry_ref[...]
        return
    low = ((position >> j) & 1) == 0

    @pl.when(low)
    def _():
        out_ref[0:2] = carry_ref[0:2]
        out_ref[2:4] = carry_ref[3:5]

    @pl.when(jnp.logical_not(low))
    def _():
        out_ref[0:4] = carry_ref[2:6]


def round_kernel(r, levels, position_ref, send_ref, got_ref, carry_ref, out_ref, new_ref, *node_refs):
    position = position_ref[0]
    odd = (position & 1) == 1

    @pl.when(odd)
    def _():
        low = ((position >> r) & 1) == 0
        climb(low, r, levels, send_ref, got_ref, out_ref)
        if r == levels - 2:
            @pl.when(((position >> (levels - 1)) & 1) == 0)
            def _():
                k1 = pick(low, got_ref, send_ref, 2)
                k2 = pick(low, got_ref, send_ref, 3)
                out_ref[0] = couple(k1, out_ref[0], k2).astype(BF16)

    @pl.when(jnp.logical_not(odd))
    def _():
        if r == 1:
            mask = (1 << (levels - 3)) - 1
            top = ((position >> 1) & mask) == mask
            new_ref[...] = carry_ref[...]

            @pl.when(top)
            def _():
                low = ((position >> (levels - 2)) & 1) == 0
                for i, own in ((0, 2), (1, 5)):
                    new_ref[2 + i] = jnp.where(low, carry_ref[own], got_ref[i])
                    new_ref[4 + i] = jnp.where(low, got_ref[i], carry_ref[own])

            fill(1, levels, position, new_ref, out_ref)
            return
        j = r - 1
        (node_ref,) = node_refs
        low = ((position >> j) & 1) == 0
        full = sent(j, levels) == 6

        @pl.when(low)
        def _():
            node_ref[0:3] = carry_ref[0:3]
            node_ref[3] = carry_ref[5]
            new_ref[...] = got_ref[0 : new_ref.shape[0]]

        @pl.when(jnp.logical_not(low))
        def _():
            node_ref[0:2] = got_ref[0:2]
            node_ref[2:4] = got_ref[3:5] if full else got_ref[2:4]
            new_ref[...] = carry_ref[...] if full else carry_ref[2:6]

        if full:
            fill(j + 1, levels, position, new_ref, out_ref)


def pack_kernel(count, position_ref, *refs):
    odd = (position_ref[0] & 1) == 1
    received, nodes, top_ref, out_ref = refs[:count], refs[count:-2], refs[-2], refs[-1]

    @pl.when(odd)
    def _():
        for i, ref in enumerate(received):
            out_ref[i] = ref[0]

    @pl.when(jnp.logical_not(odd))
    def _():
        for i, ref in enumerate(nodes):
            out_ref[4 * i : 4 * i + 4] = ref[...]
        out_ref[4 * len(nodes) : 4 * len(nodes) + 4] = top_ref[...]


def dense_kernel(a_ref, b_ref, o_ref):
    for i in range(2):
        o_ref[i] = dot(a_ref[i], b_ref[i])


def first_node(odd, send_ref, got_ref, i):
    left, right = ((4, 4), (5, 5), (6, 7), (9, 8))[i]
    return jnp.where(odd, got_ref[right], send_ref[left])


def prepare_kernel(
    position_ref, send_ref, got_ref, leaf_ref, down_ref, block_ref, base_ref, left_ref, right_ref
):
    odd = (position_ref[0] & 1) == 1
    near = couple(
        first_node(odd, send_ref, got_ref, 2), got_ref[0], first_node(odd, send_ref, got_ref, 3)
    ).astype(BF16)
    for i in range(2):
        s, w = down_ref[0, i, 0], down_ref[0, i, 1]
        leaf = couple(block_ref[0, 0, i], leaf_ref[1 - i], block_ref[0, 0, 3 - i])
        base_ref[i] = leaf + lower(s, near, w)
        left_ref[i] = dot(s, down_ref[0, 2, 0]).astype(BF16)
        right_ref[i] = contract(down_ref[0, 2, 1], w, 0, 1).astype(BF16)


def upper_kernel(
    levels, position_ref, send_ref, got_ref, mine_ref, other_ref, base_ref, left_ref, right_ref
):
    position = position_ref[0]
    odd = (position & 1) == 1
    in_left = ((position >> (levels - 1)) & 1) == 0

    def inner(height):
        return pick(odd, mine_ref, other_ref, height - 1)

    def generator(height, i):
        if height == 1:
            return first_node(odd, send_ref, got_ref, i)
        slot = 4 * (height - 2) + i
        if height >= levels - 1:
            slot = 4 * (levels - 3) + 2 * (height - levels + 1) + i - 2
        return pick(odd, other_ref, mine_ref, slot)

    base = None
    left, right = generator(levels, 2), generator(levels, 3)
    for height in range(levels - 1, 1, -1):
        near = couple(generator(height, 2), inner(height - 1), generator(height, 3))
        s, w = generator(height - 1, 0), generator(height - 1, 1)
        if base is None:
            left = jnp.where(in_left, dot(s, left), s.astype(F32)).astype(BF16)
            right = jnp.where(in_left, contract(right, w, 1, 1), w.astype(F32).T).astype(BF16)
        else:
            left = dot(s, left).astype(BF16)
            right = contract(right, w, 1, 1).astype(BF16)
        base = near if base is None else near + lower(s, base.astype(BF16), w)
    base_ref[0] = base
    left_ref[0] = left
    right_ref[0] = right


def final_kernel(
    position_ref, last_ref, other_last_ref, base_ref, left_ref, right_ref, leaf_base_ref,
    leaf_left_ref, leaf_right_ref, dense_ref, outer_ref, out_hbm, out, sems,
):
    odd = (position_ref[0] & 1) == 1
    f = pick(odd, last_ref, other_last_ref, 0)
    g = (base_ref[0] + couple(left_ref[0], f, right_ref[0])).astype(BF16)
    copies = []
    for i in range(2):
        gb = leaf_base_ref[i] + couple(leaf_left_ref[i], g, leaf_right_ref[i])
        e = dot(outer_ref[i, 0], gb.astype(BF16)).astype(BF16)
        out[i] = (dense_ref[i] + contract(e, outer_ref[i, 1], 1, 1)).astype(BF16)
        copies.append(pltpu.make_async_copy(out.at[i], out_hbm.at[i], sems.at[i]))
        copies[-1].start()
    for copy in copies:
        copy.wait()


def in_vmem(n, scalar=True):
    specs = [pl.BlockSpec(memory_space=VMEM)] * n
    return [pl.BlockSpec(memory_space=pltpu.SMEM)] + specs if scalar else specs


def small(mib=2):
    return pltpu.CompilerParams(vmem_limit_bytes=mib << 20)


def exchange(block, count, odd_bit, even_bit):
    route = [(p, p ^ (1 << (odd_bit if p & 1 else even_bit))) for p in range(count)]
    return lax.ppermute(block, AXES, route)


def stages(dense_a, dense_b, inner_basis_stack, outer_basis_stack, ascent, descent, couplings):
    count = lax.axis_size("row") * lax.axis_size("col")
    levels = count.bit_length() - 1
    rank = ascent.shape[-1]
    place = lax.axis_index(AXES).reshape(1).astype(jnp.int32)

    def mats(n, dtype=BF16):
        return jax.ShapeDtypeStruct((n, rank, rank), dtype)

    def call(kernel, outs, *refs, **extra):
        return pl.pallas_call(
            kernel,
            out_shape=tuple(mats(n) if n > 0 else mats(-n, F32) for n in outs),
            in_specs=in_vmem(len(refs)),
            out_specs=tuple(in_vmem(len(outs), False)),
            compiler_params=small(),
        )(place, *refs)

    send, leaf_inner = pl.pallas_call(
        head_kernel,
        out_shape=(mats(10), mats(2)),
        in_specs=[pl.BlockSpec(memory_space=pltpu.HBM)] * 4,
        out_specs=tuple(in_vmem(2, False)),
        scratch_shapes=[
            VMEM(inner_basis_stack.shape, BF16),
            VMEM((3, 2, rank, rank), BF16),
            pltpu.SemaphoreType.DMA((5,)),
        ],
        compiler_params=small(4),
        name="head",
    )(*[
        pltpu.with_memory_space_constraint(x, pltpu.HBM)
        for x in (inner_basis_stack, ascent, descent, couplings)
    ])
    dense = pl.pallas_call(
        dense_kernel,
        out_shape=jax.ShapeDtypeStruct(dense_a.shape, F32),
        in_specs=in_vmem(2, False),
        out_specs=in_vmem(1, False)[0],
        compiler_params=small(8),
        name="dense",
    )(dense_a, dense_b)

    def width(r):
        climbing = 4 if r <= levels - 2 else 1
        return climbing if r in (1, levels - 1) else max(climbing, sent(r - 1, levels))

    got = exchange(send, count, 0, 0)
    block, carry = call(functools.partial(start_kernel, levels), (width(1), 6), send, got)
    leaf_terms = call(prepare_kernel, (-2, 2, 2), send, got, leaf_inner, descent, couplings)
    received, nodes = [], []
    for r in range(1, levels - 1):
        new = exchange(block, count, r, levels - 2 if r == 1 else r - 1)
        received.append(new)
        outs = (width(r + 1), 4 if r == levels - 2 else 6) + ((4,) if r > 1 else ())
        kernel = functools.partial(round_kernel, r, levels)
        block, carry, *node = call(kernel, outs, block, new, carry)
        nodes += node
    last = exchange(block, count, levels - 1, 1)

    size = 4 * len(nodes) + 4
    kernel = functools.partial(pack_kernel, len(received))
    (mine,) = call(kernel, (size,), *received, *nodes, carry)
    other = exchange(mine, count, 0, 0)
    kernel = functools.partial(upper_kernel, levels)
    upper_terms = call(kernel, (-1, 1, 1), send, got, mine, other)
    other_last = exchange(last, count, 0, 0)

    return pl.pallas_call(
        final_kernel,
        out_shape=jax.ShapeDtypeStruct(dense.shape, BF16),
        in_specs=in_vmem(10),
        out_specs=pl.BlockSpec(memory_space=pltpu.HBM),
        scratch_shapes=[VMEM(dense.shape, BF16), pltpu.SemaphoreType.DMA((2,))],
        compiler_params=small(12),
        name="final",
    )(place, last, other_last, *upper_terms, *leaf_terms, dense, outer_basis_stack)


def solution(mesh):
    placed = (
        P(AXES, None, None),
        P(AXES, None, None),
        P(AXES, None, None, None),
        P(AXES, None, None, None),
        P(AXES, None, None, None, None),
        P(AXES, None, None, None, None),
        P(AXES, None, None, None, None),
    )
    return jax.shard_map(
        stages, mesh=mesh, in_specs=placed, out_specs=P(AXES, None, None), check_vma=False
    )
```

time: 33.1 us -> 30.1 us (0.909)
  waiting for transfers between devices: 15.2 us -> 12.9 us
  starting transfers between devices: 11.3 us -> 10.2 us
  Pallas kernels: 6.19 us -> 6.71 us
    ppermute x7, waiting for transfers between devices: 15.2 us -> 12.9 us  [exchange(): return lax.ppermute(block, AXES, route)]
    ppermute x7, starting transfers between devices: 11.3 us -> 10.2 us  [exchange(): return lax.ppermute(block, AXES, route)]
    pallas_call x7 -> x8, Pallas kernels: 3.54 us -> 3.91 us  [the longest x1 2.27 us: stages(): pl.pallas_call(final_kernel, out_shape=jax.ShapeDtypeStruct(dense.shape,...]
  transfers between devices with their start and end apart: 7 -> 7, of which waited for: 6 -> 5; matrix products, arithmetic and copies ran while one was open for 0% -> 0% of each run, Pallas kernels for 2% -> 7%
where the time goes in v2:
time: 30.1 us; the launch traced here: 30 us
  waiting for transfers between devices  12.9 us (43%)
  starting transfers between devices  10.2 us (34%)
  Pallas kernels  6.71 us (22%)
    ppermute x7, waiting for transfers between devices, exchange(): return lax.ppermute(block, AXES, route)  12.9 us
    ppermute x7, starting transfers between devices, exchange(): return lax.ppermute(block, AXES, route)  10.2 us
    pallas_call x1, Pallas kernels, stages(): pl.pallas_call(final_kernel, out_shape=jax.ShapeDtypeStruct(dense.shape,...  2.27 us
    pallas_call x1, Pallas kernels, stages(): pl.pallas_call(head_kernel, out_shape=(mats(10), mats(2)), in_specs=[pl.B...  2.09 us
    pallas_call x7, Pallas kernels, call(): pl.pallas_call(kernel, out_shape=tuple((mats(n) if n > 0 else mats(-n, F3...  1.64 us
    pallas_call x1, Pallas kernels, stages(): pl.pallas_call(dense_kernel, out_shape=jax.ShapeDtypeStruct(dense_a.shape...  0.71 us
  transfers between devices with their start and end apart: 7, of which 5 were waited for; matrix products, arithmetic and copies ran while one was open for 0% of the time, Pallas kernels for 7%

profile of v2, /device:TPU:0, one launch (start us, length us, event | category | flops | bytes accessed | tf_op | source)
XLA Modules:
  0.0 30.0 jit_solution(506953911514951715)
XLA Ops:
  0.0 0.0 copy-start.3
  0.0 0.0 copy-start.2
  0.0 2.1 %head.1 = (bf16[10,128,128]{2,1,0:T(8,128)(2,1)S(1)}, bf16[2,128,128]{2,1,0:T(8,128)(2,1)S(1)}) custom-call(bf16[2,2,512,128]{3,2,1,0:T(8,128)(2,1)} %inner_hbm.1, bf16[1,4,2,128,128]{4,3,2,1,0:T(8,128)(2,1)} %up_hbm.1, bf16[1,4,2,128,128]{4,3,2,1,0:T(8,128)(2,1)} %down_ref.1, bf16[1,2,4,128,128]{4,3,2,1,0:T(8,128)(2,1)} %block_ref.1), custom_call_target="tpu_custom_call" | custom-call | tf_op jit(solution)/shard_map/head/pallas_call | solution.py:294
  2.1 0.6 %collective-permute-start = (bf16[10,128,128]{2,1,0:T(8,128)(2,1)S(1)}, bf16[10,128,128]{2,1,0:T(8,128)(2,1)S(1)}, u32[]{:S(2)}, u32[]{:S(2)}) collective-permute-start(bf16[10,128,128]{2,1,0:T(8,128)(2,1)S(1)} %get-tuple-element.23.send_ref), channel_id=1, source_target_pairs={{0,1},{1,0},{2,3},{3,2},{4,5},{5,4},{6,7},{7,6},{8,9},{9,8},{10,11... | collective-permute-start | bytes 983048 | tf_op jit(solution)/shard_map/ppermute | solution.py:273
  2.7 1.3 %collective-permute-done.got_ref = bf16[10,128,128]{2,1,0:T(8,128)(2,1)S(1)} collective-permute-done((bf16[10,128,128]{2,1,0:T(8,128)(2,1)S(1)}, bf16[10,128,128]{2,1,0:T(8,128)(2,1)S(1)}, u32[]{:S(2)}, u32[]{:S(2)}) %collective-permute-start) | collective-permute-done | bytes 327712 | tf_op jit(solution)/shard_map/ppermute | solution.py:273
  4.0 3.0 %collective-permute-start.1 = (bf16[4,128,128]{2,1,0:T(8,128)(2,1)S(1)}, bf16[4,128,128]{2,1,0:T(8,128)(2,1)S(1)}, u32[]{:S(2)}, u32[]{:S(2)}) collective-permute-start(bf16[4,128,128]{2,1,0:T(8,128)(2,1)S(1)} %get-tuple-element.24.send_ref), channel_id=1, source_target_pairs={{0,8},{1,3},{2,10},{3,1},{4,12},{5,7},{6,14},{7,5},{8,0},{9,11},{1... | collective-permute-start | bytes 393224 | tf_op jit(solution)/shard_map/ppermute | solution.py:273
  7.0 2.9 %collective-permute-done.1.got_ref.refs_0_ = bf16[4,128,128]{2,1,0:T(8,128)(2,1)S(1)} collective-permute-done((bf16[4,128,128]{2,1,0:T(8,128)(2,1)S(1)}, bf16[4,128,128]{2,1,0:T(8,128)(2,1)S(1)}, u32[]{:S(2)}, u32[]{:S(2)}) %collective-permute-start.1) | collective-permute-done | bytes 131104 | tf_op jit(solution)/shard_map/ppermute | solution.py:273
  9.9 2.0 %collective-permute-start.2 = (bf16[6,128,128]{2,1,0:T(8,128)(2,1)S(1)}, bf16[6,128,128]{2,1,0:T(8,128)(2,1)S(1)}, u32[]{:S(2)}, u32[]{:S(2)}) collective-permute-start(bf16[6,128,128]{2,1,0:T(8,128)(2,1)S(1)} %get-tuple-element.26.send_ref), channel_id=1, source_target_pairs={{0,2},{1,5},{2,0},{3,7},{4,6},{5,1},{6,4},{7,3},{8,10},{9,13},{10,... | collective-permute-start | bytes 589832 | tf_op jit(solution)/shard_map/ppermute | solution.py:273
  12.0 3.7 %collective-permute-done.2.got_ref.refs_1_ = bf16[6,128,128]{2,1,0:T(8,128)(2,1)S(1)} collective-permute-done((bf16[6,128,128]{2,1,0:T(8,128)(2,1)S(1)}, bf16[6,128,128]{2,1,0:T(8,128)(2,1)S(1)}, u32[]{:S(2)}, u32[]{:S(2)}) %collective-permute-start.2) | collective-permute-done | bytes 196640 | tf_op jit(solution)/shard_map/ppermute | solution.py:273
  15.7 2.0 %collective-permute-start.3 = (bf16[4,128,128]{2,1,0:T(8,128)(2,1)S(1)}, bf16[4,128,128]{2,1,0:T(8,128)(2,1)S(1)}, u32[]{:S(2)}, u32[]{:S(2)}) collective-permute-start(bf16[4,128,128]{2,1,0:T(8,128)(2,1)S(1)} %get-tuple-element.28.send_ref), channel_id=1, source_target_pairs={{0,4},{1,9},{2,6},{3,11},{4,0},{5,13},{6,2},{7,15},{8,12},{9,1},{1... | collective-permute-start | bytes 393224 | tf_op jit(solution)/shard_map/ppermute | solution.py:273
  17.7 3.0 %collective-permute-done.3.got_ref.refs_2_ = bf16[4,128,128]{2,1,0:T(8,128)(2,1)S(1)} collective-permute-done((bf16[4,128,128]{2,1,0:T(8,128)(2,1)S(1)}, bf16[4,128,128]{2,1,0:T(8,128)(2,1)S(1)}, u32[]{:S(2)}, u32[]{:S(2)}) %collective-permute-start.3) | collective-permute-done | bytes 131104 | tf_op jit(solution)/shard_map/ppermute | solution.py:273
  20.8 0.1 collective-permute-start.6
  20.9 0.0 copy-start
  20.9 0.0 copy-start.1
  20.9 2.0 %collective-permute-start.4 = (bf16[1,128,128]{2,1,0:T(8,128)(2,1)S(1)}, bf16[1,128,128]{2,1,0:T(8,128)(2,1)S(1)}, u32[]{:S(2)}, u32[]{:S(2)}) collective-permute-start(bf16[1,128,128]{2,1,0:T(8,128)(2,1)S(1)} %get-tuple-element.30), channel_id=1, source_target_pairs={{0,2},{1,17},{2,0},{3,19},{4,6},{5,21},{6,4},{7,23},{8,10},{9,25},... | collective-permute-start | bytes 98312 | tf_op jit(solution)/shard_map/ppermute | solution.py:273
  23.0 2.0 %collective-permute-done.4.last_ref = bf16[1,128,128]{2,1,0:T(8,128)(2,1)S(1)} collective-permute-done((bf16[1,128,128]{2,1,0:T(8,128)(2,1)S(1)}, bf16[1,128,128]{2,1,0:T(8,128)(2,1)S(1)}, u32[]{:S(2)}, u32[]{:S(2)}) %collective-permute-start.4) | collective-permute-done | bytes 32800 | tf_op jit(solution)/shard_map/ppermute | solution.py:273
  24.9 0.6 %collective-permute-start.5 = (bf16[1,128,128]{2,1,0:T(8,128)(2,1)S(1)}, bf16[1,128,128]{2,1,0:T(8,128)(2,1)S(1)}, u32[]{:S(2)}, u32[]{:S(2)}) collective-permute-start(bf16[1,128,128]{2,1,0:T(8,128)(2,1)S(1)} %collective-permute-done.4.last_ref), channel_id=1, source_target_pairs={{0,1},{1,0},{2,3},{3,2},{4,5},{5,4},{6,7},{7,6},{8,9},{9,8},{10,11... | collective-permute-start | bytes 98312 | tf_op jit(solution)/shard_map/ppermute | solution.py:273
  25.5 0.0 copy-done.3
  25.5 0.0 copy-done.2
  25.5 0.7 %dense.1.dense_ref = f32[2,512,512]{2,1,0:T(8,128)S(1)} custom-call(bf16[2,512,512]{2,1,0:T(8,128)(2,1)S(1)} %copy-done.2, bf16[2,512,512]{2,1,0:T(8,128)(2,1)S(1)} %copy-done.3), custom_call_target="tpu_custom_call" | custom-call | tf_op jit(solution)/shard_map/dense/pallas_call | solution.py:310
  26.2 0.0 copy-start.4
  26.2 0.0 copy-done
  26.2 0.0 copy-done.1
  26.2 0.7 %shard_map.79 = (f32[2,128,128]{2,1,0:T(8,128)S(1)}, bf16[2,128,128]{2,1,0:T(8,128)(2,1)S(1)}, bf16[2,128,128]{2,1,0:T(8,128)(2,1)S(1)}) custom-call(s32[1]{0:T(128)} %bitcast.position_ref, bf16[10,128,128]{2,1,0:T(8,128)(2,1)S(1)} %get-tuple-element.23.send_ref, bf16[10,128,128]{2,1,0:T(8,128)(2,1)S(1)} %collective-permute-done.got_ref, ...), custom_call_target="tpu_custom_call" | custom-call | tf_op jit(solution)/shard_map/pallas_call | solution.py:286
  26.9 0.0 collective-permute-done.6.other_ref
  26.9 0.8 %shard_map.78 = (f32[1,128,128]{2,1,0:T(8,128)S(1)}, bf16[1,128,128]{2,1,0:T(8,128)(2,1)S(1)}, bf16[1,128,128]{2,1,0:T(8,128)(2,1)S(1)}) custom-call(s32[1]{0:T(128)} %bitcast.position_ref, bf16[10,128,128]{2,1,0:T(8,128)(2,1)S(1)} %get-tuple-element.23.send_ref, bf16[10,128,128]{2,1,0:T(8,128)(2,1)S(1)} %collective-permute-done.got_ref, ...), custom_call_target="tpu_custom_call" | custom-call | tf_op jit(solution)/shard_map/pallas_call | solution.py:286
  27.7 0.0 collective-permute-done.5.other_last_ref
  27.7 0.0 copy-done.4
  27.7 2.3 %final.1 = bf16[2,512,512]{2,1,0:T(8,128)(2,1)} custom-call(s32[1]{0:T(128)} %bitcast.position_ref, bf16[1,128,128]{2,1,0:T(8,128)(2,1)S(1)} %collective-permute-done.4.last_ref, bf16[1,128,128]{2,1,0:T(8,128)(2,1)S(1)} %collective-permute-done.5.other_last_ref, f32[1,128,128]{2,1,0:T(8,128)S(1)} %get-tuple-element.34.base_ref, ...), custom_call_target="tpu_custom_call" | custom-call | tf_op jit(solution)/shard_map/final/pallas_call | solution.py:344
  (5 shorter events, 0.2 us)
Async XLA Ops:
  0.0 25.5 %copy-start.3 = (bf16[2,512,512]{2,1,0:T(8,128)(2,1)S(1)}, bf16[2,512,512]{2,1,0:T(8,128)(2,1)}, u32[]{:S(2)}) copy-start(bf16[2,512,512]{2,1,0:T(8,128)(2,1)} %b_ref.1) | copy-start | bytes 3145732
  0.0 25.5 %copy-start.2 = (bf16[2,512,512]{2,1,0:T(8,128)(2,1)S(1)}, bf16[2,512,512]{2,1,0:T(8,128)(2,1)}, u32[]{:S(2)}) copy-start(bf16[2,512,512]{2,1,0:T(8,128)(2,1)} %a_ref.1) | copy-start | bytes 3145732
  2.1 1.8 %collective-permute-start = (bf16[10,128,128]{2,1,0:T(8,128)(2,1)S(1)}, bf16[10,128,128]{2,1,0:T(8,128)(2,1)S(1)}, u32[]{:S(2)}, u32[]{:S(2)}) collective-permute-start(bf16[10,128,128]{2,1,0:T(8,128)(2,1)S(1)} %get-tuple-element.23.send_ref), channel_id=1, source_target_pairs={{0,1},{1,0},{2,3},{3,2},{4,5},{5,4},{6,7},{7,6},{8,9},{9,8},{10,11... | collective-permute-start | bytes 983048 | tf_op jit(solution)/shard_map/ppermute | solution.py:273
  4.0 5.9 %collective-permute-start.1 = (bf16[4,128,128]{2,1,0:T(8,128)(2,1)S(1)}, bf16[4,128,128]{2,1,0:T(8,128)(2,1)S(1)}, u32[]{:S(2)}, u32[]{:S(2)}) collective-permute-start(bf16[4,128,128]{2,1,0:T(8,128)(2,1)S(1)} %get-tuple-element.24.send_ref), channel_id=1, source_target_pairs={{0,8},{1,3},{2,10},{3,1},{4,12},{5,7},{6,14},{7,5},{8,0},{9,11},{1... | collective-permute-start | bytes 393224 | tf_op jit(solution)/shard_map/ppermute | solution.py:273
  9.9 5.7 %collective-permute-start.2 = (bf16[6,128,128]{2,1,0:T(8,128)(2,1)S(1)}, bf16[6,128,128]{2,1,0:T(8,128)(2,1)S(1)}, u32[]{:S(2)}, u32[]{:S(2)}) collective-permute-start(bf16[6,128,128]{2,1,0:T(8,128)(2,1)S(1)} %get-tuple-element.26.send_ref), channel_id=1, source_target_pairs={{0,2},{1,5},{2,0},{3,7},{4,6},{5,1},{6,4},{7,3},{8,10},{9,13},{10,... | collective-permute-start | bytes 589832 | tf_op jit(solution)/shard_map/ppermute | solution.py:273
  15.7 5.0 %collective-permute-start.3 = (bf16[4,128,128]{2,1,0:T(8,128)(2,1)S(1)}, bf16[4,128,128]{2,1,0:T(8,128)(2,1)S(1)}, u32[]{:S(2)}, u32[]{:S(2)}) collective-permute-start(bf16[4,128,128]{2,1,0:T(8,128)(2,1)S(1)} %get-tuple-element.28.send_ref), channel_id=1, source_target_pairs={{0,4},{1,9},{2,6},{3,11},{4,0},{5,13},{6,2},{7,15},{8,12},{9,1},{1... | collective-permute-start | bytes 393224 | tf_op jit(solution)/shard_map/ppermute | solution.py:273
  20.8 6.1 %collective-permute-start.6 = (bf16[12,128,128]{2,1,0:T(8,128)(2,1)S(1)}, bf16[12,128,128]{2,1,0:T(8,128)(2,1)S(1)}, u32[]{:S(2)}, u32[]{:S(2)}) collective-permute-start(bf16[12,128,128]{2,1,0:T(8,128)(2,1)S(1)} %shard_map.77.mine_ref), channel_id=1, source_target_pairs={{0,1},{1,0},{2,3},{3,2},{4,5},{5,4},{6,7},{7,6},{8,9},{9,8},{10,11... | collective-permute-start | bytes 1179656 | tf_op jit(solution)/shard_map/ppermute | solution.py:273
  20.9 5.3 %copy-start = (bf16[1,4,2,128,128]{4,3,2,1,0:T(8,128)(2,1)S(1)}, bf16[1,4,2,128,128]{4,3,2,1,0:T(8,128)(2,1)}, u32[]{:S(2)}) copy-start(bf16[1,4,2,128,128]{4,3,2,1,0:T(8,128)(2,1)} %down_ref.1) | copy-start | bytes 786436
  20.9 5.3 %copy-start.1 = (bf16[1,2,4,128,128]{4,3,2,1,0:T(8,128)(2,1)S(1)}, bf16[1,2,4,128,128]{4,3,2,1,0:T(8,128)(2,1)}, u32[]{:S(2)}) copy-start(bf16[1,2,4,128,128]{4,3,2,1,0:T(8,128)(2,1)} %block_ref.1) | copy-start | bytes 786436
  20.9 4.0 %collective-permute-start.4 = (bf16[1,128,128]{2,1,0:T(8,128)(2,1)S(1)}, bf16[1,128,128]{2,1,0:T(8,128)(2,1)S(1)}, u32[]{:S(2)}, u32[]{:S(2)}) collective-permute-start(bf16[1,128,128]{2,1,0:T(8,128)(2,1)S(1)} %get-tuple-element.30), channel_id=1, source_target_pairs={{0,2},{1,17},{2,0},{3,19},{4,6},{5,21},{6,4},{7,23},{8,10},{9,25},... | collective-permute-start | bytes 98312 | tf_op jit(solution)/shard_map/ppermute | solution.py:273
  24.9 2.8 %collective-permute-start.5 = (bf16[1,128,128]{2,1,0:T(8,128)(2,1)S(1)}, bf16[1,128,128]{2,1,0:T(8,128)(2,1)S(1)}, u32[]{:S(2)}, u32[]{:S(2)}) collective-permute-start(bf16[1,128,128]{2,1,0:T(8,128)(2,1)S(1)} %collective-permute-done.4.last_ref), channel_id=1, source_target_pairs={{0,1},{1,0},{2,3},{3,2},{4,5},{5,4},{6,7},{7,6},{8,9},{9,8},{10,11... | collective-permute-start | bytes 98312 | tf_op jit(solution)/shard_map/ppermute | solution.py:273
  26.2 1.5 %copy-start.4 = (bf16[2,2,512,128]{3,2,1,0:T(8,128)(2,1)S(1)}, bf16[2,2,512,128]{3,2,1,0:T(8,128)(2,1)}, u32[]{:S(2)}) copy-start(bf16[2,2,512,128]{3,2,1,0:T(8,128)(2,1)} %outer_ref.1) | copy-start | bytes 1572868

commit v3 on v2

--- a/solution.py
+++ b/solution.py
@@ -11,6 +11,7 @@
 BF16 = jnp.bfloat16
 F32 = jnp.float32
 VMEM = pltpu.VMEM
+CHUNKS = 2
 
 
 def contract(a, b, left, right):
@@ -37,29 +38,42 @@
     return jnp.where(first, first_ref[i], second_ref[i])
 
 
-def head_kernel(inner_hbm, up_hbm, down_hbm, block_hbm, send_ref, leaf_ref, inner, up, sems):
+def head_kernel(
+    levels, position_ref, inner_hbm, up_hbm, down_hbm, block_hbm,
+    send_ref, pq_ref, swk_ref, leaf_ref, inner, up, sems,
+):
     copies = [
-        pltpu.make_async_copy(inner_hbm, inner, sems.at[0]),
-        pltpu.make_async_copy(up_hbm.at[0, 0:3], up, sems.at[1]),
-        pltpu.make_async_copy(up_hbm.at[0, 3], send_ref.at[2:4], sems.at[2]),
-        pltpu.make_async_copy(down_hbm.at[0, 3], send_ref.at[4:6], sems.at[3]),
-        pltpu.make_async_copy(block_hbm.at[0, 1], send_ref.at[6:10], sems.at[4]),
+        pltpu.make_async_copy(up_hbm.at[0, 0:3], up, sems.at[0]),
+        pltpu.make_async_copy(inner_hbm.at[0], inner.at[0], sems.at[1]),
+        pltpu.make_async_copy(inner_hbm.at[1], inner.at[1], sems.at[2]),
+        pltpu.make_async_copy(up_hbm.at[0, 3], pq_ref, sems.at[3]),
+        pltpu.make_async_copy(down_hbm.at[0, 3], swk_ref.at[0:2], sems.at[4]),
+        pltpu.make_async_copy(block_hbm.at[0, 1], swk_ref.at[2:6], sems.at[5]),
     ]
     for copy in copies:
         copy.start()
     copies[0].wait()
-    leaves = [contract(inner[i, 0], inner[i, 1], 0, 0).astype(BF16) for i in range(2)]
-    copies[1].wait()
-    total = None
+    twice = [[dot(up[i, k], up[2, k]).astype(BF16) for k in range(2)] for i in range(2)]
+    leaves = []
     for i in range(2):
+        copies[1 + i].wait()
+        leaves.append(contract(inner[i, 0], inner[i, 1], 0, 0).astype(BF16))
         leaf_ref[i] = leaves[i]
-        t = lift(up[i, 0], leaves[i], up[i, 1])
-        total = t if total is None else total + t
-    f0 = total.astype(BF16)
-    send_ref[0] = f0
-    send_ref[1] = lift(up[2, 0], f0, up[2, 1]).astype(BF16)
-    for copy in copies[2:]:
+    halves = [
+        (contract(up[i, 0], leaves[i], 0, 0).astype(BF16),
+         contract(twice[i][0], leaves[i], 0, 0).astype(BF16))
+        for i in range(2)
+    ]
+    f = [dot(halves[i][0], up[i, 1]) for i in range(2)]
+    t = [dot(halves[i][1], twice[i][1]) for i in range(2)]
+    send_ref[0] = (f[0] + f[1]).astype(BF16)
+    send_ref[1] = (t[0] + t[1]).astype(BF16)
+    for copy in copies[3:]:
         copy.wait()
+    odd = (position_ref[0] & 1) == 1
+    high = (position_ref[0] >> (levels - 2)) & 1
+    send_ref[2] = jnp.where(odd, swk_ref[3 - high], pq_ref[0])
+    send_ref[3] = jnp.where(odd, swk_ref[4 + high], pq_ref[1])
 
 
 def climb(low, r, levels, send_ref, got_ref, out_ref):
@@ -73,24 +87,22 @@
         out_ref[3] = pick(low, got_ref, send_ref, 3)
 
 
-def start_kernel(levels, position_ref, send_ref, got_ref, out_ref, carry_ref):
+def start_kernel(levels, position_ref, send_ref, got_ref, pq_ref, swk_ref, out_ref):
     position = position_ref[0]
     odd = (position & 1) == 1
-    high = ((position >> (levels - 2)) & 1) == 1
+    root = position == (1 << (levels - 1)) - 1
 
     @pl.when(odd)
     def _():
-        climb(False, 0, levels, send_ref, got_ref, out_ref)
-
-    @pl.when(position == (1 << (levels - 1)) - 1)
-    def _():
-        out_ref[2:4] = send_ref[7:9]
+        f = (send_ref[1].astype(F32) + got_ref[1].astype(F32)).astype(BF16)
+        out_ref[0] = f
+        out_ref[1] = lift(got_ref[2], f, got_ref[3]).astype(BF16)
+        out_ref[2] = jnp.where(root, swk_ref[3], pq_ref[0])
+        out_ref[3] = jnp.where(root, swk_ref[4], pq_ref[1])
 
     @pl.when(jnp.logical_not(odd))
     def _():
-        carry_ref[...] = got_ref[4:10]
-        out_ref[0] = jnp.where(high, got_ref[6], got_ref[7])
-        out_ref[1] = jnp.where(high, got_ref[9], got_ref[8])
+        out_ref[0:2] = got_ref[2:4]
 
 
 def sent(j, levels):
@@ -186,28 +198,35 @@
         o_ref[i] = dot(a_ref[i], b_ref[i])
 
 
-def first_node(odd, send_ref, got_ref, i):
-    left, right = ((4, 4), (5, 5), (6, 7), (9, 8))[i]
-    return jnp.where(odd, got_ref[right], send_ref[left])
+def first_node(odd, swk_ref, other_swk_ref, i):
+    left, right = ((0, 0), (1, 1), (2, 3), (5, 4))[i]
+    return jnp.where(odd, other_swk_ref[right], swk_ref[left])
 
 
 def prepare_kernel(
-    position_ref, send_ref, got_ref, leaf_ref, down_ref, block_ref, base_ref, left_ref, right_ref
+    position_ref, got_ref, swk_ref, other_swk_ref, leaf_ref, down_ref, block_ref, dense_ref,
+    outer_ref, out_ref, left_ref, right_ref,
 ):
     odd = (position_ref[0] & 1) == 1
     near = couple(
-        first_node(odd, send_ref, got_ref, 2), got_ref[0], first_node(odd, send_ref, got_ref, 3)
+        first_node(odd, swk_ref, other_swk_ref, 2),
+        got_ref[0],
+        first_node(odd, swk_ref, other_swk_ref, 3),
     ).astype(BF16)
     for i in range(2):
         s, w = down_ref[0, i, 0], down_ref[0, i, 1]
         leaf = couple(block_ref[0, 0, i], leaf_ref[1 - i], block_ref[0, 0, 3 - i])
-        base_ref[i] = leaf + lower(s, near, w)
-        left_ref[i] = dot(s, down_ref[0, 2, 0]).astype(BF16)
-        right_ref[i] = contract(down_ref[0, 2, 1], w, 0, 1).astype(BF16)
+        g = (leaf + lower(s, near, w)).astype(BF16)
+        e = dot(outer_ref[i, 0], g).astype(BF16)
+        out_ref[i] = dense_ref[i] + contract(e, outer_ref[i, 1], 1, 1)
+        left = dot(s, down_ref[0, 2, 0]).astype(BF16)
+        right = dot(w, down_ref[0, 2, 1]).astype(BF16)
+        left_ref[i] = dot(outer_ref[i, 0], left).astype(BF16)
+        right_ref[i] = dot(outer_ref[i, 1], right).astype(BF16)
 
 
 def upper_kernel(
-    levels, position_ref, send_ref, got_ref, mine_ref, other_ref, base_ref, left_ref, right_ref
+    levels, position_ref, swk_ref, other_swk_ref, mine_ref, other_ref, base_ref, left_ref, right_ref
 ):
     position = position_ref[0]
     odd = (position & 1) == 1
@@ -218,43 +237,62 @@
 
     def generator(height, i):
         if height == 1:
-            return first_node(odd, send_ref, got_ref, i)
+            return first_node(odd, swk_ref, other_swk_ref, i)
         slot = 4 * (height - 2) + i
         if height >= levels - 1:
             slot = 4 * (levels - 3) + 2 * (height - levels + 1) + i - 2
         return pick(odd, other_ref, mine_ref, slot)
 
-    base = None
-    left, right = generator(levels, 2), generator(levels, 3)
-    for height in range(levels - 1, 1, -1):
-        near = couple(generator(height, 2), inner(height - 1), generator(height, 3))
-        s, w = generator(height - 1, 0), generator(height - 1, 1)
-        if base is None:
-            left = jnp.where(in_left, dot(s, left), s.astype(F32)).astype(BF16)
-            right = jnp.where(in_left, contract(right, w, 1, 1), w.astype(F32).T).astype(BF16)
-        else:
-            left = dot(s, left).astype(BF16)
-            right = contract(right, w, 1, 1).astype(BF16)
-        base = near if base is None else near + lower(s, base.astype(BF16), w)
-    base_ref[0] = base
-    left_ref[0] = left
-    right_ref[0] = right
+    heights = range(2, levels)
+    nears = [dot(generator(h, 2), inner(h - 1)).astype(BF16) for h in heights]
+    sides = [(generator(1, 0), generator(1, 1))]
+    for n, h in enumerate(heights):
+        nears[n] = dot(nears[n], generator(h, 3))
+        if h < levels - 1:
+            s, w = (dot(x, generator(h, k)).astype(BF16) for k, x in enumerate(sides[-1]))
+            sides.append((s, w))
+    left, right = sides[-1]
+    left_ref[0] = jnp.where(in_left, dot(left, generator(levels, 2)).astype(BF16), left)
+    right_ref[0] = jnp.where(
+        in_left, contract(right, generator(levels, 3), 1, 1).astype(BF16), right
+    )
+    base = nears[0]
+    halves = [dot(s, near.astype(BF16)).astype(BF16) for (s, _), near in zip(sides, nears[1:])]
+    for half, (_, w) in zip(halves, sides):
+        base = base + contract(half, w, 1, 1)
+    base_ref[0] = base.astype(BF16)
+
+
+def merge_kernel(
+    base_ref, left_ref, right_ref, leaf_left_ref, leaf_right_ref, out_left_ref, both_left_ref,
+    both_right_ref,
+):
+    rank = base_ref.shape[-1]
+    for i in range(2):
+        both_left_ref[i] = dot(leaf_left_ref[i], base_ref[0]).astype(BF16)
+        out_left_ref[i] = dot(leaf_left_ref[i], left_ref[0]).astype(BF16)
+        both_right_ref[i, :, :rank] = dot(leaf_right_ref[i], right_ref[0]).astype(BF16)
+        both_right_ref[i, :, rank:] = leaf_right_ref[i]
 
 
 def final_kernel(
-    position_ref, last_ref, other_last_ref, base_ref, left_ref, right_ref, leaf_base_ref,
-    leaf_left_ref, leaf_right_ref, dense_ref, outer_ref, out_hbm, out, sems,
+    position_ref, last_ref, other_last_ref, part_ref, left_ref, base_ref, right_ref, out_hbm, out,
+    sems,
 ):
     odd = (position_ref[0] & 1) == 1
     f = pick(odd, last_ref, other_last_ref, 0)
-    g = (base_ref[0] + couple(left_ref[0], f, right_ref[0])).astype(BF16)
+    rows = part_ref.shape[1] // CHUNKS
     copies = []
+    lasts = [dot(left_ref[i], f).astype(BF16) for i in range(2)]
     for i in range(2):
-        gb = leaf_base_ref[i] + couple(leaf_left_ref[i], g, leaf_right_ref[i])
-        e = dot(outer_ref[i, 0], gb.astype(BF16)).astype(BF16)
-        out[i] = (dense_ref[i] + contract(e, outer_ref[i, 1], 1, 1)).astype(BF16)
-        copies.append(pltpu.make_async_copy(out.at[i], out_hbm.at[i], sems.at[i]))
-        copies[-1].start()
+        e = jnp.concatenate([lasts[i], base_ref[i]], 1)
+        for c in range(CHUNKS):
+            here = pl.ds(c * rows, rows)
+            full = part_ref[i, here] + contract(e[c * rows : (c + 1) * rows], right_ref[i], 1, 1)
+            out[i, here] = full.astype(BF16)
+            k = i * CHUNKS + c
+            copies.append(pltpu.make_async_copy(out.at[i, here], out_hbm.at[i, here], sems.at[k]))
+            copies[-1].start()
     for copy in copies:
         copy.wait()
 
@@ -279,31 +317,38 @@
     rank = ascent.shape[-1]
     place = lax.axis_index(AXES).reshape(1).astype(jnp.int32)
 
-    def mats(n, dtype=BF16):
-        return jax.ShapeDtypeStruct((n, rank, rank), dtype)
-
-    def call(kernel, outs, *refs, **extra):
+    def mats(n):
+        return jax.ShapeDtypeStruct((n, rank, rank), BF16)
+
+    tall = jax.ShapeDtypeStruct(outer_basis_stack.shape[:1] + outer_basis_stack.shape[2:], BF16)
+
+    wide = jax.ShapeDtypeStruct(tall.shape[:2] + (2 * rank,), BF16)
+    whole = jax.ShapeDtypeStruct(dense_a.shape, F32)
+
+    def call(kernel, outs, *refs, scalar=True, mib=2):
+        outs = tuple(mats(n) if isinstance(n, int) else n for n in outs)
         return pl.pallas_call(
             kernel,
-            out_shape=tuple(mats(n) if n > 0 else mats(-n, F32) for n in outs),
-            in_specs=in_vmem(len(refs)),
+            out_shape=outs,
+            in_specs=in_vmem(len(refs), scalar),
             out_specs=tuple(in_vmem(len(outs), False)),
-            compiler_params=small(),
-        )(place, *refs)
-
-    send, leaf_inner = pl.pallas_call(
-        head_kernel,
-        out_shape=(mats(10), mats(2)),
-        in_specs=[pl.BlockSpec(memory_space=pltpu.HBM)] * 4,
-        out_specs=tuple(in_vmem(2, False)),
+            compiler_params=small(mib),
+        )(*([place] if scalar else []), *refs)
+
+    send, pq, swk, leaf_inner = pl.pallas_call(
+        functools.partial(head_kernel, levels),
+        out_shape=(mats(4), mats(2), mats(6), mats(2)),
+        in_specs=[pl.BlockSpec(memory_space=pltpu.SMEM)]
+        + [pl.BlockSpec(memory_space=pltpu.HBM)] * 4,
+        out_specs=tuple(in_vmem(4, False)),
         scratch_shapes=[
             VMEM(inner_basis_stack.shape, BF16),
             VMEM((3, 2, rank, rank), BF16),
-            pltpu.SemaphoreType.DMA((5,)),
+            pltpu.SemaphoreType.DMA((6,)),
         ],
         compiler_params=small(4),
         name="head",
-    )(*[
+    )(place, *[
         pltpu.with_memory_space_constraint(x, pltpu.HBM)
         for x in (inner_basis_stack, ascent, descent, couplings)
     ])
@@ -321,8 +366,12 @@
         return climbing if r in (1, levels - 1) else max(climbing, sent(r - 1, levels))
 
     got = exchange(send, count, 0, 0)
-    block, carry = call(functools.partial(start_kernel, levels), (width(1), 6), send, got)
-    leaf_terms = call(prepare_kernel, (-2, 2, 2), send, got, leaf_inner, descent, couplings)
+    (block,) = call(functools.partial(start_kernel, levels), (width(1),), send, got, pq, swk)
+    carry = other_swk = exchange(swk, count, 0, 0)
+    part, *sides = call(
+        prepare_kernel, (whole, tall, tall), got, swk, other_swk, leaf_inner,
+        descent, couplings, dense, outer_basis_stack, mib=12,
+    )
     received, nodes = [], []
     for r in range(1, levels - 1):
         new = exchange(block, count, r, levels - 2 if r == 1 else r - 1)
@@ -338,18 +387,19 @@
     (mine,) = call(kernel, (size,), *received, *nodes, carry)
     other = exchange(mine, count, 0, 0)
     kernel = functools.partial(upper_kernel, levels)
-    upper_terms = call(kernel, (-1, 1, 1), send, got, mine, other)
+    upper_terms = call(kernel, (1, 1, 1), swk, other_swk, mine, other)
+    sides = call(merge_kernel, (tall, tall, wide), *upper_terms, *sides, scalar=False, mib=4)
     other_last = exchange(last, count, 0, 0)
 
     return pl.pallas_call(
         final_kernel,
         out_shape=jax.ShapeDtypeStruct(dense.shape, BF16),
-        in_specs=in_vmem(10),
+        in_specs=in_vmem(6),
         out_specs=pl.BlockSpec(memory_space=pltpu.HBM),
-        scratch_shapes=[VMEM(dense.shape, BF16), pltpu.SemaphoreType.DMA((2,))],
+        scratch_shapes=[VMEM(dense.shape, BF16), pltpu.SemaphoreType.DMA((2 * CHUNKS,))],
         compiler_params=small(12),
         name="final",
-    )(place, last, other_last, *upper_terms, *leaf_terms, dense, outer_basis_stack)
+    )(place, last, other_last, part, *sides)
 
 
 def solution(mesh):

time: 30.1 us -> 30.2 us (level)
  Pallas kernels: 6.71 us -> 7.16 us
  waiting for transfers between devices: 12.9 us -> 12.5 us
    pallas_call x8 -> x9, Pallas kernels: 3.73 us -> 5.11 us  [the longest x8 3.02 us: call(): pl.pallas_call(kernel, out_shape=outs, in_specs=in_vmem(len(refs), scalar...]
    pallas_call x1, Pallas kernels: 2.27 us -> 1.35 us  [stages(): pl.pallas_call(final_kernel, out_shape=jax.ShapeDtypeStruct(dense.shape,...]
    ppermute x7 -> x8, waiting for transfers between devices: 12.9 us -> 12.5 us  [exchange(): return lax.ppermute(block, AXES, route)]
    ppermute x7 -> x8, starting transfers between devices: 10.2 us -> 10.2 us  [exchange(): return lax.ppermute(block, AXES, route)]
  transfers between devices with their start and end apart: 7 -> 8, of which waited for: 5 -> 5; matrix products, arithmetic and copies ran while one was open for 0% -> 0% of each run, Pallas kernels for 7% -> 12%
where the time goes in v3:
time: 30.2 us; the launch traced here: 30.1 us
  waiting for transfers between devices  12.5 us (41%)
  starting transfers between devices  10.2 us (34%)
  Pallas kernels  7.16 us (24%)
    ppermute x8, waiting for transfers between devices, exchange(): return lax.ppermute(block, AXES, route)  12.5 us
    ppermute x8, starting transfers between devices, exchange(): return lax.ppermute(block, AXES, route)  10.2 us
    pallas_call x8, Pallas kernels, call(): pl.pallas_call(kernel, out_shape=outs, in_specs=in_vmem(len(refs), scalar...  3.02 us
    pallas_call x1, Pallas kernels, stages(): pl.pallas_call(functools.partial(head_kernel, levels), out_shape=(mats(4)...  2.08 us
    pallas_call x1, Pallas kernels, stages(): pl.pallas_call(final_kernel, out_shape=jax.ShapeDtypeStruct(dense.shape,...  1.35 us
    pallas_call x1, Pallas kernels, stages(): pl.pallas_call(dense_kernel, out_shape=jax.ShapeDtypeStruct(dense_a.shape...  0.71 us
  transfers between devices with their start and end apart: 8, of which 5 were waited for; matrix products, arithmetic and copies ran while one was open for 0% of the time, Pallas kernels for 12%

profile of v3, /device:TPU:0, one launch (start us, length us, event | category | flops | bytes accessed | tf_op | source)
XLA Modules:
  0.0 30.1 jit_solution(2674359773714317886)
XLA Ops:
  0.0 0.0 copy-start.2
  0.0 0.0 copy-start.3
  0.0 2.1 %head.1 = (bf16[4,128,128]{2,1,0:T(8,128)(2,1)S(1)}, bf16[2,128,128]{2,1,0:T(8,128)(2,1)S(1)}, bf16[6,128,128]{2,1,0:T(8,128)(2,1)S(1)}, bf16[2,128,128]{2,1,0:T(8,128)(2,1)S(1)}) custom-call(s32[1]{0:T(128)} %bitcast.position_ref, bf16[2,2,512,128]{3,2,1,0:T(8,128)(2,1)} %inner_hbm.1, bf16[1,4,2,128,128]{4,3,2,1,0:T(8,128)(2,1)} %up_hbm.1, ...), custom_call_target="tpu_custom_call" | custom-call | tf_op jit(solution)/shard_map/head/pallas_call | solution.py:338
  2.1 0.6 %collective-permute-start = (bf16[4,128,128]{2,1,0:T(8,128)(2,1)S(1)}, bf16[4,128,128]{2,1,0:T(8,128)(2,1)S(1)}, u32[]{:S(2)}, u32[]{:S(2)}) collective-permute-start(bf16[4,128,128]{2,1,0:T(8,128)(2,1)S(1)} %get-tuple-element.26.send_ref), channel_id=1, source_target_pairs={{0,1},{1,0},{2,3},{3,2},{4,5},{5,4},{6,7},{7,6},{8,9},{9,8},{10,11... | collective-permute-start | bytes 393224 | tf_op jit(solution)/shard_map/ppermute | solution.py:311
  2.7 0.1 collective-permute-start.2
  2.7 0.9 %collective-permute-done.got_ref = bf16[4,128,128]{2,1,0:T(8,128)(2,1)S(1)} collective-permute-done((bf16[4,128,128]{2,1,0:T(8,128)(2,1)S(1)}, bf16[4,128,128]{2,1,0:T(8,128)(2,1)S(1)}, u32[]{:S(2)}, u32[]{:S(2)}) %collective-permute-start) | collective-permute-done | bytes 131104 | tf_op jit(solution)/shard_map/ppermute | solution.py:311
  3.6 2.9 %collective-permute-start.1 = (bf16[4,128,128]{2,1,0:T(8,128)(2,1)S(1)}, bf16[4,128,128]{2,1,0:T(8,128)(2,1)S(1)}, u32[]{:S(2)}, u32[]{:S(2)}) collective-permute-start(bf16[4,128,128]{2,1,0:T(8,128)(2,1)S(1)} %shard_map.73.send_ref), channel_id=1, source_target_pairs={{0,8},{1,3},{2,10},{3,1},{4,12},{5,7},{6,14},{7,5},{8,0},{9,11},{1... | collective-permute-start | bytes 393224 | tf_op jit(solution)/shard_map/ppermute | solution.py:311
  6.6 0.0 collective-permute-done.2.carry_ref.other_swk_ref
  6.6 2.9 %collective-permute-done.1.got_ref.refs_0_ = bf16[4,128,128]{2,1,0:T(8,128)(2,1)S(1)} collective-permute-done((bf16[4,128,128]{2,1,0:T(8,128)(2,1)S(1)}, bf16[4,128,128]{2,1,0:T(8,128)(2,1)S(1)}, u32[]{:S(2)}, u32[]{:S(2)}) %collective-permute-start.1) | collective-permute-done | bytes 131104 | tf_op jit(solution)/shard_map/ppermute | solution.py:311
  9.5 2.0 %collective-permute-start.3 = (bf16[6,128,128]{2,1,0:T(8,128)(2,1)S(1)}, bf16[6,128,128]{2,1,0:T(8,128)(2,1)S(1)}, u32[]{:S(2)}, u32[]{:S(2)}) collective-permute-start(bf16[6,128,128]{2,1,0:T(8,128)(2,1)S(1)} %get-tuple-element.29.send_ref), channel_id=1, source_target_pairs={{0,2},{1,5},{2,0},{3,7},{4,6},{5,1},{6,4},{7,3},{8,10},{9,13},{10,... | collective-permute-start | bytes 589832 | tf_op jit(solution)/shard_map/ppermute | solution.py:311
  11.6 3.7 %collective-permute-done.3.got_ref.refs_1_ = bf16[6,128,128]{2,1,0:T(8,128)(2,1)S(1)} collective-permute-done((bf16[6,128,128]{2,1,0:T(8,128)(2,1)S(1)}, bf16[6,128,128]{2,1,0:T(8,128)(2,1)S(1)}, u32[]{:S(2)}, u32[]{:S(2)}) %collective-permute-start.3) | collective-permute-done | bytes 196640 | tf_op jit(solution)/shard_map/ppermute | solution.py:311
  15.3 2.0 %collective-permute-start.4 = (bf16[4,128,128]{2,1,0:T(8,128)(2,1)S(1)}, bf16[4,128,128]{2,1,0:T(8,128)(2,1)S(1)}, u32[]{:S(2)}, u32[]{:S(2)}) collective-permute-start(bf16[4,128,128]{2,1,0:T(8,128)(2,1)S(1)} %get-tuple-element.31.send_ref), channel_id=1, source_target_pairs={{0,4},{1,9},{2,6},{3,11},{4,0},{5,13},{6,2},{7,15},{8,12},{9,1},{1... | collective-permute-start | bytes 393224 | tf_op jit(solution)/shard_map/ppermute | solution.py:311
  17.3 3.0 %collective-permute-done.4.got_ref.refs_2_ = bf16[4,128,128]{2,1,0:T(8,128)(2,1)S(1)} collective-permute-done((bf16[4,128,128]{2,1,0:T(8,128)(2,1)S(1)}, bf16[4,128,128]{2,1,0:T(8,128)(2,1)S(1)}, u32[]{:S(2)}, u32[]{:S(2)}) %collective-permute-start.4) | collective-permute-done | bytes 131104 | tf_op jit(solution)/shard_map/ppermute | solution.py:311
  20.4 0.1 collective-permute-start.7
  20.5 0.0 copy-start
  20.5 0.0 copy-start.1
  20.5 0.0 copy-start.4
  20.5 2.0 %collective-permute-start.5 = (bf16[1,128,128]{2,1,0:T(8,128)(2,1)S(1)}, bf16[1,128,128]{2,1,0:T(8,128)(2,1)S(1)}, u32[]{:S(2)}, u32[]{:S(2)}) collective-permute-start(bf16[1,128,128]{2,1,0:T(8,128)(2,1)S(1)} %get-tuple-element.33), channel_id=1, source_target_pairs={{0,2},{1,17},{2,0},{3,19},{4,6},{5,21},{6,4},{7,23},{8,10},{9,25},... | collective-permute-start | bytes 98312 | tf_op jit(solution)/shard_map/ppermute | solution.py:311
  22.6 2.0 %collective-permute-done.5.last_ref = bf16[1,128,128]{2,1,0:T(8,128)(2,1)S(1)} collective-permute-done((bf16[1,128,128]{2,1,0:T(8,128)(2,1)S(1)}, bf16[1,128,128]{2,1,0:T(8,128)(2,1)S(1)}, u32[]{:S(2)}, u32[]{:S(2)}) %collective-permute-start.5) | collective-permute-done | bytes 32800 | tf_op jit(solution)/shard_map/ppermute | solution.py:311
  24.5 0.5 %collective-permute-start.6 = (bf16[1,128,128]{2,1,0:T(8,128)(2,1)S(1)}, bf16[1,128,128]{2,1,0:T(8,128)(2,1)S(1)}, u32[]{:S(2)}, u32[]{:S(2)}) collective-permute-start(bf16[1,128,128]{2,1,0:T(8,128)(2,1)S(1)} %collective-permute-done.5.last_ref), channel_id=1, source_target_pairs={{0,1},{1,0},{2,3},{3,2},{4,5},{5,4},{6,7},{7,6},{8,9},{9,8},{10,11... | collective-permute-start | bytes 98312 | tf_op jit(solution)/shard_map/ppermute | solution.py:311
  25.1 0.0 copy-done.2
  25.1 0.0 copy-done.3
  25.1 0.7 %dense.1.dense_ref = f32[2,512,512]{2,1,0:T(8,128)S(1)} custom-call(bf16[2,512,512]{2,1,0:T(8,128)(2,1)S(1)} %copy-done.2, bf16[2,512,512]{2,1,0:T(8,128)(2,1)S(1)} %copy-done.3), custom_call_target="tpu_custom_call" | custom-call | tf_op jit(solution)/shard_map/dense/pallas_call | solution.py:355
  25.8 0.0 copy-done
  25.8 0.0 copy-done.1
  25.8 0.0 copy-done.4
  25.8 1.9 %shard_map.77 = (f32[2,512,512]{2,1,0:T(8,128)S(1)}, bf16[2,512,128]{2,1,0:T(8,128)(2,1)S(1)}, bf16[2,512,128]{2,1,0:T(8,128)(2,1)S(1)}) custom-call(s32[1]{0:T(128)} %bitcast.position_ref, bf16[4,128,128]{2,1,0:T(8,128)(2,1)S(1)} %collective-permute-done.got_ref, bf16[6,128,128]{2,1,0:T(8,128)(2,1)S(1)} %get-tuple-element.28.swk_ref, ...), custom_call_target="tpu_custom_call" | custom-call | tf_op jit(solution)/shard_map/pallas_call | solution.py:330
  27.7 0.0 collective-permute-done.7.other_ref
  27.7 0.6 %shard_map.79 = (bf16[1,128,128]{2,1,0:T(8,128)(2,1)S(1)}, bf16[1,128,128]{2,1,0:T(8,128)(2,1)S(1)}, bf16[1,128,128]{2,1,0:T(8,128)(2,1)S(1)}) custom-call(s32[1]{0:T(128)} %bitcast.position_ref, bf16[6,128,128]{2,1,0:T(8,128)(2,1)S(1)} %get-tuple-element.28.swk_ref, bf16[6,128,128]{2,1,0:T(8,128)(2,1)S(1)} %collective-permute-done.2.carry_ref.other_swk_ref, ...), custom_call_target="tpu_custom_call" | custom-call | tf_op jit(solution)/shard_map/pallas_call | solution.py:330
  28.4 0.4 %shard_map.80 = (bf16[2,512,128]{2,1,0:T(8,128)(2,1)S(1)}, bf16[2,512,128]{2,1,0:T(8,128)(2,1)S(1)}, bf16[2,512,256]{2,1,0:T(8,128)(2,1)S(1)}) custom-call(bf16[1,128,128]{2,1,0:T(8,128)(2,1)S(1)} %get-tuple-element.39.base_ref, bf16[1,128,128]{2,1,0:T(8,128)(2,1)S(1)} %get-tuple-element.40.left_ref, bf16[1,128,128]{2,1,0:T(8,128)(2,1)S(1)} %get-tuple-element.41.right_ref, ...), custom_call_target="tpu_custom_call" | custom-call | tf_op jit(solution)/shard_map/pallas_call | solution.py:330
  28.7 0.0 collective-permute-done.6.other_last_ref
  28.8 1.3 %final.1 = bf16[2,512,512]{2,1,0:T(8,128)(2,1)} custom-call(s32[1]{0:T(128)} %bitcast.position_ref, bf16[1,128,128]{2,1,0:T(8,128)(2,1)S(1)} %collective-permute-done.5.last_ref, bf16[1,128,128]{2,1,0:T(8,128)(2,1)S(1)} %collective-permute-done.6.other_last_ref, f32[2,512,512]{2,1,0:T(8,128)S(1)} %get-tuple-element.35.part_ref, ...), custom_call_target="tpu_custom_call" | custom-call | tf_op jit(solution)/shard_map/final/pallas_call | solution.py:394
  (5 shorter events, 0.1 us)
Async XLA Ops:
  0.0 25.1 %copy-start.2 = (bf16[2,512,512]{2,1,0:T(8,128)(2,1)S(1)}, bf16[2,512,512]{2,1,0:T(8,128)(2,1)}, u32[]{:S(2)}) copy-start(bf16[2,512,512]{2,1,0:T(8,128)(2,1)} %a_ref.1) | copy-start | bytes 3145732
  0.0 25.1 %copy-start.3 = (bf16[2,512,512]{2,1,0:T(8,128)(2,1)S(1)}, bf16[2,512,512]{2,1,0:T(8,128)(2,1)}, u32[]{:S(2)}) copy-start(bf16[2,512,512]{2,1,0:T(8,128)(2,1)} %b_ref.1) | copy-start | bytes 3145732
  2.1 1.5 %collective-permute-start = (bf16[4,128,128]{2,1,0:T(8,128)(2,1)S(1)}, bf16[4,128,128]{2,1,0:T(8,128)(2,1)S(1)}, u32[]{:S(2)}, u32[]{:S(2)}) collective-permute-start(bf16[4,128,128]{2,1,0:T(8,128)(2,1)S(1)} %get-tuple-element.26.send_ref), channel_id=1, source_target_pairs={{0,1},{1,0},{2,3},{3,2},{4,5},{5,4},{6,7},{7,6},{8,9},{9,8},{10,11... | collective-permute-start | bytes 393224 | tf_op jit(solution)/shard_map/ppermute | solution.py:311
  2.7 3.9 %collective-permute-start.2 = (bf16[6,128,128]{2,1,0:T(8,128)(2,1)S(1)}, bf16[6,128,128]{2,1,0:T(8,128)(2,1)S(1)}, u32[]{:S(2)}, u32[]{:S(2)}) collective-permute-start(bf16[6,128,128]{2,1,0:T(8,128)(2,1)S(1)} %get-tuple-element.28.swk_ref), channel_id=1, source_target_pairs={{0,1},{1,0},{2,3},{3,2},{4,5},{5,4},{6,7},{7,6},{8,9},{9,8},{10,11... | collective-permute-start | bytes 589832 | tf_op jit(solution)/shard_map/ppermute | solution.py:311
  3.6 5.9 %collective-permute-start.1 = (bf16[4,128,128]{2,1,0:T(8,128)(2,1)S(1)}, bf16[4,128,128]{2,1,0:T(8,128)(2,1)S(1)}, u32[]{:S(2)}, u32[]{:S(2)}) collective-permute-start(bf16[4,128,128]{2,1,0:T(8,128)(2,1)S(1)} %shard_map.73.send_ref), channel_id=1, source_target_pairs={{0,8},{1,3},{2,10},{3,1},{4,12},{5,7},{6,14},{7,5},{8,0},{9,11},{1... | collective-permute-start | bytes 393224 | tf_op jit(solution)/shard_map/ppermute | solution.py:311
  9.5 5.7 %collective-permute-start.3 = (bf16[6,128,128]{2,1,0:T(8,128)(2,1)S(1)}, bf16[6,128,128]{2,1,0:T(8,128)(2,1)S(1)}, u32[]{:S(2)}, u32[]{:S(2)}) collective-permute-start(bf16[6,128,128]{2,1,0:T(8,128)(2,1)S(1)} %get-tuple-element.29.send_ref), channel_id=1, source_target_pairs={{0,2},{1,5},{2,0},{3,7},{4,6},{5,1},{6,4},{7,3},{8,10},{9,13},{10,... | collective-permute-start | bytes 589832 | tf_op jit(solution)/shard_map/ppermute | solution.py:311
  15.3 5.0 %collective-permute-start.4 = (bf16[4,128,128]{2,1,0:T(8,128)(2,1)S(1)}, bf16[4,128,128]{2,1,0:T(8,128)(2,1)S(1)}, u32[]{:S(2)}, u32[]{:S(2)}) collective-permute-start(bf16[4,128,128]{2,1,0:T(8,128)(2,1)S(1)} %get-tuple-element.31.send_ref), channel_id=1, source_target_pairs={{0,4},{1,9},{2,6},{3,11},{4,0},{5,13},{6,2},{7,15},{8,12},{9,1},{1... | collective-permute-start | bytes 393224 | tf_op jit(solution)/shard_map/ppermute | solution.py:311
  20.4 7.3 %collective-permute-start.7 = (bf16[12,128,128]{2,1,0:T(8,128)(2,1)S(1)}, bf16[12,128,128]{2,1,0:T(8,128)(2,1)S(1)}, u32[]{:S(2)}, u32[]{:S(2)}) collective-permute-start(bf16[12,128,128]{2,1,0:T(8,128)(2,1)S(1)} %shard_map.78.mine_ref), channel_id=1, source_target_pairs={{0,1},{1,0},{2,3},{3,2},{4,5},{5,4},{6,7},{7,6},{8,9},{9,8},{10,11... | collective-permute-start | bytes 1179656 | tf_op jit(solution)/shard_map/ppermute | solution.py:311
  20.5 5.3 %copy-start = (bf16[1,4,2,128,128]{4,3,2,1,0:T(8,128)(2,1)S(1)}, bf16[1,4,2,128,128]{4,3,2,1,0:T(8,128)(2,1)}, u32[]{:S(2)}) copy-start(bf16[1,4,2,128,128]{4,3,2,1,0:T(8,128)(2,1)} %down_ref.1) | copy-start | bytes 786436
  20.5 5.3 %copy-start.1 = (bf16[1,2,4,128,128]{4,3,2,1,0:T(8,128)(2,1)S(1)}, bf16[1,2,4,128,128]{4,3,2,1,0:T(8,128)(2,1)}, u32[]{:S(2)}) copy-start(bf16[1,2,4,128,128]{4,3,2,1,0:T(8,128)(2,1)} %block_ref.1) | copy-start | bytes 786436
  20.5 5.3 %copy-start.4 = (bf16[2,2,512,128]{3,2,1,0:T(8,128)(2,1)S(1)}, bf16[2,2,512,128]{3,2,1,0:T(8,128)(2,1)}, u32[]{:S(2)}) copy-start(bf16[2,2,512,128]{3,2,1,0:T(8,128)(2,1)} %outer_ref.1) | copy-start | bytes 1572868
  20.5 4.0 %collective-permute-start.5 = (bf16[1,128,128]{2,1,0:T(8,128)(2,1)S(1)}, bf16[1,128,128]{2,1,0:T(8,128)(2,1)S(1)}, u32[]{:S(2)}, u32[]{:S(2)}) collective-permute-start(bf16[1,128,128]{2,1,0:T(8,128)(2,1)S(1)} %get-tuple-element.33), channel_id=1, source_target_pairs={{0,2},{1,17},{2,0},{3,19},{4,6},{5,21},{6,4},{7,23},{8,10},{9,25},... | collective-permute-start | bytes 98312 | tf_op jit(solution)/shard_map/ppermute | solution.py:311
  24.5 4.2 %collective-permute-start.6 = (bf16[1,128,128]{2,1,0:T(8,128)(2,1)S(1)}, bf16[1,128,128]{2,1,0:T(8,128)(2,1)S(1)}, u32[]{:S(2)}, u32[]{:S(2)}) collective-permute-start(bf16[1,128,128]{2,1,0:T(8,128)(2,1)S(1)} %collective-permute-done.5.last_ref), channel_id=1, source_target_pairs={{0,1},{1,0},{2,3},{3,2},{4,5},{5,4},{6,7},{7,6},{8,9},{9,8},{10,11... | collective-permute-start | bytes 98312 | tf_op jit(solution)/shard_map/ppermute | solution.py:311

commit v4 on v3

--- a/solution.py
+++ b/solution.py
@@ -77,28 +77,29 @@
 
 
 def climb(low, r, levels, send_ref, got_ref, out_ref):
-    f = (send_ref[1].astype(F32) + got_ref[1].astype(F32)).astype(BF16)
+    t = 0 if r == 1 else 1
+    f = (send_ref[t].astype(F32) + got_ref[t].astype(F32)).astype(BF16)
     out_ref[0] = f
     if r + 1 < levels - 1:
-        p = pick(low, send_ref, got_ref, 2)
-        q = pick(low, send_ref, got_ref, 3)
+        p = pick(low, send_ref, got_ref, t + 1)
+        q = pick(low, send_ref, got_ref, t + 2)
         out_ref[1] = lift(p, f, q).astype(BF16)
-        out_ref[2] = pick(low, got_ref, send_ref, 2)
-        out_ref[3] = pick(low, got_ref, send_ref, 3)
-
-
-def start_kernel(levels, position_ref, send_ref, got_ref, pq_ref, swk_ref, out_ref):
+        out_ref[2] = pick(low, got_ref, send_ref, t + 1)
+        out_ref[3] = pick(low, got_ref, send_ref, t + 2)
+
+
+def start_kernel(levels, position_ref, send_ref, got_ref, pq_ref, swk_ref, out_ref, f_ref):
     position = position_ref[0]
     odd = (position & 1) == 1
     root = position == (1 << (levels - 1)) - 1
+    f = (send_ref[1].astype(F32) + got_ref[1].astype(F32)).astype(BF16)
+    f_ref[0] = f
 
     @pl.when(odd)
     def _():
-        f = (send_ref[1].astype(F32) + got_ref[1].astype(F32)).astype(BF16)
-        out_ref[0] = f
-        out_ref[1] = lift(got_ref[2], f, got_ref[3]).astype(BF16)
-        out_ref[2] = jnp.where(root, swk_ref[3], pq_ref[0])
-        out_ref[3] = jnp.where(root, swk_ref[4], pq_ref[1])
+        out_ref[0] = lift(got_ref[2], f, got_ref[3]).astype(BF16)
+        out_ref[1] = jnp.where(root, swk_ref[3], pq_ref[0])
+        out_ref[2] = jnp.where(root, swk_ref[4], pq_ref[1])
 
     @pl.when(jnp.logical_not(odd))
     def _():
@@ -125,7 +126,11 @@
         out_ref[0:4] = carry_ref[2:6]
 
 
-def round_kernel(r, levels, position_ref, send_ref, got_ref, carry_ref, out_ref, new_ref, *node_refs):
+def round_kernel(r, levels, position_ref, send_ref, got_ref, carry_ref, *refs):
+    if r == levels - 2:
+        first_ref, out_ref, new_ref, *node_refs = refs
+    else:
+        out_ref, new_ref, *node_refs = refs
     position = position_ref[0]
     odd = (position & 1) == 1
 
@@ -175,6 +180,8 @@
 
         if full:
             fill(j + 1, levels, position, new_ref, out_ref)
+        if r == levels - 2:
+            out_ref[0] = first_ref[0]
 
 
 def pack_kernel(count, position_ref, *refs):
@@ -204,10 +211,13 @@
 
 
 def prepare_kernel(
-    position_ref, got_ref, swk_ref, other_swk_ref, leaf_ref, down_ref, block_ref, dense_ref,
-    outer_ref, out_ref, left_ref, right_ref,
+    position_ref, got_ref, swk_ref, other_swk_ref, f_ref, leaf_ref, down_ref, block_ref, dense_ref,
+    outer_ref, out_ref, left_ref, right_ref, first_ref, first_left_ref, first_right_ref,
 ):
     odd = (position_ref[0] & 1) == 1
+    low = ((position_ref[0] >> 1) & 1) == 0
+    node = [pick(odd, swk_ref, other_swk_ref, k) for k in range(2, 6)]
+    first_ref[0] = jnp.where(low, couple(node[1], f_ref[0], node[2]).astype(BF16), f_ref[0])
     near = couple(
         first_node(odd, swk_ref, other_swk_ref, 2),
         got_ref[0],
@@ -221,8 +231,12 @@
         out_ref[i] = dense_ref[i] + contract(e, outer_ref[i, 1], 1, 1)
         left = dot(s, down_ref[0, 2, 0]).astype(BF16)
         right = dot(w, down_ref[0, 2, 1]).astype(BF16)
-        left_ref[i] = dot(outer_ref[i, 0], left).astype(BF16)
-        right_ref[i] = dot(outer_ref[i, 1], right).astype(BF16)
+        left = dot(outer_ref[i, 0], left).astype(BF16)
+        right = dot(outer_ref[i, 1], right).astype(BF16)
+        left_ref[i] = left
+        right_ref[i] = right
+        first_left_ref[i] = jnp.where(low, dot(left, node[0]).astype(BF16), left)
+        first_right_ref[i] = jnp.where(low, contract(right, node[3], 1, 1).astype(BF16), right)
 
 
 def upper_kernel(
@@ -233,7 +247,7 @@
     in_left = ((position >> (levels - 1)) & 1) == 0
 
     def inner(height):
-        return pick(odd, mine_ref, other_ref, height - 1)
+        return pick(odd, mine_ref, other_ref, height - 2)
 
     def generator(height, i):
         if height == 1:
@@ -243,49 +257,52 @@
             slot = 4 * (levels - 3) + 2 * (height - levels + 1) + i - 2
         return pick(odd, other_ref, mine_ref, slot)
 
-    heights = range(2, levels)
+    heights = range(3, levels)
     nears = [dot(generator(h, 2), inner(h - 1)).astype(BF16) for h in heights]
     sides = [(generator(1, 0), generator(1, 1))]
     for n, h in enumerate(heights):
-        nears[n] = dot(nears[n], generator(h, 3))
-        if h < levels - 1:
-            s, w = (dot(x, generator(h, k)).astype(BF16) for k, x in enumerate(sides[-1]))
-            sides.append((s, w))
+        nears[n] = dot(nears[n], generator(h, 3)).astype(BF16)
+        s, w = (dot(x, generator(h - 1, k)).astype(BF16) for k, x in enumerate(sides[-1]))
+        sides.append((s, w))
     left, right = sides[-1]
     left_ref[0] = jnp.where(in_left, dot(left, generator(levels, 2)).astype(BF16), left)
     right_ref[0] = jnp.where(
         in_left, contract(right, generator(levels, 3), 1, 1).astype(BF16), right
     )
-    base = nears[0]
-    halves = [dot(s, near.astype(BF16)).astype(BF16) for (s, _), near in zip(sides, nears[1:])]
+    halves = [dot(s, near).astype(BF16) for (s, _), near in zip(sides, nears)]
+    base = None
     for half, (_, w) in zip(halves, sides):
-        base = base + contract(half, w, 1, 1)
+        term = contract(half, w, 1, 1)
+        base = term if base is None else base + term
     base_ref[0] = base.astype(BF16)
 
 
 def merge_kernel(
-    base_ref, left_ref, right_ref, leaf_left_ref, leaf_right_ref, out_left_ref, both_left_ref,
-    both_right_ref,
+    base_ref, left_ref, right_ref, leaf_left_ref, leaf_right_ref, first_right_ref, out_left_ref,
+    both_left_ref, both_right_ref,
 ):
     rank = base_ref.shape[-1]
     for i in range(2):
         both_left_ref[i] = dot(leaf_left_ref[i], base_ref[0]).astype(BF16)
         out_left_ref[i] = dot(leaf_left_ref[i], left_ref[0]).astype(BF16)
         both_right_ref[i, :, :rank] = dot(leaf_right_ref[i], right_ref[0]).astype(BF16)
-        both_right_ref[i, :, rank:] = leaf_right_ref[i]
+        both_right_ref[i, :, rank : 2 * rank] = leaf_right_ref[i]
+        both_right_ref[i, :, 2 * rank :] = first_right_ref[i]
 
 
 def final_kernel(
-    position_ref, last_ref, other_last_ref, part_ref, left_ref, base_ref, right_ref, out_hbm, out,
-    sems,
+    position_ref, last_ref, other_last_ref, part_ref, first_left_ref, left_ref, base_ref, right_ref,
+    out_hbm, out, sems,
 ):
     odd = (position_ref[0] & 1) == 1
     f = pick(odd, last_ref, other_last_ref, 0)
+    first = pick(odd, other_last_ref, last_ref, 0)
     rows = part_ref.shape[1] // CHUNKS
     copies = []
     lasts = [dot(left_ref[i], f).astype(BF16) for i in range(2)]
+    firsts = [dot(first_left_ref[i], first).astype(BF16) for i in range(2)]
     for i in range(2):
-        e = jnp.concatenate([lasts[i], base_ref[i]], 1)
+        e = jnp.concatenate([lasts[i], base_ref[i], firsts[i]], 1)
         for c in range(CHUNKS):
             here = pl.ds(c * rows, rows)
             full = part_ref[i, here] + contract(e[c * rows : (c + 1) * rows], right_ref[i], 1, 1)
@@ -322,7 +339,7 @@
 
     tall = jax.ShapeDtypeStruct(outer_basis_stack.shape[:1] + outer_basis_stack.shape[2:], BF16)
 
-    wide = jax.ShapeDtypeStruct(tall.shape[:2] + (2 * rank,), BF16)
+    wide = jax.ShapeDtypeStruct(tall.shape[:2] + (3 * rank,), BF16)
     whole = jax.ShapeDtypeStruct(dense_a.shape, F32)
 
     def call(kernel, outs, *refs, scalar=True, mib=2):
@@ -362,23 +379,25 @@
     )(dense_a, dense_b)
 
     def width(r):
-        climbing = 4 if r <= levels - 2 else 1
+        climbing = 3 if r == 1 else 4 if r <= levels - 2 else 1
         return climbing if r in (1, levels - 1) else max(climbing, sent(r - 1, levels))
 
     got = exchange(send, count, 0, 0)
-    (block,) = call(functools.partial(start_kernel, levels), (width(1),), send, got, pq, swk)
+    block, first = call(functools.partial(start_kernel, levels), (width(1), 1), send, got, pq, swk)
     carry = other_swk = exchange(swk, count, 0, 0)
-    part, *sides = call(
-        prepare_kernel, (whole, tall, tall), got, swk, other_swk, leaf_inner,
-        descent, couplings, dense, outer_basis_stack, mib=12,
+    part, left, right, first, first_left, first_right = call(
+        prepare_kernel, (whole, tall, tall, 1, tall, tall), got, swk, other_swk, first,
+        leaf_inner, descent, couplings, dense, outer_basis_stack, mib=12,
     )
     received, nodes = [], []
     for r in range(1, levels - 1):
         new = exchange(block, count, r, levels - 2 if r == 1 else r - 1)
-        received.append(new)
+        if r > 1:
+            received.append(new)
         outs = (width(r + 1), 4 if r == levels - 2 else 6) + ((4,) if r > 1 else ())
         kernel = functools.partial(round_kernel, r, levels)
-        block, carry, *node = call(kernel, outs, block, new, carry)
+        more = (first,) if r == levels - 2 else ()
+        block, carry, *node = call(kernel, outs, block, new, carry, *more)
         nodes += node
     last = exchange(block, count, levels - 1, 1)
 
@@ -388,18 +407,21 @@
     other = exchange(mine, count, 0, 0)
     kernel = functools.partial(upper_kernel, levels)
     upper_terms = call(kernel, (1, 1, 1), swk, other_swk, mine, other)
-    sides = call(merge_kernel, (tall, tall, wide), *upper_terms, *sides, scalar=False, mib=4)
+    sides = call(
+        merge_kernel, (tall, tall, wide), *upper_terms, left, right, first_right,
+        scalar=False, mib=4,
+    )
     other_last = exchange(last, count, 0, 0)
 
     return pl.pallas_call(
         final_kernel,
         out_shape=jax.ShapeDtypeStruct(dense.shape, BF16),
-        in_specs=in_vmem(6),
+        in_specs=in_vmem(7),
         out_specs=pl.BlockSpec(memory_space=pltpu.HBM),
         scratch_shapes=[VMEM(dense.shape, BF16), pltpu.SemaphoreType.DMA((2 * CHUNKS,))],
         compiler_params=small(12),
         name="final",
-    )(place, last, other_last, part, *sides)
+    )(place, last, other_last, part, first_left, *sides)
 
 
 def solution(mesh):

time: 30.2 us -> 27.6 us (0.914)
  waiting for transfers between devices: 12.5 us -> 9.25 us
  Pallas kernels: 7.16 us -> 7.72 us
    ppermute x8, waiting for transfers between devices: 12.5 us -> 9.25 us  [exchange(): return lax.ppermute(block, AXES, route)]
    pallas_call x8, Pallas kernels: 3.02 us -> 3.35 us  [call(): pl.pallas_call(kernel, out_shape=outs, in_specs=in_vmem(len(refs), scalar...]
  transfers between devices with their start and end apart: 8 -> 8, of which waited for: 5 -> 5; matrix products, arithmetic and copies ran while one was open for 0% -> 0% of each run, Pallas kernels for 12% -> 14%
where the time goes in v4:
time: 27.6 us; the launch traced here: 27.5 us
  starting transfers between devices  10.3 us (37%)
  waiting for transfers between devices  9.25 us (34%)
  Pallas kernels  7.72 us (28%)
    ppermute x8, starting transfers between devices, exchange(): return lax.ppermute(block, AXES, route)  10.3 us
    ppermute x8, waiting for transfers between devices, exchange(): return lax.ppermute(block, AXES, route)  9.25 us
    pallas_call x8, Pallas kernels, call(): pl.pallas_call(kernel, out_shape=outs, in_specs=in_vmem(len(refs), scalar...  3.35 us
    pallas_call x1, Pallas kernels, stages(): pl.pallas_call(functools.partial(head_kernel, levels), out_shape=(mats(4)...  2.08 us
    pallas_call x1, Pallas kernels, stages(): pl.pallas_call(final_kernel, out_shape=jax.ShapeDtypeStruct(dense.shape,...  1.58 us
    pallas_call x1, Pallas kernels, stages(): pl.pallas_call(dense_kernel, out_shape=jax.ShapeDtypeStruct(dense_a.shape...  0.71 us
  transfers between devices with their start and end apart: 8, of which 5 were waited for; matrix products, arithmetic and copies ran while one was open for 0% of the time, Pallas kernels for 14%

profile of v4, /device:TPU:0, one launch (start us, length us, event | category | flops | bytes accessed | tf_op | source)
XLA Modules:
  0.0 27.5 jit_solution(9266568091804966719)
XLA Ops:
  0.0 0.0 copy-start.2
  0.0 0.0 copy-start.3
  0.0 2.1 %head.1 = (bf16[4,128,128]{2,1,0:T(8,128)(2,1)S(1)}, bf16[2,128,128]{2,1,0:T(8,128)(2,1)S(1)}, bf16[6,128,128]{2,1,0:T(8,128)(2,1)S(1)}, bf16[2,128,128]{2,1,0:T(8,128)(2,1)S(1)}) custom-call(s32[1]{0:T(128)} %bitcast.position_ref, bf16[2,2,512,128]{3,2,1,0:T(8,128)(2,1)} %inner_hbm.1, bf16[1,4,2,128,128]{4,3,2,1,0:T(8,128)(2,1)} %up_hbm.1, ...), custom_call_target="tpu_custom_call" | custom-call | tf_op jit(solution)/shard_map/head/pallas_call | solution.py:355
  2.1 0.6 %collective-permute-start = (bf16[4,128,128]{2,1,0:T(8,128)(2,1)S(1)}, bf16[4,128,128]{2,1,0:T(8,128)(2,1)S(1)}, u32[]{:S(2)}, u32[]{:S(2)}) collective-permute-start(bf16[4,128,128]{2,1,0:T(8,128)(2,1)S(1)} %get-tuple-element.31.send_ref), channel_id=1, source_target_pairs={{0,1},{1,0},{2,3},{3,2},{4,5},{5,4},{6,7},{7,6},{8,9},{9,8},{10,11... | collective-permute-start | bytes 393224 | tf_op jit(solution)/shard_map/ppermute | solution.py:328
  2.7 0.1 collective-permute-start.2
  2.7 0.9 %collective-permute-done.got_ref = bf16[4,128,128]{2,1,0:T(8,128)(2,1)S(1)} collective-permute-done((bf16[4,128,128]{2,1,0:T(8,128)(2,1)S(1)}, bf16[4,128,128]{2,1,0:T(8,128)(2,1)S(1)}, u32[]{:S(2)}, u32[]{:S(2)}) %collective-permute-start) | collective-permute-done | bytes 131104 | tf_op jit(solution)/shard_map/ppermute | solution.py:328
  3.7 3.0 %collective-permute-start.1 = (bf16[3,128,128]{2,1,0:T(8,128)(2,1)S(1)}, bf16[3,128,128]{2,1,0:T(8,128)(2,1)S(1)}, u32[]{:S(2)}, u32[]{:S(2)}) collective-permute-start(bf16[3,128,128]{2,1,0:T(8,128)(2,1)S(1)} %get-tuple-element.34.send_ref), channel_id=1, source_target_pairs={{0,8},{1,3},{2,10},{3,1},{4,12},{5,7},{6,14},{7,5},{8,0},{9,11},{1... | collective-permute-start | bytes 294920 | tf_op jit(solution)/shard_map/ppermute | solution.py:328
  6.6 0.0 collective-permute-done.2.carry_ref.other_swk_ref
  6.6 2.6 %collective-permute-done.1.got_ref = bf16[3,128,128]{2,1,0:T(8,128)(2,1)S(1)} collective-permute-done((bf16[3,128,128]{2,1,0:T(8,128)(2,1)S(1)}, bf16[3,128,128]{2,1,0:T(8,128)(2,1)S(1)}, u32[]{:S(2)}, u32[]{:S(2)}) %collective-permute-start.1) | collective-permute-done | bytes 98336 | tf_op jit(solution)/shard_map/ppermute | solution.py:328
  9.3 2.0 %collective-permute-start.3 = (bf16[6,128,128]{2,1,0:T(8,128)(2,1)S(1)}, bf16[6,128,128]{2,1,0:T(8,128)(2,1)S(1)}, u32[]{:S(2)}, u32[]{:S(2)}) collective-permute-start(bf16[6,128,128]{2,1,0:T(8,128)(2,1)S(1)} %get-tuple-element.35.send_ref), channel_id=1, source_target_pairs={{0,2},{1,5},{2,0},{3,7},{4,6},{5,1},{6,4},{7,3},{8,10},{9,13},{10,... | collective-permute-start | bytes 589832 | tf_op jit(solution)/shard_map/ppermute | solution.py:328
  11.3 3.7 %collective-permute-done.3.got_ref.refs_0_ = bf16[6,128,128]{2,1,0:T(8,128)(2,1)S(1)} collective-permute-done((bf16[6,128,128]{2,1,0:T(8,128)(2,1)S(1)}, bf16[6,128,128]{2,1,0:T(8,128)(2,1)S(1)}, u32[]{:S(2)}, u32[]{:S(2)}) %collective-permute-start.3) | collective-permute-done | bytes 196640 | tf_op jit(solution)/shard_map/ppermute | solution.py:328
  15.1 0.0 copy-start
  15.1 0.0 copy-start.1
  15.1 0.0 copy-start.4
  15.1 2.0 %collective-permute-start.4 = (bf16[4,128,128]{2,1,0:T(8,128)(2,1)S(1)}, bf16[4,128,128]{2,1,0:T(8,128)(2,1)S(1)}, u32[]{:S(2)}, u32[]{:S(2)}) collective-permute-start(bf16[4,128,128]{2,1,0:T(8,128)(2,1)S(1)} %get-tuple-element.37.send_ref), channel_id=1, source_target_pairs={{0,4},{1,9},{2,6},{3,11},{4,0},{5,13},{6,2},{7,15},{8,12},{9,1},{1... | collective-permute-start | bytes 393224 | tf_op jit(solution)/shard_map/ppermute | solution.py:328
  17.1 0.0 copy-done.2
  17.1 0.0 copy-done.3
  17.1 0.7 %dense.1.dense_ref = f32[2,512,512]{2,1,0:T(8,128)S(1)} custom-call(bf16[2,512,512]{2,1,0:T(8,128)(2,1)S(1)} %copy-done.2, bf16[2,512,512]{2,1,0:T(8,128)(2,1)S(1)} %copy-done.3), custom_call_target="tpu_custom_call" | custom-call | tf_op jit(solution)/shard_map/dense/pallas_call | solution.py:372
  17.8 0.0 copy-done
  17.8 0.0 copy-done.1
  17.8 0.0 copy-done.4
  17.8 2.2 %shard_map.76 = (f32[2,512,512]{2,1,0:T(8,128)S(1)}, bf16[2,512,128]{2,1,0:T(8,128)(2,1)S(1)}, bf16[2,512,128]{2,1,0:T(8,128)(2,1)S(1)}, bf16[1,128,128]{2,1,0:T...) custom-call(s32[1]{0:T(128)} %bitcast.position_ref, ...), custom_call_target="tpu_custom_call" | custom-call | tf_op jit(solution)/shard_map/pallas_call | solution.py:347
  20.0 0.1 collective-permute-done.4.got_ref.refs_1_
  20.2 0.1 collective-permute-start.7
  20.3 2.0 %collective-permute-start.5 = (bf16[1,128,128]{2,1,0:T(8,128)(2,1)S(1)}, bf16[1,128,128]{2,1,0:T(8,128)(2,1)S(1)}, u32[]{:S(2)}, u32[]{:S(2)}) collective-permute-start(bf16[1,128,128]{2,1,0:T(8,128)(2,1)S(1)} %get-tuple-element.42), channel_id=1, source_target_pairs={{0,2},{1,17},{2,0},{3,19},{4,6},{5,21},{6,4},{7,23},{8,10},{9,25},... | collective-permute-start | bytes 98312 | tf_op jit(solution)/shard_map/ppermute | solution.py:328
  22.3 2.0 %collective-permute-done.5.last_ref = bf16[1,128,128]{2,1,0:T(8,128)(2,1)S(1)} collective-permute-done((bf16[1,128,128]{2,1,0:T(8,128)(2,1)S(1)}, bf16[1,128,128]{2,1,0:T(8,128)(2,1)S(1)}, u32[]{:S(2)}, u32[]{:S(2)}) %collective-permute-start.5) | collective-permute-done | bytes 32800 | tf_op jit(solution)/shard_map/ppermute | solution.py:328
  24.3 0.6 %collective-permute-start.6 = (bf16[1,128,128]{2,1,0:T(8,128)(2,1)S(1)}, bf16[1,128,128]{2,1,0:T(8,128)(2,1)S(1)}, u32[]{:S(2)}, u32[]{:S(2)}) collective-permute-start(bf16[1,128,128]{2,1,0:T(8,128)(2,1)S(1)} %collective-permute-done.5.last_ref), channel_id=1, source_target_pairs={{0,1},{1,0},{2,3},{3,2},{4,5},{5,4},{6,7},{7,6},{8,9},{9,8},{10,11... | collective-permute-start | bytes 98312 | tf_op jit(solution)/shard_map/ppermute | solution.py:328
  24.8 0.0 collective-permute-done.7.other_ref
  24.8 0.6 %shard_map.79 = (bf16[1,128,128]{2,1,0:T(8,128)(2,1)S(1)}, bf16[1,128,128]{2,1,0:T(8,128)(2,1)S(1)}, bf16[1,128,128]{2,1,0:T(8,128)(2,1)S(1)}) custom-call(s32[1]{0:T(128)} %bitcast.position_ref, bf16[6,128,128]{2,1,0:T(8,128)(2,1)S(1)} %get-tuple-element.33.swk_ref, bf16[6,128,128]{2,1,0:T(8,128)(2,1)S(1)} %collective-permute-done.2.carry_ref.other_swk_ref, ...), custom_call_target="tpu_custom_call" | custom-call | tf_op jit(solution)/shard_map/pallas_call | solution.py:347
  25.5 0.4 %shard_map.80 = (bf16[2,512,128]{2,1,0:T(8,128)(2,1)S(1)}, bf16[2,512,128]{2,1,0:T(8,128)(2,1)S(1)}, bf16[2,512,384]{2,1,0:T(8,128)(2,1)S(1)}) custom-call(bf16[1,128,128]{2,1,0:T(8,128)(2,1)S(1)} %get-tuple-element.48.base_ref, bf16[1,128,128]{2,1,0:T(8,128)(2,1)S(1)} %get-tuple-element.49.left_ref, bf16[1,128,128]{2,1,0:T(8,128)(2,1)S(1)} %get-tuple-element.50.right_ref, ...), custom_call_target="tpu_custom_call" | custom-call | tf_op jit(solution)/shard_map/pallas_call | solution.py:347
  25.9 0.0 collective-permute-done.6.other_last_ref
  25.9 1.6 %final.1 = bf16[2,512,512]{2,1,0:T(8,128)(2,1)} custom-call(s32[1]{0:T(128)} %bitcast.position_ref, bf16[1,128,128]{2,1,0:T(8,128)(2,1)S(1)} %collective-permute-done.5.last_ref, bf16[1,128,128]{2,1,0:T(8,128)(2,1)S(1)} %collective-permute-done.6.other_last_ref, f32[2,512,512]{2,1,0:T(8,128)S(1)} %get-tuple-element.43.part_ref, ...), custom_call_target="tpu_custom_call" | custom-call | tf_op jit(solution)/shard_map/final/pallas_call | solution.py:416
  (5 shorter events, 0.1 us)
Async XLA Ops:
  0.0 17.1 %copy-start.2 = (bf16[2,512,512]{2,1,0:T(8,128)(2,1)S(1)}, bf16[2,512,512]{2,1,0:T(8,128)(2,1)}, u32[]{:S(2)}) copy-start(bf16[2,512,512]{2,1,0:T(8,128)(2,1)} %a_ref.1) | copy-start | bytes 3145732
  0.0 17.1 %copy-start.3 = (bf16[2,512,512]{2,1,0:T(8,128)(2,1)S(1)}, bf16[2,512,512]{2,1,0:T(8,128)(2,1)}, u32[]{:S(2)}) copy-start(bf16[2,512,512]{2,1,0:T(8,128)(2,1)} %b_ref.1) | copy-start | bytes 3145732
  2.1 1.5 %collective-permute-start = (bf16[4,128,128]{2,1,0:T(8,128)(2,1)S(1)}, bf16[4,128,128]{2,1,0:T(8,128)(2,1)S(1)}, u32[]{:S(2)}, u32[]{:S(2)}) collective-permute-start(bf16[4,128,128]{2,1,0:T(8,128)(2,1)S(1)} %get-tuple-element.31.send_ref), channel_id=1, source_target_pairs={{0,1},{1,0},{2,3},{3,2},{4,5},{5,4},{6,7},{7,6},{8,9},{9,8},{10,11... | collective-permute-start | bytes 393224 | tf_op jit(solution)/shard_map/ppermute | solution.py:328
  2.7 4.0 %collective-permute-start.2 = (bf16[6,128,128]{2,1,0:T(8,128)(2,1)S(1)}, bf16[6,128,128]{2,1,0:T(8,128)(2,1)S(1)}, u32[]{:S(2)}, u32[]{:S(2)}) collective-permute-start(bf16[6,128,128]{2,1,0:T(8,128)(2,1)S(1)} %get-tuple-element.33.swk_ref), channel_id=1, source_target_pairs={{0,1},{1,0},{2,3},{3,2},{4,5},{5,4},{6,7},{7,6},{8,9},{9,8},{10,11... | collective-permute-start | bytes 589832 | tf_op jit(solution)/shard_map/ppermute | solution.py:328
  3.7 5.6 %collective-permute-start.1 = (bf16[3,128,128]{2,1,0:T(8,128)(2,1)S(1)}, bf16[3,128,128]{2,1,0:T(8,128)(2,1)S(1)}, u32[]{:S(2)}, u32[]{:S(2)}) collective-permute-start(bf16[3,128,128]{2,1,0:T(8,128)(2,1)S(1)} %get-tuple-element.34.send_ref), channel_id=1, source_target_pairs={{0,8},{1,3},{2,10},{3,1},{4,12},{5,7},{6,14},{7,5},{8,0},{9,11},{1... | collective-permute-start | bytes 294920 | tf_op jit(solution)/shard_map/ppermute | solution.py:328
  9.3 5.7 %collective-permute-start.3 = (bf16[6,128,128]{2,1,0:T(8,128)(2,1)S(1)}, bf16[6,128,128]{2,1,0:T(8,128)(2,1)S(1)}, u32[]{:S(2)}, u32[]{:S(2)}) collective-permute-start(bf16[6,128,128]{2,1,0:T(8,128)(2,1)S(1)} %get-tuple-element.35.send_ref), channel_id=1, source_target_pairs={{0,2},{1,5},{2,0},{3,7},{4,6},{5,1},{6,4},{7,3},{8,10},{9,13},{10,... | collective-permute-start | bytes 589832 | tf_op jit(solution)/shard_map/ppermute | solution.py:328
  15.1 2.8 %copy-start = (bf16[1,4,2,128,128]{4,3,2,1,0:T(8,128)(2,1)S(1)}, bf16[1,4,2,128,128]{4,3,2,1,0:T(8,128)(2,1)}, u32[]{:S(2)}) copy-start(bf16[1,4,2,128,128]{4,3,2,1,0:T(8,128)(2,1)} %down_ref.1) | copy-start | bytes 786436
  15.1 2.8 %copy-start.1 = (bf16[1,2,4,128,128]{4,3,2,1,0:T(8,128)(2,1)S(1)}, bf16[1,2,4,128,128]{4,3,2,1,0:T(8,128)(2,1)}, u32[]{:S(2)}) copy-start(bf16[1,2,4,128,128]{4,3,2,1,0:T(8,128)(2,1)} %block_ref.1) | copy-start | bytes 786436
  15.1 2.7 %copy-start.4 = (bf16[2,2,512,128]{3,2,1,0:T(8,128)(2,1)S(1)}, bf16[2,2,512,128]{3,2,1,0:T(8,128)(2,1)}, u32[]{:S(2)}) copy-start(bf16[2,2,512,128]{3,2,1,0:T(8,128)(2,1)} %outer_ref.1) | copy-start | bytes 1572868
  15.1 5.0 %collective-permute-start.4 = (bf16[4,128,128]{2,1,0:T(8,128)(2,1)S(1)}, bf16[4,128,128]{2,1,0:T(8,128)(2,1)S(1)}, u32[]{:S(2)}, u32[]{:S(2)}) collective-permute-start(bf16[4,128,128]{2,1,0:T(8,128)(2,1)S(1)} %get-tuple-element.37.send_ref), channel_id=1, source_target_pairs={{0,4},{1,9},{2,6},{3,11},{4,0},{5,13},{6,2},{7,15},{8,12},{9,1},{1... | collective-permute-start | bytes 393224 | tf_op jit(solution)/shard_map/ppermute | solution.py:328
  20.2 4.6 %collective-permute-start.7 = (bf16[12,128,128]{2,1,0:T(8,128)(2,1)S(1)}, bf16[12,128,128]{2,1,0:T(8,128)(2,1)S(1)}, u32[]{:S(2)}, u32[]{:S(2)}) collective-permute-start(bf16[12,128,128]{2,1,0:T(8,128)(2,1)S(1)} %shard_map.78.mine_ref), channel_id=1, source_target_pairs={{0,1},{1,0},{2,3},{3,2},{4,5},{5,4},{6,7},{7,6},{8,9},{9,8},{10,11... | collective-permute-start | bytes 1179656 | tf_op jit(solution)/shard_map/ppermute | solution.py:328
  20.3 4.0 %collective-permute-start.5 = (bf16[1,128,128]{2,1,0:T(8,128)(2,1)S(1)}, bf16[1,128,128]{2,1,0:T(8,128)(2,1)S(1)}, u32[]{:S(2)}, u32[]{:S(2)}) collective-permute-start(bf16[1,128,128]{2,1,0:T(8,128)(2,1)S(1)} %get-tuple-element.42), channel_id=1, source_target_pairs={{0,2},{1,17},{2,0},{3,19},{4,6},{5,21},{6,4},{7,23},{8,10},{9,25},... | collective-permute-start | bytes 98312 | tf_op jit(solution)/shard_map/ppermute | solution.py:328
  24.3 1.6 %collective-permute-start.6 = (bf16[1,128,128]{2,1,0:T(8,128)(2,1)S(1)}, bf16[1,128,128]{2,1,0:T(8,128)(2,1)S(1)}, u32[]{:S(2)}, u32[]{:S(2)}) collective-permute-start(bf16[1,128,128]{2,1,0:T(8,128)(2,1)S(1)} %collective-permute-done.5.last_ref), channel_id=1, source_target_pairs={{0,1},{1,0},{2,3},{3,2},{4,5},{5,4},{6,7},{7,6},{8,9},{9,8},{10,11... | collective-permute-start | bytes 98312 | tf_op jit(solution)/shard_map/ppermute | solution.py:328

commit v5 on v4

--- a/solution.py
+++ b/solution.py
@@ -278,21 +278,21 @@
 
 
 def merge_kernel(
-    base_ref, left_ref, right_ref, leaf_left_ref, leaf_right_ref, first_right_ref, out_left_ref,
-    both_left_ref, both_right_ref,
+    base_ref, left_ref, right_ref, part_ref, leaf_left_ref, leaf_right_ref, first_right_ref,
+    out_ref, out_left_ref, both_right_ref,
 ):
     rank = base_ref.shape[-1]
+    bases = [dot(leaf_left_ref[i], base_ref[0]).astype(BF16) for i in range(2)]
     for i in range(2):
-        both_left_ref[i] = dot(leaf_left_ref[i], base_ref[0]).astype(BF16)
         out_left_ref[i] = dot(leaf_left_ref[i], left_ref[0]).astype(BF16)
         both_right_ref[i, :, :rank] = dot(leaf_right_ref[i], right_ref[0]).astype(BF16)
-        both_right_ref[i, :, rank : 2 * rank] = leaf_right_ref[i]
-        both_right_ref[i, :, 2 * rank :] = first_right_ref[i]
+        both_right_ref[i, :, rank:] = first_right_ref[i]
+        out_ref[i] = part_ref[i] + contract(bases[i], leaf_right_ref[i], 1, 1)
 
 
 def final_kernel(
-    position_ref, last_ref, other_last_ref, part_ref, first_left_ref, left_ref, base_ref, right_ref,
-    out_hbm, out, sems,
+    position_ref, last_ref, other_last_ref, first_left_ref, part_ref, left_ref, right_ref, out_hbm,
+    out, sems,
 ):
     odd = (position_ref[0] & 1) == 1
     f = pick(odd, last_ref, other_last_ref, 0)
@@ -302,7 +302,7 @@
     lasts = [dot(left_ref[i], f).astype(BF16) for i in range(2)]
     firsts = [dot(first_left_ref[i], first).astype(BF16) for i in range(2)]
     for i in range(2):
-        e = jnp.concatenate([lasts[i], base_ref[i], firsts[i]], 1)
+        e = jnp.concatenate([lasts[i], firsts[i]], 1)
         for c in range(CHUNKS):
             here = pl.ds(c * rows, rows)
             full = part_ref[i, here] + contract(e[c * rows : (c + 1) * rows], right_ref[i], 1, 1)
@@ -339,7 +339,7 @@
 
     tall = jax.ShapeDtypeStruct(outer_basis_stack.shape[:1] + outer_basis_stack.shape[2:], BF16)
 
-    wide = jax.ShapeDtypeStruct(tall.shape[:2] + (3 * rank,), BF16)
+    wide = jax.ShapeDtypeStruct(tall.shape[:2] + (2 * rank,), BF16)
     whole = jax.ShapeDtypeStruct(dense_a.shape, F32)
 
     def call(kernel, outs, *refs, scalar=True, mib=2):
@@ -408,20 +408,20 @@
     kernel = functools.partial(upper_kernel, levels)
     upper_terms = call(kernel, (1, 1, 1), swk, other_swk, mine, other)
     sides = call(
-        merge_kernel, (tall, tall, wide), *upper_terms, left, right, first_right,
-        scalar=False, mib=4,
+        merge_kernel, (whole, tall, wide), *upper_terms, part, left, right, first_right,
+        scalar=False, mib=12,
     )
     other_last = exchange(last, count, 0, 0)
 
     return pl.pallas_call(
         final_kernel,
         out_shape=jax.ShapeDtypeStruct(dense.shape, BF16),
-        in_specs=in_vmem(7),
+        in_specs=in_vmem(6),
         out_specs=pl.BlockSpec(memory_space=pltpu.HBM),
         scratch_shapes=[VMEM(dense.shape, BF16), pltpu.SemaphoreType.DMA((2 * CHUNKS,))],
         compiler_params=small(12),
         name="final",
-    )(place, last, other_last, part, first_left, *sides)
+    )(place, last, other_last, first_left, *sides)
 
 
 def solution(mesh):

time: 27.6 us -> 27.7 us (level)
  transfers between devices with their start and end apart: 8 -> 8, of which waited for: 5 -> 5; matrix products, arithmetic and copies ran while one was open for 0% -> 0% of each run, Pallas kernels for 14% -> 15%
where the time goes in v5:
time: 27.7 us; the launch traced here: 27.6 us
  starting transfers between devices  10.3 us (37%)
  waiting for transfers between devices  9.25 us (33%)
  Pallas kernels  7.82 us (28%)
    ppermute x8, starting transfers between devices, exchange(): return lax.ppermute(block, AXES, route)  10.3 us
    ppermute x8, waiting for transfers between devices, exchange(): return lax.ppermute(block, AXES, route)  9.25 us
    pallas_call x8, Pallas kernels, call(): pl.pallas_call(kernel, out_shape=outs, in_specs=in_vmem(len(refs), scalar...  3.58 us
    pallas_call x1, Pallas kernels, stages(): pl.pallas_call(functools.partial(head_kernel, levels), out_shape=(mats(4)...  2.08 us
    pallas_call x1, Pallas kernels, stages(): pl.pallas_call(final_kernel, out_shape=jax.ShapeDtypeStruct(dense.shape,...  1.45 us
    pallas_call x1, Pallas kernels, stages(): pl.pallas_call(dense_kernel, out_shape=jax.ShapeDtypeStruct(dense_a.shape...  0.71 us
  transfers between devices with their start and end apart: 8, of which 5 were waited for; matrix products, arithmetic and copies ran while one was open for 0% of the time, Pallas kernels for 15%

profile of v5, /device:TPU:0, one launch (start us, length us, event | category | flops | bytes accessed | tf_op | source)
XLA Modules:
  0.0 27.6 jit_solution(15396495793553080214)
XLA Ops:
  0.0 0.0 copy-start.2
  0.0 0.0 copy-start.3
  0.0 2.1 %head.1 = (bf16[4,128,128]{2,1,0:T(8,128)(2,1)S(1)}, bf16[2,128,128]{2,1,0:T(8,128)(2,1)S(1)}, bf16[6,128,128]{2,1,0:T(8,128)(2,1)S(1)}, bf16[2,128,128]{2,1,0:T(8,128)(2,1)S(1)}) custom-call(s32[1]{0:T(128)} %bitcast.position_ref, bf16[2,2,512,128]{3,2,1,0:T(8,128)(2,1)} %inner_hbm.1, bf16[1,4,2,128,128]{4,3,2,1,0:T(8,128)(2,1)} %up_hbm.1, ...), custom_call_target="tpu_custom_call" | custom-call | tf_op jit(solution)/shard_map/head/pallas_call | solution.py:355
  2.1 0.6 %collective-permute-start = (bf16[4,128,128]{2,1,0:T(8,128)(2,1)S(1)}, bf16[4,128,128]{2,1,0:T(8,128)(2,1)S(1)}, u32[]{:S(2)}, u32[]{:S(2)}) collective-permute-start(bf16[4,128,128]{2,1,0:T(8,128)(2,1)S(1)} %get-tuple-element.31.send_ref), channel_id=1, source_target_pairs={{0,1},{1,0},{2,3},{3,2},{4,5},{5,4},{6,7},{7,6},{8,9},{9,8},{10,11... | collective-permute-start | bytes 393224 | tf_op jit(solution)/shard_map/ppermute | solution.py:328
  2.7 0.1 collective-permute-start.2
  2.7 0.9 %collective-permute-done.got_ref = bf16[4,128,128]{2,1,0:T(8,128)(2,1)S(1)} collective-permute-done((bf16[4,128,128]{2,1,0:T(8,128)(2,1)S(1)}, bf16[4,128,128]{2,1,0:T(8,128)(2,1)S(1)}, u32[]{:S(2)}, u32[]{:S(2)}) %collective-permute-start) | collective-permute-done | bytes 131104 | tf_op jit(solution)/shard_map/ppermute | solution.py:328
  3.7 3.0 %collective-permute-start.1 = (bf16[3,128,128]{2,1,0:T(8,128)(2,1)S(1)}, bf16[3,128,128]{2,1,0:T(8,128)(2,1)S(1)}, u32[]{:S(2)}, u32[]{:S(2)}) collective-permute-start(bf16[3,128,128]{2,1,0:T(8,128)(2,1)S(1)} %get-tuple-element.34.send_ref), channel_id=1, source_target_pairs={{0,8},{1,3},{2,10},{3,1},{4,12},{5,7},{6,14},{7,5},{8,0},{9,11},{1... | collective-permute-start | bytes 294920 | tf_op jit(solution)/shard_map/ppermute | solution.py:328
  6.6 0.0 collective-permute-done.2.carry_ref.other_swk_ref
  6.6 2.6 %collective-permute-done.1.got_ref = bf16[3,128,128]{2,1,0:T(8,128)(2,1)S(1)} collective-permute-done((bf16[3,128,128]{2,1,0:T(8,128)(2,1)S(1)}, bf16[3,128,128]{2,1,0:T(8,128)(2,1)S(1)}, u32[]{:S(2)}, u32[]{:S(2)}) %collective-permute-start.1) | collective-permute-done | bytes 98336 | tf_op jit(solution)/shard_map/ppermute | solution.py:328
  9.3 2.0 %collective-permute-start.3 = (bf16[6,128,128]{2,1,0:T(8,128)(2,1)S(1)}, bf16[6,128,128]{2,1,0:T(8,128)(2,1)S(1)}, u32[]{:S(2)}, u32[]{:S(2)}) collective-permute-start(bf16[6,128,128]{2,1,0:T(8,128)(2,1)S(1)} %get-tuple-element.35.send_ref), channel_id=1, source_target_pairs={{0,2},{1,5},{2,0},{3,7},{4,6},{5,1},{6,4},{7,3},{8,10},{9,13},{10,... | collective-permute-start | bytes 589832 | tf_op jit(solution)/shard_map/ppermute | solution.py:328
  11.3 3.7 %collective-permute-done.3.got_ref.refs_0_ = bf16[6,128,128]{2,1,0:T(8,128)(2,1)S(1)} collective-permute-done((bf16[6,128,128]{2,1,0:T(8,128)(2,1)S(1)}, bf16[6,128,128]{2,1,0:T(8,128)(2,1)S(1)}, u32[]{:S(2)}, u32[]{:S(2)}) %collective-permute-start.3) | collective-permute-done | bytes 196640 | tf_op jit(solution)/shard_map/ppermute | solution.py:328
  15.1 0.0 copy-start
  15.1 0.0 copy-start.1
  15.1 0.0 copy-start.4
  15.1 2.0 %collective-permute-start.4 = (bf16[4,128,128]{2,1,0:T(8,128)(2,1)S(1)}, bf16[4,128,128]{2,1,0:T(8,128)(2,1)S(1)}, u32[]{:S(2)}, u32[]{:S(2)}) collective-permute-start(bf16[4,128,128]{2,1,0:T(8,128)(2,1)S(1)} %get-tuple-element.37.send_ref), channel_id=1, source_target_pairs={{0,4},{1,9},{2,6},{3,11},{4,0},{5,13},{6,2},{7,15},{8,12},{9,1},{1... | collective-permute-start | bytes 393224 | tf_op jit(solution)/shard_map/ppermute | solution.py:328
  17.1 0.0 copy-done.2
  17.1 0.0 copy-done.3
  17.1 0.7 %dense.1.dense_ref = f32[2,512,512]{2,1,0:T(8,128)S(1)} custom-call(bf16[2,512,512]{2,1,0:T(8,128)(2,1)S(1)} %copy-done.2, bf16[2,512,512]{2,1,0:T(8,128)(2,1)S(1)} %copy-done.3), custom_call_target="tpu_custom_call" | custom-call | tf_op jit(solution)/shard_map/dense/pallas_call | solution.py:372
  17.8 0.0 copy-done
  17.8 0.0 copy-done.1
  17.8 0.0 copy-done.4
  17.8 2.2 %shard_map.76 = (f32[2,512,512]{2,1,0:T(8,128)S(1)}, bf16[2,512,128]{2,1,0:T(8,128)(2,1)S(1)}, bf16[2,512,128]{2,1,0:T(8,128)(2,1)S(1)}, bf16[1,128,128]{2,1,0:T...) custom-call(s32[1]{0:T(128)} %bitcast.position_ref, ...), custom_call_target="tpu_custom_call" | custom-call | tf_op jit(solution)/shard_map/pallas_call | solution.py:347
  20.0 0.1 collective-permute-done.4.got_ref.refs_1_
  20.2 0.1 collective-permute-start.7
  20.3 2.0 %collective-permute-start.5 = (bf16[1,128,128]{2,1,0:T(8,128)(2,1)S(1)}, bf16[1,128,128]{2,1,0:T(8,128)(2,1)S(1)}, u32[]{:S(2)}, u32[]{:S(2)}) collective-permute-start(bf16[1,128,128]{2,1,0:T(8,128)(2,1)S(1)} %get-tuple-element.42), channel_id=1, source_target_pairs={{0,2},{1,17},{2,0},{3,19},{4,6},{5,21},{6,4},{7,23},{8,10},{9,25},... | collective-permute-start | bytes 98312 | tf_op jit(solution)/shard_map/ppermute | solution.py:328
  22.3 2.0 %collective-permute-done.5.last_ref = bf16[1,128,128]{2,1,0:T(8,128)(2,1)S(1)} collective-permute-done((bf16[1,128,128]{2,1,0:T(8,128)(2,1)S(1)}, bf16[1,128,128]{2,1,0:T(8,128)(2,1)S(1)}, u32[]{:S(2)}, u32[]{:S(2)}) %collective-permute-start.5) | collective-permute-done | bytes 32800 | tf_op jit(solution)/shard_map/ppermute | solution.py:328
  24.3 0.6 %collective-permute-start.6 = (bf16[1,128,128]{2,1,0:T(8,128)(2,1)S(1)}, bf16[1,128,128]{2,1,0:T(8,128)(2,1)S(1)}, u32[]{:S(2)}, u32[]{:S(2)}) collective-permute-start(bf16[1,128,128]{2,1,0:T(8,128)(2,1)S(1)} %collective-permute-done.5.last_ref), channel_id=1, source_target_pairs={{0,1},{1,0},{2,3},{3,2},{4,5},{5,4},{6,7},{7,6},{8,9},{9,8},{10,11... | collective-permute-start | bytes 98312 | tf_op jit(solution)/shard_map/ppermute | solution.py:328
  24.8 0.0 collective-permute-done.7.other_ref
  24.8 0.6 %shard_map.79 = (bf16[1,128,128]{2,1,0:T(8,128)(2,1)S(1)}, bf16[1,128,128]{2,1,0:T(8,128)(2,1)S(1)}, bf16[1,128,128]{2,1,0:T(8,128)(2,1)S(1)}) custom-call(s32[1]{0:T(128)} %bitcast.position_ref, bf16[6,128,128]{2,1,0:T(8,128)(2,1)S(1)} %get-tuple-element.33.swk_ref, bf16[6,128,128]{2,1,0:T(8,128)(2,1)S(1)} %collective-permute-done.2.carry_ref.other_swk_ref, ...), custom_call_target="tpu_custom_call" | custom-call | tf_op jit(solution)/shard_map/pallas_call | solution.py:347
  25.5 0.6 %shard_map.80 = (f32[2,512,512]{2,1,0:T(8,128)S(1)}, bf16[2,512,128]{2,1,0:T(8,128)(2,1)S(1)}, bf16[2,512,256]{2,1,0:T(8,128)(2,1)S(1)}) custom-call(bf16[1,128,128]{2,1,0:T(8,128)(2,1)S(1)} %get-tuple-element.47.base_ref, bf16[1,128,128]{2,1,0:T(8,128)(2,1)S(1)} %get-tuple-element.48.left_ref, bf16[1,128,128]{2,1,0:T(8,128)(2,1)S(1)} %get-tuple-element.49.right_ref, ...), custom_call_target="tpu_custom_call" | custom-call | tf_op jit(solution)/shard_map/pallas_call | solution.py:347
  26.1 0.0 collective-permute-done.6.other_last_ref
  26.1 1.5 %final.1 = bf16[2,512,512]{2,1,0:T(8,128)(2,1)} custom-call(s32[1]{0:T(128)} %bitcast.position_ref, bf16[1,128,128]{2,1,0:T(8,128)(2,1)S(1)} %collective-permute-done.5.last_ref, bf16[1,128,128]{2,1,0:T(8,128)(2,1)S(1)} %collective-permute-done.6.other_last_ref, bf16[2,512,128]{2,1,0:T(8,128)(2,1)S(1)} %get-tuple-element.43.first_left_ref, ...), custom_call_target="tpu_custom_call" | custom-call | tf_op jit(solution)/shard_map/final/pallas_call | solution.py:416
  (5 shorter events, 0.1 us)
Async XLA Ops:
  0.0 17.1 %copy-start.2 = (bf16[2,512,512]{2,1,0:T(8,128)(2,1)S(1)}, bf16[2,512,512]{2,1,0:T(8,128)(2,1)}, u32[]{:S(2)}) copy-start(bf16[2,512,512]{2,1,0:T(8,128)(2,1)} %a_ref.1) | copy-start | bytes 3145732
  0.0 17.1 %copy-start.3 = (bf16[2,512,512]{2,1,0:T(8,128)(2,1)S(1)}, bf16[2,512,512]{2,1,0:T(8,128)(2,1)}, u32[]{:S(2)}) copy-start(bf16[2,512,512]{2,1,0:T(8,128)(2,1)} %b_ref.1) | copy-start | bytes 3145732
  2.1 1.5 %collective-permute-start = (bf16[4,128,128]{2,1,0:T(8,128)(2,1)S(1)}, bf16[4,128,128]{2,1,0:T(8,128)(2,1)S(1)}, u32[]{:S(2)}, u32[]{:S(2)}) collective-permute-start(bf16[4,128,128]{2,1,0:T(8,128)(2,1)S(1)} %get-tuple-element.31.send_ref), channel_id=1, source_target_pairs={{0,1},{1,0},{2,3},{3,2},{4,5},{5,4},{6,7},{7,6},{8,9},{9,8},{10,11... | collective-permute-start | bytes 393224 | tf_op jit(solution)/shard_map/ppermute | solution.py:328
  2.7 4.0 %collective-permute-start.2 = (bf16[6,128,128]{2,1,0:T(8,128)(2,1)S(1)}, bf16[6,128,128]{2,1,0:T(8,128)(2,1)S(1)}, u32[]{:S(2)}, u32[]{:S(2)}) collective-permute-start(bf16[6,128,128]{2,1,0:T(8,128)(2,1)S(1)} %get-tuple-element.33.swk_ref), channel_id=1, source_target_pairs={{0,1},{1,0},{2,3},{3,2},{4,5},{5,4},{6,7},{7,6},{8,9},{9,8},{10,11... | collective-permute-start | bytes 589832 | tf_op jit(solution)/shard_map/ppermute | solution.py:328
  3.7 5.6 %collective-permute-start.1 = (bf16[3,128,128]{2,1,0:T(8,128)(2,1)S(1)}, bf16[3,128,128]{2,1,0:T(8,128)(2,1)S(1)}, u32[]{:S(2)}, u32[]{:S(2)}) collective-permute-start(bf16[3,128,128]{2,1,0:T(8,128)(2,1)S(1)} %get-tuple-element.34.send_ref), channel_id=1, source_target_pairs={{0,8},{1,3},{2,10},{3,1},{4,12},{5,7},{6,14},{7,5},{8,0},{9,11},{1... | collective-permute-start | bytes 294920 | tf_op jit(solution)/shard_map/ppermute | solution.py:328
  9.3 5.7 %collective-permute-start.3 = (bf16[6,128,128]{2,1,0:T(8,128)(2,1)S(1)}, bf16[6,128,128]{2,1,0:T(8,128)(2,1)S(1)}, u32[]{:S(2)}, u32[]{:S(2)}) collective-permute-start(bf16[6,128,128]{2,1,0:T(8,128)(2,1)S(1)} %get-tuple-element.35.send_ref), channel_id=1, source_target_pairs={{0,2},{1,5},{2,0},{3,7},{4,6},{5,1},{6,4},{7,3},{8,10},{9,13},{10,... | collective-permute-start | bytes 589832 | tf_op jit(solution)/shard_map/ppermute | solution.py:328
  15.1 2.8 %copy-start = (bf16[1,4,2,128,128]{4,3,2,1,0:T(8,128)(2,1)S(1)}, bf16[1,4,2,128,128]{4,3,2,1,0:T(8,128)(2,1)}, u32[]{:S(2)}) copy-start(bf16[1,4,2,128,128]{4,3,2,1,0:T(8,128)(2,1)} %down_ref.1) | copy-start | bytes 786436
  15.1 2.8 %copy-start.1 = (bf16[1,2,4,128,128]{4,3,2,1,0:T(8,128)(2,1)S(1)}, bf16[1,2,4,128,128]{4,3,2,1,0:T(8,128)(2,1)}, u32[]{:S(2)}) copy-start(bf16[1,2,4,128,128]{4,3,2,1,0:T(8,128)(2,1)} %block_ref.1) | copy-start | bytes 786436
  15.1 2.7 %copy-start.4 = (bf16[2,2,512,128]{3,2,1,0:T(8,128)(2,1)S(1)}, bf16[2,2,512,128]{3,2,1,0:T(8,128)(2,1)}, u32[]{:S(2)}) copy-start(bf16[2,2,512,128]{3,2,1,0:T(8,128)(2,1)} %outer_ref.1) | copy-start | bytes 1572868
  15.1 5.0 %collective-permute-start.4 = (bf16[4,128,128]{2,1,0:T(8,128)(2,1)S(1)}, bf16[4,128,128]{2,1,0:T(8,128)(2,1)S(1)}, u32[]{:S(2)}, u32[]{:S(2)}) collective-permute-start(bf16[4,128,128]{2,1,0:T(8,128)(2,1)S(1)} %get-tuple-element.37.send_ref), channel_id=1, source_target_pairs={{0,4},{1,9},{2,6},{3,11},{4,0},{5,13},{6,2},{7,15},{8,12},{9,1},{1... | collective-permute-start | bytes 393224 | tf_op jit(solution)/shard_map/ppermute | solution.py:328
  20.2 4.6 %collective-permute-start.7 = (bf16[12,128,128]{2,1,0:T(8,128)(2,1)S(1)}, bf16[12,128,128]{2,1,0:T(8,128)(2,1)S(1)}, u32[]{:S(2)}, u32[]{:S(2)}) collective-permute-start(bf16[12,128,128]{2,1,0:T(8,128)(2,1)S(1)} %shard_map.78.mine_ref), channel_id=1, source_target_pairs={{0,1},{1,0},{2,3},{3,2},{4,5},{5,4},{6,7},{7,6},{8,9},{9,8},{10,11... | collective-permute-start | bytes 1179656 | tf_op jit(solution)/shard_map/ppermute | solution.py:328
  20.3 4.0 %collective-permute-start.5 = (bf16[1,128,128]{2,1,0:T(8,128)(2,1)S(1)}, bf16[1,128,128]{2,1,0:T(8,128)(2,1)S(1)}, u32[]{:S(2)}, u32[]{:S(2)}) collective-permute-start(bf16[1,128,128]{2,1,0:T(8,128)(2,1)S(1)} %get-tuple-element.42), channel_id=1, source_target_pairs={{0,2},{1,17},{2,0},{3,19},{4,6},{5,21},{6,4},{7,23},{8,10},{9,25},... | collective-permute-start | bytes 98312 | tf_op jit(solution)/shard_map/ppermute | solution.py:328
  24.3 1.8 %collective-permute-start.6 = (bf16[1,128,128]{2,1,0:T(8,128)(2,1)S(1)}, bf16[1,128,128]{2,1,0:T(8,128)(2,1)S(1)}, u32[]{:S(2)}, u32[]{:S(2)}) collective-permute-start(bf16[1,128,128]{2,1,0:T(8,128)(2,1)S(1)} %collective-permute-done.5.last_ref), channel_id=1, source_target_pairs={{0,1},{1,0},{2,3},{3,2},{4,5},{5,4},{6,7},{7,6},{8,9},{9,8},{10,11... | collective-permute-start | bytes 98312 | tf_op jit(solution)/shard_map/ppermute | solution.py:328

commit v6 on v5

--- a/solution.py
+++ b/solution.py
@@ -282,12 +282,18 @@
     out_ref, out_left_ref, both_right_ref,
 ):
     rank = base_ref.shape[-1]
-    bases = [dot(leaf_left_ref[i], base_ref[0]).astype(BF16) for i in range(2)]
     for i in range(2):
         out_left_ref[i] = dot(leaf_left_ref[i], left_ref[0]).astype(BF16)
         both_right_ref[i, :, :rank] = dot(leaf_right_ref[i], right_ref[0]).astype(BF16)
         both_right_ref[i, :, rank:] = first_right_ref[i]
+    bases = [dot(leaf_left_ref[i], base_ref[0]).astype(BF16) for i in range(2)]
+    for i in range(2):
         out_ref[i] = part_ref[i] + contract(bases[i], leaf_right_ref[i], 1, 1)
+
+
+def top_kernel(levels, *refs):
+    upper_kernel(levels, *refs[:5], *refs[-3:])
+    merge_kernel(*refs[-3:], *refs[5:-3])
 
 
 def final_kernel(
@@ -342,15 +348,16 @@
     wide = jax.ShapeDtypeStruct(tall.shape[:2] + (2 * rank,), BF16)
     whole = jax.ShapeDtypeStruct(dense_a.shape, F32)
 
-    def call(kernel, outs, *refs, scalar=True, mib=2):
+    def call(kernel, outs, *refs, mib=2, scratch=0):
         outs = tuple(mats(n) if isinstance(n, int) else n for n in outs)
         return pl.pallas_call(
             kernel,
             out_shape=outs,
-            in_specs=in_vmem(len(refs), scalar),
+            in_specs=in_vmem(len(refs)),
+            scratch_shapes=[VMEM((1, rank, rank), BF16)] * scratch,
             out_specs=tuple(in_vmem(len(outs), False)),
             compiler_params=small(mib),
-        )(*([place] if scalar else []), *refs)
+        )(place, *refs)
 
     send, pq, swk, leaf_inner = pl.pallas_call(
         functools.partial(head_kernel, levels),
@@ -405,11 +412,10 @@
     kernel = functools.partial(pack_kernel, len(received))
     (mine,) = call(kernel, (size,), *received, *nodes, carry)
     other = exchange(mine, count, 0, 0)
-    kernel = functools.partial(upper_kernel, levels)
-    upper_terms = call(kernel, (1, 1, 1), swk, other_swk, mine, other)
+    kernel = functools.partial(top_kernel, levels)
     sides = call(
-        merge_kernel, (whole, tall, wide), *upper_terms, part, left, right, first_right,
-        scalar=False, mib=12,
+        kernel, (whole, tall, wide), swk, other_swk, mine, other, part, left, right,
+        first_right, mib=12, scratch=3,
     )
     other_last = exchange(last, count, 0, 0)
 

time: 27.7 us -> 27.7 us (level)
    pallas_call x8 -> x7, Pallas kernels: 3.58 us -> 3.58 us  [call(): pl.pallas_call(kernel, out_shape=outs, in_specs=in_vmem(len(refs)), scrat...]
where the time goes in v6:
time: 27.7 us; the launch traced here: 27.5 us
  starting transfers between devices  10.3 us (37%)
  waiting for transfers between devices  9.25 us (33%)
  Pallas kernels  7.81 us (28%)
    ppermute x8, starting transfers between devices, exchange(): return lax.ppermute(block, AXES, route)  10.3 us
    ppermute x8, waiting for transfers between devices, exchange(): return lax.ppermute(block, AXES, route)  9.25 us
    pallas_call x7, Pallas kernels, call(): pl.pallas_call(kernel, out_shape=outs, in_specs=in_vmem(len(refs)), scrat...  3.58 us
    pallas_call x1, Pallas kernels, stages(): pl.pallas_call(functools.partial(head_kernel, levels), out_shape=(mats(4)...  2.08 us
    pallas_call x1, Pallas kernels, stages(): pl.pallas_call(final_kernel, out_shape=jax.ShapeDtypeStruct(dense.shape,...  1.44 us
    pallas_call x1, Pallas kernels, stages(): pl.pallas_call(dense_kernel, out_shape=jax.ShapeDtypeStruct(dense_a.shape...  0.71 us
  transfers between devices with their start and end apart: 8, of which 5 were waited for; matrix products, arithmetic and copies ran while one was open for 0% of the time, Pallas kernels for 15%

profile of v6, /device:TPU:0, one launch (start us, length us, event | category | flops | bytes accessed | tf_op | source)
XLA Modules:
  0.0 27.5 jit_solution(9027275489669977881)
XLA Ops:
  0.0 0.0 copy-start.2
  0.0 0.0 copy-start.3
  0.0 2.1 %head.1 = (bf16[4,128,128]{2,1,0:T(8,128)(2,1)S(1)}, bf16[2,128,128]{2,1,0:T(8,128)(2,1)S(1)}, bf16[6,128,128]{2,1,0:T(8,128)(2,1)S(1)}, bf16[2,128,128]{2,1,0:T(8,128)(2,1)S(1)}) custom-call(s32[1]{0:T(128)} %bitcast.position_ref.refs_0_, bf16[2,2,512,128]{3,2,1,0:T(8,128)(2,1)} %inner_hbm.1, bf16[1,4,2,128,128]{4,3,2,1,0:T(8,128)(2,1)} %up_hbm.1, ...), custom_call_target="tpu_custom_call" | custom-call | tf_op jit(solution)/shard_map/head/pallas_call | solution.py:362
  2.1 0.6 %collective-permute-start = (bf16[4,128,128]{2,1,0:T(8,128)(2,1)S(1)}, bf16[4,128,128]{2,1,0:T(8,128)(2,1)S(1)}, u32[]{:S(2)}, u32[]{:S(2)}) collective-permute-start(bf16[4,128,128]{2,1,0:T(8,128)(2,1)S(1)} %get-tuple-element.28.send_ref), channel_id=1, source_target_pairs={{0,1},{1,0},{2,3},{3,2},{4,5},{5,4},{6,7},{7,6},{8,9},{9,8},{10,11... | collective-permute-start | bytes 393224 | tf_op jit(solution)/shard_map/ppermute | solution.py:334
  2.7 0.1 collective-permute-start.2
  2.7 0.9 %collective-permute-done.got_ref = bf16[4,128,128]{2,1,0:T(8,128)(2,1)S(1)} collective-permute-done((bf16[4,128,128]{2,1,0:T(8,128)(2,1)S(1)}, bf16[4,128,128]{2,1,0:T(8,128)(2,1)S(1)}, u32[]{:S(2)}, u32[]{:S(2)}) %collective-permute-start) | collective-permute-done | bytes 131104 | tf_op jit(solution)/shard_map/ppermute | solution.py:334
  3.7 3.0 %collective-permute-start.1 = (bf16[3,128,128]{2,1,0:T(8,128)(2,1)S(1)}, bf16[3,128,128]{2,1,0:T(8,128)(2,1)S(1)}, u32[]{:S(2)}, u32[]{:S(2)}) collective-permute-start(bf16[3,128,128]{2,1,0:T(8,128)(2,1)S(1)} %get-tuple-element.31.send_ref), channel_id=1, source_target_pairs={{0,8},{1,3},{2,10},{3,1},{4,12},{5,7},{6,14},{7,5},{8,0},{9,11},{1... | collective-permute-start | bytes 294920 | tf_op jit(solution)/shard_map/ppermute | solution.py:334
  6.6 0.0 collective-permute-done.2.carry_ref.other_swk_ref.refs_2_
  6.6 2.6 %collective-permute-done.1.got_ref = bf16[3,128,128]{2,1,0:T(8,128)(2,1)S(1)} collective-permute-done((bf16[3,128,128]{2,1,0:T(8,128)(2,1)S(1)}, bf16[3,128,128]{2,1,0:T(8,128)(2,1)S(1)}, u32[]{:S(2)}, u32[]{:S(2)}) %collective-permute-start.1) | collective-permute-done | bytes 98336 | tf_op jit(solution)/shard_map/ppermute | solution.py:334
  9.3 2.0 %collective-permute-start.3 = (bf16[6,128,128]{2,1,0:T(8,128)(2,1)S(1)}, bf16[6,128,128]{2,1,0:T(8,128)(2,1)S(1)}, u32[]{:S(2)}, u32[]{:S(2)}) collective-permute-start(bf16[6,128,128]{2,1,0:T(8,128)(2,1)S(1)} %get-tuple-element.32.send_ref), channel_id=1, source_target_pairs={{0,2},{1,5},{2,0},{3,7},{4,6},{5,1},{6,4},{7,3},{8,10},{9,13},{10,... | collective-permute-start | bytes 589832 | tf_op jit(solution)/shard_map/ppermute | solution.py:334
  11.3 3.7 %collective-permute-done.3.got_ref.refs_0_ = bf16[6,128,128]{2,1,0:T(8,128)(2,1)S(1)} collective-permute-done((bf16[6,128,128]{2,1,0:T(8,128)(2,1)S(1)}, bf16[6,128,128]{2,1,0:T(8,128)(2,1)S(1)}, u32[]{:S(2)}, u32[]{:S(2)}) %collective-permute-start.3) | collective-permute-done | bytes 196640 | tf_op jit(solution)/shard_map/ppermute | solution.py:334
  15.1 0.0 copy-start
  15.1 0.0 copy-start.1
  15.1 0.0 copy-start.4
  15.1 2.0 %collective-permute-start.4 = (bf16[4,128,128]{2,1,0:T(8,128)(2,1)S(1)}, bf16[4,128,128]{2,1,0:T(8,128)(2,1)S(1)}, u32[]{:S(2)}, u32[]{:S(2)}) collective-permute-start(bf16[4,128,128]{2,1,0:T(8,128)(2,1)S(1)} %get-tuple-element.34.send_ref), channel_id=1, source_target_pairs={{0,4},{1,9},{2,6},{3,11},{4,0},{5,13},{6,2},{7,15},{8,12},{9,1},{1... | collective-permute-start | bytes 393224 | tf_op jit(solution)/shard_map/ppermute | solution.py:334
  17.1 0.0 copy-done.2
  17.1 0.0 copy-done.3
  17.1 0.7 %dense.1.dense_ref = f32[2,512,512]{2,1,0:T(8,128)S(1)} custom-call(bf16[2,512,512]{2,1,0:T(8,128)(2,1)S(1)} %copy-done.2, bf16[2,512,512]{2,1,0:T(8,128)(2,1)S(1)} %copy-done.3), custom_call_target="tpu_custom_call" | custom-call | tf_op jit(solution)/shard_map/dense/pallas_call | solution.py:379
  17.8 0.0 copy-done
  17.8 0.0 copy-done.1
  17.8 0.0 copy-done.4
  17.8 2.2 %shard_map.76 = (f32[2,512,512]{2,1,0:T(8,128)S(1)}, bf16[2,512,128]{2,1,0:T(8,128)(2,1)S(1)}, bf16[2,512,128]{2,1,0:T(8,128)(2,1)S(1)}, bf16[1,128,128]{2,1,0:T...) custom-call(s32[1]{0:T(128)} %bitcast.position_ref.refs_0_, ...), custom_call_target="tpu_custom_call" | custom-call | tf_op jit(solution)/shard_map/pallas_call | solution.py:353
  20.0 0.1 collective-permute-done.4.got_ref.refs_1_
  20.2 0.1 collective-permute-start.7
  20.3 2.0 %collective-permute-start.5 = (bf16[1,128,128]{2,1,0:T(8,128)(2,1)S(1)}, bf16[1,128,128]{2,1,0:T(8,128)(2,1)S(1)}, u32[]{:S(2)}, u32[]{:S(2)}) collective-permute-start(bf16[1,128,128]{2,1,0:T(8,128)(2,1)S(1)} %get-tuple-element.39), channel_id=1, source_target_pairs={{0,2},{1,17},{2,0},{3,19},{4,6},{5,21},{6,4},{7,23},{8,10},{9,25},... | collective-permute-start | bytes 98312 | tf_op jit(solution)/shard_map/ppermute | solution.py:334
  22.3 2.0 %collective-permute-done.5.last_ref = bf16[1,128,128]{2,1,0:T(8,128)(2,1)S(1)} collective-permute-done((bf16[1,128,128]{2,1,0:T(8,128)(2,1)S(1)}, bf16[1,128,128]{2,1,0:T(8,128)(2,1)S(1)}, u32[]{:S(2)}, u32[]{:S(2)}) %collective-permute-start.5) | collective-permute-done | bytes 32800 | tf_op jit(solution)/shard_map/ppermute | solution.py:334
  24.3 0.6 %collective-permute-start.6 = (bf16[1,128,128]{2,1,0:T(8,128)(2,1)S(1)}, bf16[1,128,128]{2,1,0:T(8,128)(2,1)S(1)}, u32[]{:S(2)}, u32[]{:S(2)}) collective-permute-start(bf16[1,128,128]{2,1,0:T(8,128)(2,1)S(1)} %collective-permute-done.5.last_ref), channel_id=1, source_target_pairs={{0,1},{1,0},{2,3},{3,2},{4,5},{5,4},{6,7},{7,6},{8,9},{9,8},{10,11... | collective-permute-start | bytes 98312 | tf_op jit(solution)/shard_map/ppermute | solution.py:334
  24.8 0.0 collective-permute-done.7.refs_4_
  24.8 1.2 %shard_map.79 = (f32[2,512,512]{2,1,0:T(8,128)S(1)}, bf16[2,512,128]{2,1,0:T(8,128)(2,1)S(1)}, bf16[2,512,256]{2,1,0:T(8,128)(2,1)S(1)}) custom-call(s32[1]{0:T(128)} %bitcast.position_ref.refs_0_, bf16[6,128,128]{2,1,0:T(8,128)(2,1)S(1)} %get-tuple-element.30.swk_ref.refs_1_, ...), custom_call_target="tpu_custom_call" | custom-call | tf_op jit(solution)/shard_map/pallas_call | solution.py:353
  26.1 0.0 collective-permute-done.6.other_last_ref
  26.1 1.4 %final.1 = bf16[2,512,512]{2,1,0:T(8,128)(2,1)} custom-call(s32[1]{0:T(128)} %bitcast.position_ref.refs_0_, bf16[1,128,128]{2,1,0:T(8,128)(2,1)S(1)} %collective-permute-done.5.last_ref, bf16[1,128,128]{2,1,0:T(8,128)(2,1)S(1)} %collective-permute-done.6.other_last_ref, bf16[2,512,128]{2,1,0:T(8,128)(2,1)S(1)} %get-tuple-element.40.first_left_ref, ...), custom_call_target="tpu_custom_call" | custom-call | tf_op jit(solution)/shard_map/final/pallas_call | solution.py:422
  (5 shorter events, 0.1 us)
Async XLA Ops:
  0.0 17.1 %copy-start.2 = (bf16[2,512,512]{2,1,0:T(8,128)(2,1)S(1)}, bf16[2,512,512]{2,1,0:T(8,128)(2,1)}, u32[]{:S(2)}) copy-start(bf16[2,512,512]{2,1,0:T(8,128)(2,1)} %a_ref.1) | copy-start | bytes 3145732
  0.0 17.1 %copy-start.3 = (bf16[2,512,512]{2,1,0:T(8,128)(2,1)S(1)}, bf16[2,512,512]{2,1,0:T(8,128)(2,1)}, u32[]{:S(2)}) copy-start(bf16[2,512,512]{2,1,0:T(8,128)(2,1)} %b_ref.1) | copy-start | bytes 3145732
  2.1 1.5 %collective-permute-start = (bf16[4,128,128]{2,1,0:T(8,128)(2,1)S(1)}, bf16[4,128,128]{2,1,0:T(8,128)(2,1)S(1)}, u32[]{:S(2)}, u32[]{:S(2)}) collective-permute-start(bf16[4,128,128]{2,1,0:T(8,128)(2,1)S(1)} %get-tuple-element.28.send_ref), channel_id=1, source_target_pairs={{0,1},{1,0},{2,3},{3,2},{4,5},{5,4},{6,7},{7,6},{8,9},{9,8},{10,11... | collective-permute-start | bytes 393224 | tf_op jit(solution)/shard_map/ppermute | solution.py:334
  2.7 4.0 %collective-permute-start.2 = (bf16[6,128,128]{2,1,0:T(8,128)(2,1)S(1)}, bf16[6,128,128]{2,1,0:T(8,128)(2,1)S(1)}, u32[]{:S(2)}, u32[]{:S(2)}) collective-permute-start(bf16[6,128,128]{2,1,0:T(8,128)(2,1)S(1)} %get-tuple-element.30.swk_ref.refs_1_), channel_id=1, source_target_pairs={{0,1},{1,0},{2,3},{3,2},{4,5},{5,4},{6,7},{7,6},{8,9},{9,8},{10,11... | collective-permute-start | bytes 589832 | tf_op jit(solution)/shard_map/ppermute | solution.py:334
  3.7 5.6 %collective-permute-start.1 = (bf16[3,128,128]{2,1,0:T(8,128)(2,1)S(1)}, bf16[3,128,128]{2,1,0:T(8,128)(2,1)S(1)}, u32[]{:S(2)}, u32[]{:S(2)}) collective-permute-start(bf16[3,128,128]{2,1,0:T(8,128)(2,1)S(1)} %get-tuple-element.31.send_ref), channel_id=1, source_target_pairs={{0,8},{1,3},{2,10},{3,1},{4,12},{5,7},{6,14},{7,5},{8,0},{9,11},{1... | collective-permute-start | bytes 294920 | tf_op jit(solution)/shard_map/ppermute | solution.py:334
  9.3 5.7 %collective-permute-start.3 = (bf16[6,128,128]{2,1,0:T(8,128)(2,1)S(1)}, bf16[6,128,128]{2,1,0:T(8,128)(2,1)S(1)}, u32[]{:S(2)}, u32[]{:S(2)}) collective-permute-start(bf16[6,128,128]{2,1,0:T(8,128)(2,1)S(1)} %get-tuple-element.32.send_ref), channel_id=1, source_target_pairs={{0,2},{1,5},{2,0},{3,7},{4,6},{5,1},{6,4},{7,3},{8,10},{9,13},{10,... | collective-permute-start | bytes 589832 | tf_op jit(solution)/shard_map/ppermute | solution.py:334
  15.1 2.8 %copy-start = (bf16[1,4,2,128,128]{4,3,2,1,0:T(8,128)(2,1)S(1)}, bf16[1,4,2,128,128]{4,3,2,1,0:T(8,128)(2,1)}, u32[]{:S(2)}) copy-start(bf16[1,4,2,128,128]{4,3,2,1,0:T(8,128)(2,1)} %down_ref.1) | copy-start | bytes 786436
  15.1 2.8 %copy-start.1 = (bf16[1,2,4,128,128]{4,3,2,1,0:T(8,128)(2,1)S(1)}, bf16[1,2,4,128,128]{4,3,2,1,0:T(8,128)(2,1)}, u32[]{:S(2)}) copy-start(bf16[1,2,4,128,128]{4,3,2,1,0:T(8,128)(2,1)} %block_ref.1) | copy-start | bytes 786436
  15.1 2.7 %copy-start.4 = (bf16[2,2,512,128]{3,2,1,0:T(8,128)(2,1)S(1)}, bf16[2,2,512,128]{3,2,1,0:T(8,128)(2,1)}, u32[]{:S(2)}) copy-start(bf16[2,2,512,128]{3,2,1,0:T(8,128)(2,1)} %outer_ref.1) | copy-start | bytes 1572868
  15.1 5.0 %collective-permute-start.4 = (bf16[4,128,128]{2,1,0:T(8,128)(2,1)S(1)}, bf16[4,128,128]{2,1,0:T(8,128)(2,1)S(1)}, u32[]{:S(2)}, u32[]{:S(2)}) collective-permute-start(bf16[4,128,128]{2,1,0:T(8,128)(2,1)S(1)} %get-tuple-element.34.send_ref), channel_id=1, source_target_pairs={{0,4},{1,9},{2,6},{3,11},{4,0},{5,13},{6,2},{7,15},{8,12},{9,1},{1... | collective-permute-start | bytes 393224 | tf_op jit(solution)/shard_map/ppermute | solution.py:334
  20.2 4.6 %collective-permute-start.7 = (bf16[12,128,128]{2,1,0:T(8,128)(2,1)S(1)}, bf16[12,128,128]{2,1,0:T(8,128)(2,1)S(1)}, u32[]{:S(2)}, u32[]{:S(2)}) collective-permute-start(bf16[12,128,128]{2,1,0:T(8,128)(2,1)S(1)} %shard_map.78.refs_3_), channel_id=1, source_target_pairs={{0,1},{1,0},{2,3},{3,2},{4,5},{5,4},{6,7},{7,6},{8,9},{9,8},{10,11... | collective-permute-start | bytes 1179656 | tf_op jit(solution)/shard_map/ppermute | solution.py:334
  20.3 4.0 %collective-permute-start.5 = (bf16[1,128,128]{2,1,0:T(8,128)(2,1)S(1)}, bf16[1,128,128]{2,1,0:T(8,128)(2,1)S(1)}, u32[]{:S(2)}, u32[]{:S(2)}) collective-permute-start(bf16[1,128,128]{2,1,0:T(8,128)(2,1)S(1)} %get-tuple-element.39), channel_id=1, source_target_pairs={{0,2},{1,17},{2,0},{3,19},{4,6},{5,21},{6,4},{7,23},{8,10},{9,25},... | collective-permute-start | bytes 98312 | tf_op jit(solution)/shard_map/ppermute | solution.py:334
  24.3 1.8 %collective-permute-start.6 = (bf16[1,128,128]{2,1,0:T(8,128)(2,1)S(1)}, bf16[1,128,128]{2,1,0:T(8,128)(2,1)S(1)}, u32[]{:S(2)}, u32[]{:S(2)}) collective-permute-start(bf16[1,128,128]{2,1,0:T(8,128)(2,1)S(1)} %collective-permute-done.5.last_ref), channel_id=1, source_target_pairs={{0,1},{1,0},{2,3},{3,2},{4,5},{5,4},{6,7},{7,6},{8,9},{9,8},{10,11... | collective-permute-start | bytes 98312 | tf_op jit(solution)/shard_map/ppermute | solution.py:334
